TPU v7x, 16 devices: a whole 2x2x2 slice. The times are simulated.
16 devices in a mesh: dp: 4 (over z, y), sp: 4 (over x, core).
Axes of the slice: x: 2, y: 2, z: 2, core: 2. Of those that a mesh axis runs over, the one named last changes fastest.
Arguments:
- image_in: bfloat16 [16, 256, 1536], P('dp', 'sp'), parts along dimension 0
- text_in: bfloat16 [16, 333, 1536], P('dp'), parts along dimension 0
- cond_vec: bfloat16 [16, 1536], P('dp'), parts along dimension 0
- w_ada: bfloat16 [2, 1536, 4608], replicated
- b_ada: float32 [2, 4608], replicated
- w_qkv: bfloat16 [2, 1536, 4608], replicated
- b_qkv: float32 [2, 4608], replicated
- qk_gain: float32 [2, 2, 64], replicated
- w_out: bfloat16 [2, 1536, 1536], replicated
- b_out: float32 [2, 1536], replicated
- image_cot: bfloat16 [16, 256, 1536], P('dp', 'sp'), parts along dimension 0
- text_cot: bfloat16 [16, 333, 1536], P('dp'), parts along dimension 0
Outputs:
- output 1: bfloat16 [16, 256, 1536], P('dp', 'sp'), parts along dimension 0
- output 2: bfloat16 [16, 333, 1536], P('dp'), parts along dimension 0
- output 3: bfloat16 [16, 256, 1536], P('dp', 'sp'), parts along dimension 0
- output 4: bfloat16 [16, 333, 1536], P('dp'), parts along dimension 0
- output 5: float32 [16, 1536], P('dp'), parts along dimension 0
- output 6: float32 [8, 1536, 4608], P('dp'), parts along dimension 0
- output 7: float32 [8, 4608], P('dp'), parts along dimension 0
- output 8: float32 [8, 1536, 4608], P('dp'), parts along dimension 0
- output 9: float32 [8, 4608], P('dp'), parts along dimension 0
- output 10: float32 [8, 2, 64], P('dp'), parts along dimension 0
- output 11: float32 [8, 1536, 1536], P('dp'), parts along dimension 0
- output 12: float32 [8, 1536], P('dp'), parts along dimension 0
There are 4 independent parts. A program takes and returns all parts, laid end to end along the dimension named above; an argument that names none is the same for every part.
All inputs are finite; a program needn't handle non-finite values.
Results may differ from a plain program's by a relative error of at most 0.0130064.
Values are sent between devices in bfloat16 or wider.
A program may use at most 1 GiB of HBM per device.

v0:
```python
import math
import jax
import jax.numpy as jnp
from jax import lax
from jax.sharding import PartitionSpec as P

NORM_EPS = 1e-6


def norm_modulate(tokens, shift_vec, scale_vec):
    avg_val = jnp.mean(tokens, axis=-1, keepdims=True)
    centred = tokens - avg_val
    var_val = jnp.mean(centred * centred, axis=-1, keepdims=True)
    normed = centred * lax.rsqrt(var_val + NORM_EPS)
    return (normed * (1.0 + scale_vec[:, None, :]) + shift_vec[:, None, :]).astype(jnp.bfloat16)


def head_rms(raw_vals, gain_vec):
    inv_rms = lax.rsqrt(jnp.mean(raw_vals * raw_vals, axis=-1, keepdims=True) + NORM_EPS)
    return (raw_vals * inv_rms * gain_vec).astype(jnp.bfloat16)


def attend_fwd(q_rows, key_rows, val_rows, att_scale):
    scores = jnp.einsum('bqhf,bkhf->bhqk', q_rows, key_rows, preferred_element_type=jnp.float32) * att_scale
    prob_mat = jax.nn.softmax(scores, axis=-1).astype(jnp.bfloat16)
    return jnp.einsum('bhqk,bkhf->bqhf', prob_mat, val_rows, preferred_element_type=jnp.float32).astype(jnp.bfloat16)


def attend_bwd(q_rows, out_rows, dout_rows, key_rows, val_rows, att_scale):
    scores = jnp.einsum('bqhf,bkhf->bhqk', q_rows, key_rows, preferred_element_type=jnp.float32) * att_scale
    prob_mat = jax.nn.softmax(scores, axis=-1)
    d_prob = jnp.einsum('bqhf,bkhf->bhqk', dout_rows, val_rows, preferred_element_type=jnp.float32)
    row_delta = jnp.einsum('bqhf,bqhf->bhq', dout_rows, out_rows, preferred_element_type=jnp.float32)
    d_scores = (prob_mat * (d_prob - row_delta[..., None]) * att_scale).astype(jnp.bfloat16)
    d_query = jnp.einsum('bhqk,bkhf->bqhf', d_scores, key_rows, preferred_element_type=jnp.float32).astype(jnp.bfloat16)
    d_keys = jnp.einsum('bhqk,bqhf->bkhf', d_scores, q_rows, preferred_element_type=jnp.float32)
    d_vals = jnp.einsum('bhqk,bqhf->bkhf', prob_mat.astype(jnp.bfloat16), dout_rows, preferred_element_type=jnp.float32)
    return d_query, d_keys, d_vals


def split_rows(array_in, rows_per):
    lead_shape = (array_in.shape[0], array_in.shape[1] // rows_per, rows_per)
    return array_in.reshape(lead_shape + array_in.shape[2:]).swapaxes(0, 1)


def join_rows(array_in):
    lead_shape = (array_in.shape[1], array_in.shape[0] * array_in.shape[2])
    return array_in.swapaxes(0, 1).reshape(lead_shape + array_in.shape[3:])


def attention_forward(q_txt, q_img, key_rows, val_rows, att_scale, query_rows):
    out_txt = attend_fwd(q_txt, key_rows, val_rows, att_scale)
    out_img = join_rows(lax.map(lambda q_block: attend_fwd(q_block, key_rows, val_rows, att_scale), split_rows(q_img, query_rows)))
    return out_txt, out_img


def attention_backward(q_txt, q_img, out_txt, out_img, d_txt, d_img, key_rows, val_rows, att_scale, query_rows):
    dq_txt, dk_sum, dv_sum = attend_bwd(q_txt, out_txt, d_txt, key_rows, val_rows, att_scale)

    def scan_step(acc_pair, block_in):
        dq_block, dk_block, dv_block = attend_bwd(block_in[0], block_in[1], block_in[2], key_rows, val_rows, att_scale)
        return (acc_pair[0] + dk_block, acc_pair[1] + dv_block), dq_block

    blocks_in = (split_rows(q_img, query_rows), split_rows(out_img, query_rows), split_rows(d_img, query_rows))
    (dk_sum, dv_sum), dq_blocks = lax.scan(scan_step, (dk_sum, dv_sum), blocks_in)
    return dq_txt, join_rows(dq_blocks), dk_sum, dv_sum


def solution(mesh):
    sp_size = mesh.shape['sp']

    def device_fn(image_in, text_in, cond_vec, w_ada, b_ada, w_qkv, b_qkv, qk_gain, w_out, b_out, image_cot, text_cot):
        n_batch, tok_dev, d_model = image_in.shape
        ctx_len = text_in.shape[1]
        head_dim = qk_gain.shape[-1]
        n_heads = d_model // head_dim
        local_heads = n_heads // sp_size
        att_scale = head_dim ** -0.5
        head_lo = lax.axis_index('sp') * local_heads
        query_rows = math.gcd(tok_dev * sp_size, 512)
        two_width = 2 * d_model

        cond_act = jax.nn.silu(cond_vec.astype(jnp.float32)).astype(jnp.bfloat16)
        cond_mod = jnp.einsum('bd,sde->sbe', cond_act, w_ada, preferred_element_type=jnp.float32) + b_ada[:, None, :]
        shift_img, scale_img, gate_img = cond_mod[0, :, :d_model], cond_mod[0, :, d_model:two_width], cond_mod[0, :, two_width:]
        shift_txt, scale_txt, gate_txt = cond_mod[1, :, :d_model], cond_mod[1, :, d_model:two_width], cond_mod[1, :, two_width:]

        image_f32 = image_in.astype(jnp.float32)
        hid_img = norm_modulate(image_f32, shift_img, scale_img)
        proj_img = jnp.einsum('btd,de->bte', hid_img, w_qkv[0], preferred_element_type=jnp.float32) + b_qkv[0]
        proj_img = proj_img.reshape(n_batch, tok_dev, 3, n_heads, head_dim)
        qkv_img = jnp.stack([head_rms(proj_img[:, :, 0], qk_gain[0, 0]), head_rms(proj_img[:, :, 1], qk_gain[0, 1]), proj_img[:, :, 2].astype(jnp.bfloat16)], axis=2)
        qkv_heads = lax.all_to_all(qkv_img, 'sp', 3, 1, tiled=True)

        text_f32 = text_in.astype(jnp.float32)
        hid_txt = norm_modulate(text_f32, shift_txt, scale_txt)
        w_qkv_own = lax.dynamic_slice_in_dim(w_qkv[1].reshape(d_model, 3, n_heads, head_dim), head_lo, local_heads, axis=2)
        b_qkv_own = lax.dynamic_slice_in_dim(b_qkv[1].reshape(3, n_heads, head_dim), head_lo, local_heads, axis=1)
        proj_txt = jnp.einsum('bld,dchf->blchf', hid_txt, w_qkv_own, preferred_element_type=jnp.float32) + b_qkv_own
        q_txt = head_rms(proj_txt[:, :, 0], qk_gain[1, 0])
        k_txt = head_rms(proj_txt[:, :, 1], qk_gain[1, 1])
        v_txt = proj_txt[:, :, 2].astype(jnp.bfloat16)

        q_img_h = qkv_heads[:, :, 0]
        key_rows = jnp.concatenate([k_txt, qkv_heads[:, :, 1]], axis=1)
        val_rows = jnp.concatenate([v_txt, qkv_heads[:, :, 2]], axis=1)
        out_txt, out_img_h = attention_forward(q_txt, q_img_h, key_rows, val_rows, att_scale, query_rows)
        out_img = lax.all_to_all(out_img_h, 'sp', 1, 2, tiled=True)

        w_out_img = w_out[0].reshape(n_heads, head_dim, d_model)
        y_img = jnp.einsum('bthf,hfe->bte', out_img, w_out_img, preferred_element_type=jnp.float32) + b_out[0]
        image_new = (image_f32 + gate_img[:, None, :] * y_img).astype(jnp.bfloat16)
        w_out_own = lax.dynamic_slice_in_dim(w_out[1].reshape(n_heads, head_dim, d_model), head_lo, local_heads, axis=0)
        y_txt = lax.psum(jnp.einsum('blhf,hfe->ble', out_txt, w_out_own, preferred_element_type=jnp.float32), 'sp') + b_out[1]
        text_new = (text_f32 + gate_txt[:, None, :] * y_txt).astype(jnp.bfloat16)

        cot_img = image_cot.astype(jnp.float32)
        cot_txt = text_cot.astype(jnp.float32)
        dgate_img = jnp.sum(cot_img * y_img, axis=1)
        dy_img_f = cot_img * gate_img[:, None, :]
        db_out_img = jnp.sum(dy_img_f, axis=(0, 1))
        dy_img = dy_img_f.astype(jnp.bfloat16)
        dw_out_img = jnp.einsum('bthf,bte->hfe', out_img, dy_img, preferred_element_type=jnp.float32)
        d_out_img = jnp.einsum('bte,hfe->bthf', dy_img, w_out_img, preferred_element_type=jnp.float32).astype(jnp.bfloat16)
        d_out_img_h = lax.all_to_all(d_out_img, 'sp', 2, 1, tiled=True)

        dgate_txt = jnp.sum(cot_txt * y_txt, axis=1)
        dy_txt_f = cot_txt * gate_txt[:, None, :]
        db_out_txt = jnp.sum(dy_txt_f, axis=(0, 1))
        dy_txt = dy_txt_f.astype(jnp.bfloat16)
        dw_out_own = jnp.einsum('blhf,ble->hfe', out_txt, dy_txt, preferred_element_type=jnp.float32)
        d_out_txt = jnp.einsum('ble,hfe->blhf', dy_txt, w_out_own, preferred_element_type=jnp.float32).astype(jnp.bfloat16)

        dq_txt, dq_img_h, dk_rows, dv_rows = attention_backward(q_txt, q_img_h, out_txt, out_img_h, d_out_txt, d_out_img_h, key_rows, val_rows, att_scale, query_rows)
        d_qkv_heads = jnp.stack([dq_img_h, dk_rows[:, ctx_len:].astype(jnp.bfloat16), dv_rows[:, ctx_len:].astype(jnp.bfloat16)], axis=2)
        d_qkv_img = lax.all_to_all(d_qkv_heads, 'sp', 1, 3, tiled=True)

        _, pull_q = jax.vjp(head_rms, proj_img[:, :, 0], qk_gain[0, 0])
        dq_raw, dgain_q_img = pull_q(d_qkv_img[:, :, 0])
        _, pull_k = jax.vjp(head_rms, proj_img[:, :, 1], qk_gain[0, 1])
        dk_raw, dgain_k_img = pull_k(d_qkv_img[:, :, 1])
        d_proj_img = jnp.stack([dq_raw, dk_raw, d_qkv_img[:, :, 2].astype(jnp.float32)], axis=2).reshape(n_batch, tok_dev, 3 * d_model)
        db_qkv_img = jnp.sum(d_proj_img, axis=(0, 1))
        d_proj_img = d_proj_img.astype(jnp.bfloat16)
        dw_qkv_img = jnp.einsum('btd,bte->de', hid_img, d_proj_img, preferred_element_type=jnp.float32)
        d_hid_img = jnp.einsum('bte,de->btd', d_proj_img, w_qkv[0], preferred_element_type=jnp.float32).astype(jnp.bfloat16)
        _, pull_img = jax.vjp(norm_modulate, image_f32, shift_img, scale_img)
        d_image_norm, dshift_img, dscale_img = pull_img(d_hid_img)
        grad_image = (cot_img + d_image_norm).astype(jnp.bfloat16)
        dmod_img = jnp.concatenate([dshift_img, dscale_img, dgate_img], axis=-1)

        _, pull_tq = jax.vjp(head_rms, proj_txt[:, :, 0], qk_gain[1, 0])
        dq_txt_raw, dgain_q_txt = pull_tq(dq_txt)
        _, pull_tk = jax.vjp(head_rms, proj_txt[:, :, 1], qk_gain[1, 1])
        dk_txt_raw, dgain_k_txt = pull_tk(dk_rows[:, :ctx_len].astype(jnp.bfloat16))
        dv_txt_raw = dv_rows[:, :ctx_len].astype(jnp.bfloat16).astype(jnp.float32)
        d_proj_txt = jnp.stack([dq_txt_raw, dk_txt_raw, dv_txt_raw], axis=2)
        db_qkv_own = jnp.sum(d_proj_txt, axis=(0, 1))
        d_proj_txt = d_proj_txt.astype(jnp.bfloat16)
        dw_qkv_own = jnp.einsum('bld,blchf->dchf', hid_txt, d_proj_txt, preferred_element_type=jnp.float32)
        d_hid_part = jnp.einsum('blchf,dchf->bld', d_proj_txt, w_qkv_own, preferred_element_type=jnp.float32)

        summed = lax.psum((dmod_img, db_out_img, dw_out_img, jnp.stack([dgain_q_img, dgain_k_img]), db_qkv_img, dw_qkv_img, d_hid_part, jnp.stack([dgain_q_txt, dgain_k_txt])), 'sp')
        dmod_img, db_out_img, dw_out_img, dgain_img, db_qkv_img, dw_qkv_img, d_hid_txt, dgain_txt = summed
        _, pull_txt = jax.vjp(norm_modulate, text_f32, shift_txt, scale_txt)
        d_text_norm, dshift_txt, dscale_txt = pull_txt(d_hid_txt.astype(jnp.bfloat16))
        grad_text = (cot_txt + d_text_norm).astype(jnp.bfloat16)
        dmod_txt = jnp.concatenate([dshift_txt, dscale_txt, dgate_txt], axis=-1)
        dw_qkv_txt = lax.all_gather(dw_qkv_own, 'sp', axis=2, tiled=True).reshape(d_model, 3 * d_model)
        db_qkv_txt = lax.all_gather(db_qkv_own, 'sp', axis=1, tiled=True).reshape(3 * d_model)
        dw_out_txt = lax.all_gather(dw_out_own, 'sp', axis=0, tiled=True).reshape(d_model, d_model)

        d_mod = jnp.stack([dmod_img, dmod_txt])
        dw_ada = jnp.einsum('bd,sbe->sde', cond_act.astype(jnp.float32), d_mod)
        db_ada = jnp.sum(d_mod, axis=1)
        d_act = jnp.einsum('sbe,sde->bd', d_mod.astype(jnp.bfloat16), w_ada, preferred_element_type=jnp.float32).astype(jnp.bfloat16)
        _, pull_act = jax.vjp(jax.nn.silu, cond_vec.astype(jnp.float32))
        grad_cond = pull_act(d_act.astype(jnp.float32))[0]
        return (image_new, text_new, grad_image, grad_text, grad_cond, dw_ada, db_ada, jnp.stack([dw_qkv_img, dw_qkv_txt]), jnp.stack([db_qkv_img, db_qkv_txt]), jnp.stack([dgain_img, dgain_txt]), jnp.stack([dw_out_img.reshape(d_model, d_model), dw_out_txt]), jnp.stack([db_out_img, db_out_txt]))

    data_spec = P('dp', 'sp', None)
    batch_spec = P('dp')
    rep_spec = P()
    in_specs = (data_spec, batch_spec, batch_spec, rep_spec, rep_spec, rep_spec, rep_spec, rep_spec, rep_spec, rep_spec, data_spec, batch_spec)
    out_specs = (data_spec, batch_spec, data_spec, batch_spec, batch_spec, batch_spec, batch_spec, batch_spec, batch_spec, batch_spec, batch_spec, batch_spec)
    return jax.shard_map(device_fn, mesh=mesh, in_specs=in_specs, out_specs=out_specs, check_vma=False)
```

profile of v0, /device:TPU:0, one launch (start us, length us, event | category | flops | bytes accessed | tf_op | source)
XLA Modules:
  0.0 1617.9 jit_solution(7971370163470480536)
XLA Ops:
  7.2 13.0 fusion.39
  37.0 12.6 slice.120
  50.0 11.2 fusion.33
  77.3 17.6 %copy.127 = bf16[1,1536,4608]{1,2,0:T(8,128)(2,1)} copy(bf16[1,1536,4608]{2,1,0:T(8,128)(2,1)} %slice.120) | data formatting | bytes 28311552 | tf_op jit(solution)/shard_map/slice | solution.py:97
  108.1 10.3 broadcast_add_fusion
  188.2 12.5 fusion.178
  200.7 12.2 fusion.179
  226.8 9.7 fusion.38
  253.5 14.3 multiply_convert_fusion
  390.3 10.2 fusion.175
  400.7 12.2 convolution_bitcast_fusion.1
  425.3 10.4 fusion.97
  444.2 9.6 convolution_bitcast_fusion.4
  453.9 10.9 convolution_bitcast_fusion.2
  476.0 279.1 %all-reduce.6 = (bf16[4,333,1536]{2,1,0:T(8,128)(2,1)}, f32[1,4608]{1,0:T(1,128)S(1)}, f32[1,2,64]{2,1,0:T(2,128)S(1)}, f32[1,2,64]{2,1,0:T(2,128)S(1)}, f32[1,1536]{1,0:T(1,128)S(1)}) all-reduce(f32[4,333,1536]{2,1,0:T(8,128)} %convolution_bitcast_fusion.2, f32[1,4608]{1,0:T(1,128)S(1)} %stack.111, ...), channel_id=1, replica_groups=mesh['dp'=4,'sp'=4] {'sp'}, use_global_device_ids=true, to_apply=%region_19.20 | all-reduce | flops 2052352 | bytes 12326912 | tf_op jit(solution)/shard_map/psum | solution.py:163
  766.6 542.8 %all-reduce.5.cloned.1.call-done = (f32[4,333,1536]{2,1,0:T(8,128)}, f32[1,4,4608]{2,1,0:T(4,128)}, f32[1,1536,4608]{2,1,0:T(8,128)}, f32[1,1536,1536]{2,1,0:T(8,128)}) async-done(((f32[4,333,1536]{2,1,0:T(8,128)}, f32[1,4,4608]{2,1,0:T(4,128)}, f32[1,1536,4608]{2,1,0:T(8,128)}, f32[1,1536,1536]{2,1,0:T(8,128)}), (f32[4,333,1536]{2,1,0:T(8,128)}, f32[1,4,4608]{2,1,0:T(4,128)}, f32[1,1536,4608]{2,1,0:T(8,128)}, ...) | async-done | bytes 46006288 | tf_op jit(solution)/shard_map/psum | solution.py:114
  1309.4 11.7 fusion.19
  1331.4 21.4 %convolution_bitcast_fusion = f32[2,1536,4608]{1,2,0:T(8,128)} fusion(f32[1,4,4608]{2,1,0:T(4,128)S(1)} %maximum_bitcast_fusion.1, f32[1,4,4608]{2,1,0:T(4,128)S(1)} %copy-done.52, bf16[4,1536]{1,0:T(4,128)(2,1)S(1)} %copy-done.71), kind=kOutput, calls=%fused_computation.3 | convolution fusion | flops 113430528 | bytes 56782848 | tf_op jit(solution)/shard_map/bd,sbe->sde/dot_general | solution.py:174
  1352.8 54.9 %copy.155 = f32[2,1536,4608]{2,1,0:T(8,128)} copy(f32[2,1536,4608]{1,2,0:T(8,128)} %convolution_bitcast_fusion) | data formatting | bytes 113246208
  1409.1 14.6 pad_maximum_fusion.1
  1423.7 13.4 fusion.153
  1437.1 108.2 %all-gather.3.cloned.1.call-done = f32[1536,3,24,64]{0,3,2,1:T(8,128)} async-done(((f32[1536,3,6,64]{0,3,2,1:T(8,128)}), f32[1536,3,24,64]{0,3,2,1:T(8,128)}) %all-gather.3.cloned.1.call-update) | async-done | bytes 28311568 | tf_op jit(solution)/shard_map/all_gather | solution.py:169
  1545.3 27.7 %copy.149 = f32[1,1536,4608]{2,1,0:T(8,128)} copy(f32[1,1536,4608]{1,2,0:T(8,128)} %bitcast.348) | data formatting | bytes 56623104 | tf_op jit(solution)/shard_map/stack;reshape | solution.py:179
  1573.0 37.9 %pad_maximum_fusion = f32[2,1536,4608]{2,1,0:T(8,128)} fusion(f32[1,1536,4608]{2,1,0:T(8,128)} %copy.149, f32[1,1536,4608]{2,1,0:T(8,128)} %get-tuple-element.149), kind=kLoop, calls=%fused_computation.2 | loop fusion | flops 14155776 | bytes 113246208 | tf_op jit(solution)/shard_map/stack | solution.py:179
  (345 shorter events, 323.8 us)
Async XLA Ops:
  20.2 29.8 %copy-start.75 = (f32[4,1536]{1,0:T(4,128)}, f32[4,1536]{1,0:T(4,128)S(1)}, u32[]{:S(2)}) copy-start(f32[4,1536]{1,0:T(4,128)S(1)} %get-tuple-element.167) | copy-start | bytes 73732
  20.2 29.8 %copy-start.88 = (f32[4,1536]{1,0:T(4,128)}, f32[4,1536]{1,0:T(4,128)S(1)}, u32[]{:S(2)}) copy-start(f32[4,1536]{1,0:T(4,128)S(1)} %get-tuple-element.166) | copy-start | bytes 73732
  20.2 87.7 %copy-start.67 = (f32[4,1536]{1,0:T(4,128)}, f32[4,1536]{1,0:T(4,128)S(1)}, u32[]{:S(2)}) copy-start(f32[4,1536]{1,0:T(4,128)S(1)} %get-tuple-element.169) | copy-start | bytes 73732
  20.2 87.7 %copy-start.86 = (f32[4,1536]{1,0:T(4,128)}, f32[4,1536]{1,0:T(4,128)S(1)}, u32[]{:S(2)}) copy-start(f32[4,1536]{1,0:T(4,128)S(1)} %get-tuple-element.168) | copy-start | bytes 73732
  20.2 123.9 %copy-start.72 = (f32[4,1536]{1,0:T(4,128)}, f32[4,1536]{1,0:T(4,128)S(1)}, u32[]{:S(2)}) copy-start(f32[4,1536]{1,0:T(4,128)S(1)} %get-tuple-element.165) | copy-start | bytes 73732
  31.9 97.7 %all-to-all-start.2 = ((bf16[4,2,49152]{2,1,0:T(2,128)(2,1)}), bf16[4,2,49152]{2,1,0:T(2,128)(2,1)}, u32[]{:S(2)}, u32[]{:S(2)}) async-start(bf16[4,2,49152]{2,1,0:T(2,128)(2,1)} %reshape.261), calls=%async_computation.2 | async-start | bytes 1572864 | tf_op jit(solution)/shard_map/all_to_all | solution.py:125
  36.9 13.1 copy-start.90
  77.2 41.2 %copy-start.5 = (f32[4,64,1,24,64]{4,3,2,1,0:T(8,128)}, f32[4,64,1,24,64]{4,3,2,1,0:T(8,128)S(1)}, u32[]{:S(2)}) copy-start(f32[4,64,1,24,64]{4,3,2,1,0:T(8,128)S(1)} %get-tuple-element.153) | copy-start | bytes 4718596
  100.3 18.0 %copy-start.101 = (f32[64]{0:T(128)}, f32[64]{0:T(128)S(1)}, u32[]{:S(2)}) copy-start(f32[64]{0:T(128)S(1)} %get-tuple-element.173) | copy-start | bytes 772
  100.3 38.9 %copy-start.103 = (f32[64]{0:T(128)}, f32[64]{0:T(128)S(1)}, u32[]{:S(2)}) copy-start(f32[64]{0:T(128)S(1)} %get-tuple-element.171) | copy-start | bytes 772
  100.3 38.9 %copy-start.105 = (f32[64]{0:T(128)}, f32[64]{0:T(128)S(1)}, u32[]{:S(2)}) copy-start(f32[64]{0:T(128)S(1)} %get-tuple-element.174) | copy-start | bytes 772
  104.9 13.4 copy-start.50
  129.6 33.5 %all-to-all-start = ((bf16[4,2,147456]{2,1,0:T(2,128)(2,1)}), bf16[4,2,147456]{2,1,0:T(2,128)(2,1)}, u32[]{:S(2)}, u32[]{:S(2)}) async-start(bf16[4,2,147456]{2,1,0:T(2,128)(2,1)} %reshape.257), calls=%async_computation | async-start | bytes 4718592 | tf_op jit(solution)/shard_map/all_to_all | solution.py:93
  253.5 14.3 copy-start.38
  297.3 21.0 %all-to-all-start.1 = ((bf16[4,2,49152]{2,1,0:T(2,128)(2,1)}), bf16[4,2,49152]{2,1,0:T(2,128)(2,1)}, u32[]{:S(2)}, u32[]{:S(2)}) async-start(bf16[4,2,49152]{2,1,0:T(2,128)(2,1)} %reshape.259), calls=%async_computation.1 | async-start | bytes 1572864 | tf_op jit(solution)/shard_map/all_to_all | solution.py:108
  318.3 32.0 %all-to-all-start.3 = ((bf16[4,2,147456]{2,1,0:T(2,128)(2,1)}), bf16[4,2,147456]{2,1,0:T(2,128)(2,1)S(1)}, u32[]{:S(2)}, u32[]{:S(2)}) async-start(bf16[4,2,147456]{2,1,0:T(2,128)(2,1)} %reshape.263), calls=%async_computation.3 | async-start | bytes 4718592 | tf_op jit(solution)/shard_map/all_to_all | solution.py:136
  322.0 987.3 %all-reduce.5.cloned.1.call-start = ((), (), s32[]{:S(2)}) async-start(), calls=%async_computation.6 | async-start | bytes 92160000 | tf_op jit(solution)/shard_map/psum | solution.py:114
  360.0 15.0 copy-start.13
  390.3 23.4 %slice-start = ((s8[4718592]{0:T(1024)(128)(4,1)}), s8[524288]{0:T(1024)(128)(4,1)S(1)}, s32[]{:S(2)}) async-start(s8[4718592]{0:T(1024)(128)(4,1)} %bitcast.367), calls=%async_computation.7 | async-start | bytes 1048576
  418.1 991.0 %all-gather.5.cloned.1.call-start = ((), (), s32[]{:S(2)}) async-start(), calls=%async_computation.5 | async-start | bytes 11796480 | tf_op jit(solution)/shard_map/all_gather | solution.py:171
  425.0 1120.3 %all-gather.3.cloned.1.call-start = ((), (), s32[]{:S(2)}) async-start(), calls=%async_computation.4 | async-start | bytes 35389440 | tf_op jit(solution)/shard_map/all_gather | solution.py:169
  437.5 16.4 %copy-start.20 = (f32[4,333,1,6,64]{1,4,3,0,2:T(8,128)}, f32[4,333,1,6,64]{1,4,3,0,2:T(8,128)S(1)}, u32[]{:S(2)}) copy-start(f32[4,333,1,6,64]{1,4,3,0,2:T(8,128)S(1)} %fusion.125) | copy-start | bytes 6137860
  761.6 547.8 %copy-start.74 = (f32[4,1536]{1,0:T(4,128)S(1)}, f32[4,1536]{1,0:T(4,128)}, u32[]{:S(2)}) copy-start(f32[4,1536]{1,0:T(4,128)} %copy-done.72) | copy-start | bytes 73732
  761.6 547.8 %copy-start.85 = (f32[1536]{0:T(1024)S(1)}, f32[1536]{0:T(1024)}, u32[]{:S(2)}) copy-start(f32[1536]{0:T(1024)} %get-tuple-element.140) | copy-start | bytes 18436
  (95 other events, 549.3 us)
Sparse Core Ops, SparseCore 0:
  418.2 891.1 all-reduce.4
  1310.9 62.6 all-gather.4
  1375.2 170.0 all-gather.2
where the time goes:
time: 1630 us; the launch traced here: 1620 us
  waiting for transfers between devices  663 us (41%)
  blocking collectives  285 us (17%)
  local copies, waits for them, and re-layouts  254 us (16%)
  matrix products  238 us (15%)
  other arithmetic  144 us (9%)
  starting transfers between devices  17.7 us (1%)
    psum x1, waiting for transfers between devices, device_fn(): lax.psum(jnp.einsum('blhf,hfe->ble', out_txt, w_out_own, preferred_elemen...  543 us
    psum x1, blocking collectives, device_fn(): lax.psum((dmod_img, db_out_img, dw_out_img, jnp.stack([dgain_q_img, dgain...  279 us
    unnamed x236, local copies, waits for them, and re-layouts  116 us
    all_gather x1, waiting for transfers between devices, device_fn(): lax.all_gather(dw_qkv_own, 'sp', axis=2, tiled=True)  108 us
    another operation x1, other arithmetic, device_fn(): jnp.stack([dw_qkv_img, dw_qkv_txt])  37.9 us
  transfers between devices with their start and end apart: 7, of which 4 were waited for; matrix products, arithmetic and copies ran while one was open for 21% of the time, Pallas kernels for 0%

commit v1 on v0

v1 whole, which is shorter than its diff:
```python
import functools
import math
import jax
import jax.numpy as jnp
from jax import lax
from jax.experimental import pallas as pl
from jax.experimental.pallas import tpu as pltpu
from jax.sharding import PartitionSpec as P

NORM_EPS = 1e-6
F32 = jnp.float32
BF16 = jnp.bfloat16
NN = (((1,), (0,)), ((), ()))
NT = (((1,), (1,)), ((), ()))
TN = (((0,), (0,)), ((), ()))


def dot(lhs, rhs, dims=NN):
    return lax.dot_general(lhs, rhs, dims, preferred_element_type=F32)


def round_up(num, mult):
    return -(-num // mult) * mult


def stats(tokens):
    avg_val = jnp.mean(tokens, axis=-1, keepdims=True)
    centred = tokens - avg_val
    var_val = jnp.mean(centred * centred, axis=-1, keepdims=True)
    inv_std = lax.rsqrt(var_val + NORM_EPS)
    return centred * inv_std, inv_std


def prologue(tok_ref, cot_ref, mod_ref, hid_ref, dy_ref, chunk):
    @pl.loop(0, tok_ref.shape[0] // chunk)
    def _(step):
        rows = pl.ds(pl.multiple_of(step * chunk, chunk), chunk)
        normed, _ = stats(tok_ref[rows].astype(F32))
        hid_ref[rows] = (normed * (1.0 + mod_ref[1:2]) + mod_ref[0:1]).astype(BF16)
        dy_ref[rows] = (cot_ref[rows].astype(F32) * mod_ref[2:3]).astype(BF16)


def epilogue(tok_ref, cot_ref, mod_ref, bias, y_ref, acc_ref, new_ref, grad_ref, sums_ref, base, chunk):
    sums_ref[base:base + 4] = jnp.zeros((4, sums_ref.shape[1]), F32)

    @pl.loop(0, tok_ref.shape[0] // chunk)
    def _(step):
        rows = pl.ds(pl.multiple_of(step * chunk, chunk), chunk)
        tokens, cot = tok_ref[rows].astype(F32), cot_ref[rows].astype(F32)
        gate = mod_ref[2:3]
        y_out = y_ref[rows] + bias
        new_ref[rows] = (tokens + gate * y_out).astype(BF16)
        normed, inv_std = stats(tokens)
        d_hid = acc_ref[rows].astype(BF16).astype(F32)
        d_normed = d_hid * (1.0 + mod_ref[1:2])
        mean_d = jnp.mean(d_normed, axis=-1, keepdims=True)
        mean_dn = jnp.mean(d_normed * normed, axis=-1, keepdims=True)
        grad_ref[rows] = (cot + inv_std * (d_normed - mean_d - normed * mean_dn)).astype(BF16)
        sums_ref[base:base + 1] += jnp.sum(d_hid, axis=0, keepdims=True)
        sums_ref[base + 1:base + 2] += jnp.sum(d_hid * normed, axis=0, keepdims=True)
        sums_ref[base + 2:base + 3] += jnp.sum(cot * y_out, axis=0, keepdims=True)
        sums_ref[base + 3:base + 4] += jnp.sum(cot * gate, axis=0, keepdims=True)


def block_kernel(n_keys, heads, tok_i_ref, cot_i_ref, tok_t_ref, cot_t_ref, mod_ref, bo_ref, wq_ref, wk_ref, wv_ref, bq_ref, bk_ref, bv_ref, gain_ref, wo_ref,
                 hid_i_ref, hid_t_ref, dy_i_ref, dy_t_ref, o_i_ref, o_t_ref, dp_i_ref, dp_t_ref, new_i_ref, new_t_ref, grad_i_ref, grad_t_ref, sums_ref, dg_ref, db_ref,
                 tok_ref, cot_ref, y_i_ref, y_t_ref, acc_i_ref, acc_t_ref, hat_ref, inv_ref, nat_ref, trn_ref, v_ref, do_nat_ref, do_trn_ref, o_trn_ref, dq_ref, dk_ref, dv_ref):
    step_b, step_g = pl.program_id(0), pl.program_id(1)
    n_grp = pl.num_programs(1)
    n_img = hid_i_ref.shape[1]
    width = wq_ref.shape[2]
    head_dim = width // heads
    att_scale = head_dim ** -0.5
    n_tok = n_img + hid_t_ref.shape[1]
    k_rows = round_up(n_keys, 16)
    k_main = k_rows - 16

    @pl.when(step_g == 0)
    def _():
        tok_ref[...] = tok_i_ref[:, 0, 0].reshape(tok_ref.shape)
        cot_ref[...] = cot_i_ref[:, 0, 0].reshape(cot_ref.shape)
        prologue(tok_ref, cot_ref, mod_ref.at[0, 0], hid_i_ref.at[0], dy_i_ref.at[0], 16)
        prologue(tok_t_ref.at[0], cot_t_ref.at[0], mod_ref.at[0, 1], hid_t_ref.at[0], dy_t_ref.at[0], 16)
        hid_t_ref[0, n_keys - n_img:] = jnp.zeros((n_tok - n_keys, hid_t_ref.shape[2]), BF16)

    hid_i, hid_t = hid_i_ref[0], hid_t_ref[0]

    for idx, (w_ref, b_ref) in enumerate(((wq_ref, bq_ref), (wk_ref, bk_ref), (wv_ref, bv_ref))):
        raw_i = dot(hid_i, w_ref[0]) + b_ref[0:1, :]
        raw_t = dot(hid_t, w_ref[1]) + b_ref[1:2, :]
        if idx == 2:
            v_ref[:n_img] = raw_i.astype(BF16)
            v_ref[n_img:] = raw_t.astype(BF16)
            trn_ref[2, :, :n_img] = raw_i.T.astype(BF16)
            trn_ref[2, :, n_img:] = raw_t.T.astype(BF16)
        else:
            raw = jnp.concatenate([raw_i.T, raw_t.T], axis=1).reshape(heads, head_dim, n_tok)
            inv = lax.rsqrt(jnp.mean(raw * raw, axis=1, keepdims=True) + NORM_EPS)
            hat = (raw * inv).reshape(width, n_tok)
            normed = hat * gain_ref[idx]
            hat_ref[idx] = hat
            inv_ref[idx] = inv
            trn_ref[idx] = normed.astype(BF16)
            nat_ref[idx] = normed.T.astype(BF16)

    do_i = dot(dy_i_ref[0], wo_ref[0], NT)
    do_t = dot(dy_t_ref[0], wo_ref[1], NT)
    do_nat_ref[:n_img] = do_i.astype(BF16)
    do_nat_ref[n_img:] = do_t.astype(BF16)
    do_trn_ref[:, :n_img] = do_i.T.astype(BF16)
    do_trn_ref[:, n_img:] = do_t.T.astype(BF16)
    dk_ref[k_rows:] = jnp.zeros((n_tok - k_rows, width), F32)
    dv_ref[k_rows:] = jnp.zeros((n_tok - k_rows, width), F32)

    exp_scale = att_scale * math.log2(math.e)
    for head in range(heads):
        rows = slice(head * head_dim, (head + 1) * head_dim)
        q_trn, k_trn, v_trn = trn_ref[0, rows, :], trn_ref[1, rows, :k_rows], trn_ref[2, rows, :k_rows]
        q_nat, k_nat, v_nat = nat_ref[0, :, rows], nat_ref[1, :k_rows, rows], v_ref[:k_rows, rows]
        scores = dot(k_nat, q_trn)
        tail_row = k_main + lax.broadcasted_iota(jnp.int32, (16, n_tok), 0)
        tail = jnp.where(tail_row < n_keys, scores[k_main:], -jnp.inf)
        scores = jnp.concatenate([scores[:k_main], tail], axis=0)
        peak = jnp.max(scores, axis=0, keepdims=True)
        exps = jnp.exp2((scores - peak) * exp_scale)
        prob = exps * (1.0 / jnp.sum(exps, axis=0, keepdims=True))
        prob_lo = prob.astype(BF16)
        out_trn = dot(v_trn, prob_lo).astype(BF16)
        o_trn_ref[rows] = out_trn
        do_trn = do_trn_ref[rows]
        delta = jnp.sum(out_trn.astype(F32) * do_trn.astype(F32), axis=0, keepdims=True)
        d_prob = dot(v_nat, do_trn)
        d_score = (prob * (d_prob - delta)).astype(BF16)
        dv_ref[:k_rows, rows] = dot(prob_lo, do_nat_ref[:, rows])
        dk_ref[:k_rows, rows] = dot(d_score, q_nat) * att_scale
        dq_ref[rows] = dot(k_trn, d_score) * att_scale

    o_nat = o_trn_ref[...].astype(F32).T.astype(BF16)
    o_i_ref[0] = o_nat[:n_img]
    o_t_ref[0] = o_nat[n_img:]

    @pl.when(step_g == 0)
    def _():
        y_i_ref[...] = jnp.zeros_like(y_i_ref)
        y_t_ref[...] = jnp.zeros_like(y_t_ref)
        acc_i_ref[...] = jnp.zeros_like(acc_i_ref)
        acc_t_ref[...] = jnp.zeros_like(acc_t_ref)

    @pl.when((step_g == 0) & (step_b == 0))
    def _():
        dg_ref[...] = jnp.zeros_like(dg_ref)

    y_i_ref[...] += dot(o_nat[:n_img], wo_ref[0])
    y_t_ref[...] += dot(o_nat[n_img:], wo_ref[1])

    d_raw = []
    for idx in range(2):
        d_out = dq_ref[...] if idx == 0 else dk_ref[...].T
        d_out = d_out.astype(BF16).astype(F32)
        hat = hat_ref[idx]
        prod = d_out * hat
        dg_ref[idx] += sum(prod[:, lo:lo + 128] for lo in range(0, n_img, 128))
        dg_ref[2 + idx] += sum(prod[:, lo:lo + 128] for lo in range(n_img, n_tok, 128))
        d_hat = (d_out * gain_ref[idx]).reshape(heads, head_dim, n_tok)
        hat = hat.reshape(heads, head_dim, n_tok)
        mean_dh = jnp.mean(d_hat * hat, axis=1, keepdims=True)
        d_raw.append((inv_ref[idx] * (d_hat - hat * mean_dh)).reshape(width, n_tok).T)
    d_raw.append(dv_ref[...].astype(BF16).astype(F32))
    sums = []
    d_lo = []
    for idx in range(3):
        lo = d_raw[idx].astype(BF16)
        dp_i_ref[0, idx] = lo[:n_img]
        dp_t_ref[0, idx] = lo[n_img:]
        d_lo.append(lo)
        db_ref[0, idx:idx + 1, :] = jnp.sum(d_raw[idx][:n_img], axis=0, keepdims=True)
        db_ref[0, 3 + idx:4 + idx, :] = jnp.sum(d_raw[idx][n_img:], axis=0, keepdims=True)
    db_ref[0, 6:8, :] = jnp.zeros((2, width), F32)
    w_refs = (wq_ref, wk_ref, wv_ref)
    acc_i_ref[...] += sum(dot(d_lo[idx][:n_img], w_refs[idx][0], NT) for idx in range(3))
    acc_t_ref[...] += sum(dot(d_lo[idx][n_img:], w_refs[idx][1], NT) for idx in range(3))

    @pl.when(step_g == n_grp - 1)
    def _():
        epilogue(tok_ref, cot_ref, mod_ref.at[0, 0], bo_ref[0:1], y_i_ref, acc_i_ref, new_i_ref.at[0], grad_i_ref.at[0], sums_ref.at[0], 0, 16)
        epilogue(tok_t_ref.at[0], cot_t_ref.at[0], mod_ref.at[0, 1], bo_ref[1:2], y_t_ref, acc_t_ref, new_t_ref.at[0], grad_t_ref.at[0], sums_ref.at[0], 4, 16)


def fused_block(tokens, text, cot_t, mod, b_out, w_qkv, b_qkv, qk_gain, w_out, n_keys, heads):
    n_src, _, n_b, tok_dev, d_model = tokens.shape
    n_img, n_txt = n_src * tok_dev, text.shape[1]
    n_tok = n_img + n_txt
    head_dim = qk_gain.shape[-1]
    width = heads * head_dim
    n_grp = d_model // width
    gain_cols = jnp.tile(qk_gain, (1, 1, heads))
    gain_full = jnp.concatenate([jnp.broadcast_to(gain_cols[0][:, :, None], (2, width, n_img)), jnp.broadcast_to(gain_cols[1][:, :, None], (2, width, n_txt))], axis=2)

    def rows_spec(n_rows):
        return pl.BlockSpec((1, n_rows, d_model), lambda b, g: (b, 0, 0))

    def w_spec(idx):
        return pl.BlockSpec((2, d_model, width), lambda b, g: (0, 0, idx * n_grp + g))

    def b_spec(idx):
        return pl.BlockSpec((2, width), lambda b, g: (0, idx * n_grp + g))

    def img_spec(idx):
        return pl.BlockSpec((n_src, 1, 1, tok_dev, d_model), lambda b, g: (0, idx, b, 0, 0))

    in_specs = [img_spec(0), img_spec(1), rows_spec(n_txt), rows_spec(n_txt), pl.BlockSpec((1, 2, 3, d_model), lambda b, g: (b, 0, 0, 0)), pl.BlockSpec((2, d_model), lambda b, g: (0, 0)), w_spec(0), w_spec(1), w_spec(2), b_spec(0), b_spec(1), b_spec(2),
                pl.BlockSpec((2, width, n_tok), lambda b, g: (0, 0, 0)), pl.BlockSpec((2, width, d_model), lambda b, g: (0, g, 0))]
    out_specs = [rows_spec(n_img), rows_spec(n_txt), rows_spec(n_img), rows_spec(n_txt), pl.BlockSpec((1, n_img, width), lambda b, g: (b, 0, g)), pl.BlockSpec((1, n_txt, width), lambda b, g: (b, 0, g)),
                 pl.BlockSpec((1, 3, n_img, width), lambda b, g: (b, 0, 0, g)), pl.BlockSpec((1, 3, n_txt, width), lambda b, g: (b, 0, 0, g)),
                 rows_spec(n_img), rows_spec(n_txt), rows_spec(n_img), rows_spec(n_txt), pl.BlockSpec((1, 8, d_model), lambda b, g: (b, 0, 0)),
                 pl.BlockSpec((4, width, 128), lambda b, g: (0, 0, 0)), pl.BlockSpec((1, 8, width), lambda b, g: (b, 0, g))]
    shape = jax.ShapeDtypeStruct
    rows_shape = [shape((n_b, n_img, d_model), BF16), shape((n_b, n_txt, d_model), BF16)]
    out_shape = rows_shape * 3 + [
                 shape((n_b, 3, n_img, d_model), BF16), shape((n_b, 3, n_txt, d_model), BF16),
                 *(rows_shape * 2), shape((n_b, 8, d_model), F32),
                 shape((4, width, 128), F32), shape((n_b, 8, d_model), F32)]
    scratch = [pltpu.VMEM((n_img, d_model), BF16), pltpu.VMEM((n_img, d_model), BF16), pltpu.VMEM((n_img, d_model), F32), pltpu.VMEM((n_txt, d_model), F32), pltpu.VMEM((n_img, d_model), F32), pltpu.VMEM((n_txt, d_model), F32), pltpu.VMEM((2, width, n_tok), F32), pltpu.VMEM((2, heads, 1, n_tok), F32),
               pltpu.VMEM((2, n_tok, width), BF16), pltpu.VMEM((3, width, n_tok), BF16), pltpu.VMEM((n_tok, width), BF16),
               pltpu.VMEM((n_tok, width), BF16), pltpu.VMEM((width, n_tok), BF16), pltpu.VMEM((width, n_tok), BF16),
               pltpu.VMEM((width, n_tok), F32), pltpu.VMEM((n_tok, width), F32), pltpu.VMEM((n_tok, width), F32)]
    flops = n_b * n_tok * d_model * d_model * 16 + n_b * d_model * n_tok * n_tok * 12
    return pl.pallas_call(
        functools.partial(block_kernel, n_keys, heads),
        out_shape=out_shape, grid=(n_b, n_grp), in_specs=in_specs, out_specs=out_specs, scratch_shapes=scratch,
        compiler_params=pltpu.CompilerParams(dimension_semantics=("arbitrary", "arbitrary"), vmem_limit_bytes=67043328),
        cost_estimate=pl.CostEstimate(flops=flops, bytes_accessed=100 * 1024 * 1024, transcendentals=0),
        name="fused_block",
    )(tokens, tokens, text, cot_t, mod, b_out, w_qkv, w_qkv, w_qkv, b_qkv, b_qkv, b_qkv, gain_full, w_out)


def wgrad_kernel(core_ref, lo_i_ref, lp_i_ref, lo_t_ref, lp_t_ref, ro_i_ref, rp_i_ref, ro_t_ref, rp_t_ref, out_ref, trn_i_ref, trn_t_ref, rhs_i_ref, rhs_t_ref):
    branch, step = pl.program_id(0), pl.program_id(1)
    core = core_ref[0]

    def run(lo_ref, lp_ref, ro_ref, rp_ref, trn_ref, rhs_ref):
        n_b, n_rows, _ = lo_ref.shape

        @pl.when(step == 0)
        def _():
            for idx in range(n_b):
                trn_ref[:, pl.ds(pl.multiple_of((core * n_b + idx) * n_rows, n_rows), n_rows)] = lo_ref[idx].T
                trn_ref[:, pl.ds(pl.multiple_of(((1 - core) * n_b + idx) * n_rows, n_rows), n_rows)] = lp_ref[idx].T

        for idx in range(n_b):
            rhs_ref[pl.ds(pl.multiple_of((core * n_b + idx) * n_rows, n_rows), n_rows)] = ro_ref[idx, 0]
            rhs_ref[pl.ds(pl.multiple_of(((1 - core) * n_b + idx) * n_rows, n_rows), n_rows)] = rp_ref[idx, 0]
        out_ref[0] = dot(trn_ref[...], rhs_ref[...])

    @pl.when(branch == 0)
    def _():
        run(lo_i_ref, lp_i_ref, ro_i_ref, rp_i_ref, trn_i_ref, rhs_i_ref)

    @pl.when(branch == 1)
    def _():
        run(lo_t_ref, lp_t_ref, ro_t_ref, rp_t_ref, trn_t_ref, rhs_t_ref)


def wgrad(core, left_i, left_t, right_i, right_t, block, name):
    n_b, n_img, d_model = left_i[0].shape
    n_txt = left_t[0].shape[1]
    n_c = right_i[0].shape[1]
    per = right_i[0].shape[3] // block
    n_blk = n_c * per
    last = n_blk - 1

    def left_spec(n_rows):
        return pl.BlockSpec((n_b, n_rows, d_model), lambda s, j: (0, 0, 0), pipeline_mode=pl.Buffered(1))

    def img_map(s, j):
        pos = jnp.where(s == 0, j, last)
        return (0, pos // per, 0, pos % per)

    def txt_map(s, j):
        pos = jnp.where(s == 1, j, 0)
        return (0, pos // per, 0, pos % per)

    img_spec, txt_spec = pl.BlockSpec((n_b, 1, n_img, block), img_map), pl.BlockSpec((n_b, 1, n_txt, block), txt_map)
    in_specs = [pl.BlockSpec(memory_space=pltpu.SMEM), left_spec(n_img), left_spec(n_img), left_spec(n_txt), left_spec(n_txt), img_spec, img_spec, txt_spec, txt_spec]
    return pl.pallas_call(
        wgrad_kernel,
        out_shape=jax.ShapeDtypeStruct((2, d_model, n_blk * block), F32), grid=(2, n_blk), in_specs=in_specs,
        out_specs=pl.BlockSpec((1, d_model, block), lambda s, j: (s, 0, j)),
        scratch_shapes=[pltpu.VMEM((d_model, 2 * n_b * n_img), BF16), pltpu.VMEM((d_model, 2 * n_b * n_txt), BF16),
                        pltpu.VMEM((2 * n_b * n_img, block), BF16), pltpu.VMEM((2 * n_b * n_txt, block), BF16)],
        compiler_params=pltpu.CompilerParams(dimension_semantics=("arbitrary", "arbitrary"), vmem_limit_bytes=60 * 1024 * 1024),
        cost_estimate=pl.CostEstimate(flops=4 * n_b * (n_img + n_txt) * d_model * n_blk * block, bytes_accessed=8 * d_model * n_blk * block, transcendentals=0),
        name=name,
    )(core[None], *left_i, *left_t, *right_i, *right_t)


def ada_fwd_kernel(act_ref, w_ref, b_ref, out_ref):
    out_ref[0] = dot(act_ref[...], w_ref[0]) + b_ref[pl.ds(pl.program_id(0), 1), :]


def ada_fwd(cond_act, w_ada, b_ada, block):
    n_b, d_model = cond_act.shape
    wide = w_ada.shape[2]
    act = jnp.pad(cond_act, ((0, 16 - n_b), (0, 0)))
    return pl.pallas_call(
        ada_fwd_kernel,
        out_shape=jax.ShapeDtypeStruct((2, 16, wide), F32), grid=(2, wide // block),
        in_specs=[pl.BlockSpec((16, d_model), lambda s, j: (0, 0)), pl.BlockSpec((1, d_model, block), lambda s, j: (s, 0, j)), pl.BlockSpec((2, block), lambda s, j: (0, j))],
        out_specs=pl.BlockSpec((1, 16, block), lambda s, j: (s, 0, j)),
        compiler_params=pltpu.CompilerParams(dimension_semantics=("arbitrary", "arbitrary"), vmem_limit_bytes=40 * 1024 * 1024),
        cost_estimate=pl.CostEstimate(flops=64 * d_model * wide, bytes_accessed=4 * d_model * wide, transcendentals=0),
        name="ada_fwd",
    )(act, w_ada, b_ada)[:, :n_b]


def ada_bwd_kernel(act_ref, dmod_ref, w_ref, dw_ref, dact_ref):
    @pl.when((pl.program_id(0) == 0) & (pl.program_id(1) == 0))
    def _():
        dact_ref[...] = jnp.zeros_like(dact_ref)

    dmod = dmod_ref[0].astype(BF16)
    dw_ref[0] = dot(act_ref[...], dmod)
    dact_ref[...] += dot(dmod, w_ref[0], NT)


def ada_bwd(cond_act, d_mod, w_ada, block):
    n_b, d_model = cond_act.shape
    wide = w_ada.shape[2]
    act_trn = jnp.pad(cond_act, ((0, 16 - n_b), (0, 0))).T
    d_mod = jnp.pad(d_mod, ((0, 0), (0, 16 - n_b), (0, 0)))
    dw_ada, d_act = pl.pallas_call(
        ada_bwd_kernel,
        out_shape=[jax.ShapeDtypeStruct(w_ada.shape, F32), jax.ShapeDtypeStruct((16, d_model), F32)], grid=(2, wide // block),
        in_specs=[pl.BlockSpec((d_model, 16), lambda s, j: (0, 0)), pl.BlockSpec((1, 16, block), lambda s, j: (s, 0, j)), pl.BlockSpec((1, d_model, block), lambda s, j: (s, 0, j))],
        out_specs=[pl.BlockSpec((1, d_model, block), lambda s, j: (s, 0, j)), pl.BlockSpec((16, d_model), lambda s, j: (0, 0))],
        compiler_params=pltpu.CompilerParams(dimension_semantics=("arbitrary", "arbitrary"), vmem_limit_bytes=40 * 1024 * 1024),
        cost_estimate=pl.CostEstimate(flops=8 * d_model * wide * 16, bytes_accessed=12 * d_model * wide, transcendentals=0),
        name="ada_bwd",
    )(act_trn, d_mod, w_ada)
    return dw_ada, d_act[:n_b]


def solution(mesh):
    sp_size = mesh.shape['sp']
    pair = 2
    n_chips = sp_size // pair
    pairs = [(idx, idx + 1 - 2 * (idx % pair)) for idx in range(sp_size)]

    def swap(arr):
        return lax.ppermute(arr, 'sp', pairs)

    def both(arr):
        return arr, swap(arr)

    def device_fn(image_in, text_in, cond_vec, w_ada, b_ada, w_qkv, b_qkv, qk_gain, w_out, b_out, image_cot, text_cot):
        n_batch, tok_dev, d_model = image_in.shape
        ctx_len = text_in.shape[1]
        n_img = tok_dev * sp_size
        n_own = n_batch // pair
        n_txt = round_up(n_img + ctx_len, 128) - n_img
        me = lax.axis_index('sp')
        core, chip = lax.rem(me, pair), lax.div(me, pair)
        own_lo = core * n_own

        tokens = jnp.stack([image_in, image_cot]).reshape(2, pair, n_own, tok_dev, d_model).swapaxes(0, 1)
        tokens = jnp.concatenate([tokens] * n_chips, axis=0)
        tokens = lax.all_to_all(tokens, 'sp', 0, 0)

        def own(arr, axis=0):
            return lax.dynamic_slice_in_dim(arr, own_lo, n_own, axis)

        def ordered(mine, other, axis=0):
            return jnp.where(core == 0, jnp.concatenate([mine, other], axis), jnp.concatenate([other, mine], axis))

        cond_act = jax.nn.silu(cond_vec.astype(F32)).astype(BF16)
        cond_mod = ada_fwd(cond_act, w_ada, b_ada, 1536)
        own_mod = own(cond_mod, 1).reshape(2, n_own, 3, d_model).swapaxes(0, 1)
        pad_rows = ((0, 0), (0, n_txt - ctx_len), (0, 0))
        text_own, cot_own = jnp.pad(own(text_in), pad_rows), jnp.pad(own(text_cot), pad_rows)

        hid_i, hid_t, dy_i, dy_t, o_i, o_t, dp_i, dp_t, new_i, new_t, grad_i, grad_t, sums, dg, db = fused_block(
            tokens, text_own, cot_own, own_mod, b_out, w_qkv, b_qkv, qk_gain, w_out, n_img + ctx_len, 4)

        sums = sums.reshape(n_own, 2, 4, d_model)
        d_mod = sums[:, :, :3].swapaxes(0, 1).reshape(2, n_own, 3 * d_model)
        rest = jnp.concatenate([jnp.sum(sums[:, :, 3], 0).reshape(-1), jnp.sum(db, 0)[:6].reshape(-1), jnp.sum(jnp.sum(dg, -1).reshape(2, 2, -1, qk_gain.shape[-1]), 2).reshape(-1)])
        small = jnp.concatenate([d_mod.reshape(-1), rest])
        small_other = swap(small)
        d_mod_all = ordered(d_mod, small_other[:d_mod.size].reshape(d_mod.shape), 1)
        rest = rest + small_other[d_mod.size:]
        cut = (2 * d_model, 8 * d_model)
        db_out, db_qkv, d_gain = rest[:cut[0]].reshape(2, d_model), rest[cut[0]:cut[1]].reshape(2, 3 * d_model), rest[cut[1]:].reshape(qk_gain.shape)

        o_i, o_t, dy_i, dy_t = both(o_i), both(o_t), both(dy_i[:, None]), both(dy_t[:, None])
        hid_i, hid_t, dp_i, dp_t = both(hid_i), both(hid_t), both(dp_i), both(dp_t)
        dw_ada, d_act = ada_bwd(cond_act, d_mod_all, w_ada, 512)
        dw_out = wgrad(core, o_i, o_t, dy_i, dy_t, 512, "wgrad_out")
        dw_qkv = wgrad(core, hid_i, hid_t, dp_i, dp_t, 512, "wgrad_qkv")
        db_ada = jnp.sum(d_mod_all, axis=1)
        _, pull_act = jax.vjp(jax.nn.silu, cond_vec.astype(F32))
        grad_cond = pull_act(d_act.astype(BF16).astype(F32))[0]

        img_pair = jnp.stack([new_i, grad_i], axis=1)
        chip_lo = chip * pair * tok_dev
        img_mine = lax.dynamic_slice_in_dim(img_pair, chip_lo + core * tok_dev, tok_dev, 2)
        img_send = lax.dynamic_slice_in_dim(img_pair, chip_lo + (1 - core) * tok_dev, tok_dev, 2)
        img_pair = ordered(img_mine, swap(img_send))
        text_new, grad_text = ordered(*both(new_t[:, :ctx_len])), ordered(*both(grad_t[:, :ctx_len]))
        return (img_pair[:, 0], text_new, img_pair[:, 1], grad_text, grad_cond, dw_ada, db_ada, dw_qkv, db_qkv, d_gain, dw_out, db_out)

    data_spec = P('dp', 'sp', None)
    batch_spec = P('dp')
    rep_spec = P()
    in_specs = (data_spec, batch_spec, batch_spec, rep_spec, rep_spec, rep_spec, rep_spec, rep_spec, rep_spec, rep_spec, data_spec, batch_spec)
    out_specs = (data_spec, batch_spec, data_spec, batch_spec, batch_spec, batch_spec, batch_spec, batch_spec, batch_spec, batch_spec, batch_spec, batch_spec)
    return jax.shard_map(device_fn, mesh=mesh, in_specs=in_specs, out_specs=out_specs, check_vma=False)
```

time: 1630 us -> 394 us (0.24)
  waiting for transfers between devices: 663 us -> 15.2 us
  Pallas kernels: 0 us -> 302 us
  blocking collectives: 285 us -> 0 us
  matrix products: 238 us -> 0 us
  local copies, waits for them, and re-layouts: 254 us -> 42.6 us
  other arithmetic: 144 us -> 18.5 us
    psum x1 -> x0, waiting for transfers between devices: 543 us -> none  [device_fn(): lax.psum(jnp.einsum('blhf,hfe->ble', out_txt, w_out_own, preferred_elemen...]
    pallas_call x0 -> x5, Pallas kernels: none -> 302 us  [the longest x1 182 us: fused_block(): pl.pallas_call(functools.partial(block_kernel, n_keys, heads), out_shape=...]
    psum x1 -> x0, blocking collectives: 279 us -> none  [device_fn(): lax.psum((dmod_img, db_out_img, dw_out_img, jnp.stack([dgain_q_img, dgain...]
    dot_general x25 -> x0, matrix products: 214 us -> none  [the longest x2 21.5 us: attend_bwd(): jnp.einsum('bqhf,bkhf->bhqk', dout_rows, val_rows, preferred_element_type...]
    all_gather x2 -> x0, waiting for transfers between devices: 108 us -> none  [the longest x1 108 us: device_fn(): lax.all_gather(dw_qkv_own, 'sp', axis=2, tiled=True)]
    unnamed x236 -> x32, local copies, waits for them, and re-layouts: 116 us -> 13.7 us
    another operation x11 -> x1, other arithmetic: 61 us -> 2.27 us  [device_fn(): img_pair = jnp.stack([new_i, grad_i], axis=1)]
    reduce_sum x16 -> x5, other arithmetic: 44.6 us -> 3.07 us  [the longest x1 1.25 us: device_fn(): jnp.sum(dg, -1).reshape(2, 2, -1, qk_gain.shape[-1])]
  transfers between devices with their start and end apart: 7 -> 13, of which waited for: 4 -> 2; matrix products, arithmetic and copies ran while one was open for 21% -> 15% of each run, Pallas kernels for 0% -> 18%
where the time goes in v1:
time: 394 us; the launch traced here: 388 us
  Pallas kernels  302 us (77%)
  local copies, waits for them, and re-layouts  42.6 us (11%)
  other arithmetic  18.5 us (5%)
  waiting for transfers between devices  15.2 us (4%)
  starting transfers between devices  7.88 us (2%)
    pallas_call x1, Pallas kernels, fused_block(): pl.pallas_call(functools.partial(block_kernel, n_keys, heads), out_shape=...  182 us
    pallas_call x2, Pallas kernels, wgrad(): pl.pallas_call(wgrad_kernel, out_shape=jax.ShapeDtypeStruct((2, d_model,...  74.5 us
    pallas_call x1, Pallas kernels, ada_bwd(): pl.pallas_call(ada_bwd_kernel, out_shape=[jax.ShapeDtypeStruct(w_ada.shap...  34 us
    unnamed x32, local copies, waits for them, and re-layouts  13.7 us
    all_to_all x1, waiting for transfers between devices, device_fn(): tokens = lax.all_to_all(tokens, 'sp', 0, 0)  12 us
    pallas_call x1, Pallas kernels, ada_fwd(): pl.pallas_call(ada_fwd_kernel, out_shape=jax.ShapeDtypeStruct((2, 16, wid...  11.1 us
  transfers between devices with their start and end apart: 13, of which 2 were waited for; matrix products, arithmetic and copies ran while one was open for 15% of the time, Pallas kernels for 18%

profile of v1, /device:TPU:0, one launch (start us, length us, event | category | flops | bytes accessed | tf_op | source)
XLA Modules:
  0.0 387.6 jit_solution(7288579317536400547)
XLA Ops:
  2.2 1.9 pad_maximum_fusion
  4.1 4.8 %all-to-all-start = ((bf16[4,2,2,64,1536]{4,3,2,1,0:T(8,128)(2,1)}), bf16[4,2,2,64,1536]{4,3,2,1,0:T(8,128)(2,1)}, u32[]{:S(2)}, u32[]{:S(2)}) async-start(bf16[4,2,2,64,1536]{4,3,2,1,0:T(8,128)(2,1)} %pad_maximum_fusion), calls=%async_computation | async-start | bytes 6291456 | tf_op jit(solution)/shard_map/all_to_all | solution.py:367
  9.8 11.1 %ada_fwd.1 = f32[2,16,4608]{2,1,0:T(8,128)S(1)} custom-call(bf16[16,1536]{1,0:T(8,128)(2,1)S(1)} %pad.18.clone.act_ref, bf16[2,1536,4608]{2,1,0:T(8,128)(2,1)} %w_ref.3, f32[2,4608]{1,0:T(2,128)S(1)} %copy-done), custom_call_target="tpu_custom_call" | custom-call | flops 452984832 | bytes 28311552 | tf_op jit(solution)/shard_map/ada_fwd/pallas_call | solution.py:305
  21.8 7.6 %constant_dynamic-slice_fusion.1 = (bf16[2,333,1536]{2,0,1:T(2,128)(2,1)S(1)}, bf16[2,333,1536]{2,0,1:T(2,128)(2,1)S(1)}) fusion(bf16[4,333,1536]{2,0,1:T(4,128)(2,1)} %param.23, s32[]{:T(128)S(6)} %select_n.40, bf16[4,333,1536]{2,0,1:T(4,128)(2,1)} %param.13), kind=kLoop, calls=%fused_computation.28 | loop fusion | bytes 8183812 | tf_op jit(solution)/shard_map/dynamic_slice | solution.py:370
  29.6 1.6 pad.17.cot_t_ref
  31.4 1.6 pad.16.tok_t_ref
  34.4 12.0 %all-to-all-done.tok_i_ref.cot_i_ref = bf16[4,2,2,64,1536]{4,3,2,1,0:T(8,128)(2,1)} async-done(((bf16[4,2,2,64,1536]{4,3,2,1,0:T(8,128)(2,1)}), bf16[4,2,2,64,1536]{4,3,2,1,0:T(8,128)(2,1)}, u32[]{:S(2)}, u32[]{:S(2)}) %all-to-all-start) | async-done | bytes 3145760 | tf_op jit(solution)/shard_map/all_to_all | solution.py:367
  46.4 182.3 %fused_block.1 = (bf16[2,256,1536]{2,1,0:T(8,128)(2,1)}, bf16[2,384,1536]{2,1,0:T(8,128)(2,1)}, bf16[2,256,1536]{2,1,0:T(8,128)(2,1)}, bf16[2,384,1536]{2,1,0:T(...) custom-call(bf16[4,2,2,64,1536]{4,3,2,1,0:T(8,128)(2,1)} %all-to-all, ...), custom_call_target="tpu_custom_call" | custom-call | flops 63417876480 | bytes 104857600 | tf_op jit(solution)/shard_map/fused_block/pallas_call | solution.py:228
  233.0 2.3 fusion.3
  236.0 3.4 copy.96
  239.4 3.2 collective-permute-done.3
  242.8 3.4 copy.99
  248.8 34.0 %ada_bwd.1 = (f32[2,1536,4608]{2,1,0:T(8,128)}, f32[16,1536]{1,0:T(8,128)S(1)}) custom-call(bf16[1536,16]{1,0:T(8,128)(2,1)S(1)} %pad_bitcast_fusion.act_ref, f32[2,16,4608]{2,1,0:T(8,128)S(1)} %pad.19.dmod_ref, bf16[2,1536,4608]{2,1,0:T(8,128)(2,1)} %w_ref.3), custom_call_target="tpu_custom_call" | custom-call | flops 905969664 | bytes 84934656 | tf_op jit(solution)/shard_map/ada_bwd/pallas_call | solution.py:331
  286.4 2.3 fusion.1
  288.7 2.0 copy.109
  290.7 2.2 maximum_select_fusion.2
  294.4 1.9 copy.97
  296.5 2.0 maximum_select_fusion
  298.6 5.1 %copy.107 = bf16[4,333,1536]{2,0,1:T(4,128)(2,1)} copy(bf16[4,333,1536]{2,1,0:T(8,128)(2,1)S(1)} %maximum_select_fusion) | data formatting | bytes 8183808
  303.7 1.8 copy.100
  305.9 1.8 maximum_select_fusion.1
  307.7 5.1 %copy.108 = bf16[4,333,1536]{2,0,1:T(4,128)(2,1)} copy(bf16[4,333,1536]{2,1,0:T(8,128)(2,1)S(1)} %maximum_select_fusion.1) | data formatting | bytes 8183808
  312.8 22.8 %wgrad_out.1 = f32[2,1536,1536]{2,1,0:T(8,128)} custom-call(s32[1]{0:T(128)} %bitcast.12.core_ref, bf16[2,256,1536]{2,1,0:T(8,128)(2,1)} %get-tuple-element.42.lo_i_ref, bf16[2,256,1536]{2,1,0:T(8,128)(2,1)} %collective-permute-done.8.lp_i_ref, bf16[2,384,1536]{2,1,0:T(8,128)(2,1)} %get-tuple-element.43.lo_t_ref, ...), custom_call_target="tpu_custom_call" | custom-call | flops 12079595520 | bytes 18874368 | tf_op jit(solution)/shard_map/wgrad_out/pallas_call | solution.py:285
  335.7 51.6 %wgrad_qkv.1 = f32[2,1536,4608]{2,1,0:T(8,128)} custom-call(s32[1]{0:T(128)} %bitcast.12.core_ref, bf16[2,256,1536]{2,1,0:T(8,128)(2,1)} %get-tuple-element.38.lo_i_ref, bf16[2,256,1536]{2,1,0:T(8,128)(2,1)} %collective-permute-done.4.lp_i_ref, bf16[2,384,1536]{2,1,0:T(8,128)(2,1)} %get-tuple-element.39.lo_t_ref, ...), custom_call_target="tpu_custom_call" | custom-call | flops 36238786560 | bytes 56623104 | tf_op jit(solution)/shard_map/wgrad_qkv/pallas_call | solution.py:285
  (98 shorter events, 18.2 us)
Async XLA Ops:
  4.1 4.8 %copy-start.12 = (f32[2,2,64]{2,1,0:T(2,128)S(1)}, f32[2,2,64]{2,1,0:T(2,128)}, u32[]{:S(2)}) copy-start(f32[2,2,64]{2,1,0:T(2,128)} %param.19) | copy-start | bytes 3076
  4.1 5.0 %copy-start.11 = (bf16[4,1536]{1,0:T(4,128)(2,1)S(1)}, bf16[4,1536]{1,0:T(4,128)(2,1)}, u32[]{:S(2)}) copy-start(bf16[4,1536]{1,0:T(4,128)(2,1)} %param.14) | copy-start | bytes 36868
  4.1 42.3 %all-to-all-start = ((bf16[4,2,2,64,1536]{4,3,2,1,0:T(8,128)(2,1)}), bf16[4,2,2,64,1536]{4,3,2,1,0:T(8,128)(2,1)}, u32[]{:S(2)}, u32[]{:S(2)}) async-start(bf16[4,2,2,64,1536]{4,3,2,1,0:T(8,128)(2,1)} %pad_maximum_fusion), calls=%async_computation | async-start | bytes 6291456 | tf_op jit(solution)/shard_map/all_to_all | solution.py:367
  9.3 11.6 %copy-start.3 = (f32[4,1536]{0,1:T(8,128)}, f32[4,1536]{0,1:T(8,128)S(1)}, u32[]{:S(2)}) copy-start(f32[4,1536]{0,1:T(8,128)S(1)} %copy.93) | copy-start | bytes 73732
  9.6 11.4 %copy-start.5 = (bf16[4,1536]{0,1:T(8,128)(2,1)}, bf16[4,1536]{0,1:T(8,128)(2,1)S(1)}, u32[]{:S(2)}) copy-start(bf16[4,1536]{0,1:T(8,128)(2,1)S(1)} %multiply_convert_fusion) | copy-start | bytes 36868
  228.8 4.2 %copy-start.9 = (bf16[2,256,1536]{2,1,0:T(8,128)(2,1)S(1)}, bf16[2,256,1536]{2,1,0:T(8,128)(2,1)}, u32[]{:S(2)}) copy-start(bf16[2,256,1536]{2,1,0:T(8,128)(2,1)} %get-tuple-element.29) | copy-start | bytes 4718596
  228.8 106.9 %collective-permute-start.7 = (bf16[2,3,384,1536]{3,2,1,0:T(8,128)(2,1)}, bf16[2,3,384,1536]{3,2,1,0:T(8,128)(2,1)}, u32[]{:S(2)}, u32[]{:S(2)}) collective-permute-start(bf16[2,3,384,1536]{3,2,1,0:T(8,128)(2,1)} %get-tuple-element.41.ro_t_ref), channel_id=1, source_target_pairs={{0,1},{1,0},{2,3},{3,2},{4,5},{5,4},{6,7},{7,6},{8,9},{9,8},{10,11... | collective-permute-start | bytes 21233672 | tf_op jit(solution)/shard_map/ppermute | solution.py:350
  229.9 16.7 %collective-permute-start.10 = (bf16[2,1,256,1536]{3,2,1,0:T(8,128)(2,1)}, bf16[2,1,256,1536]{3,2,1,0:T(8,128)(2,1)}, u32[]{:S(2)}, u32[]{:S(2)}) collective-permute-start(bf16[2,1,256,1536]{3,2,1,0:T(8,128)(2,1)} %bitcast.33), channel_id=1, source_target_pairs={{0,1},{1,0},{2,3},{3,2},{4,5},{5,4},{6,7},{7,6},{8,9},{9,8},{10,11... | collective-permute-start | bytes 4718600 | tf_op jit(solution)/shard_map/ppermute | solution.py:350
  232.8 9.7 %collective-permute-start.3 = (f32[30976]{0:T(1024)S(1)}, f32[30976]{0:T(1024)S(1)}, u32[]{:S(2)}, u32[]{:S(2)}) collective-permute-start(f32[30976]{0:T(1024)S(1)} %pad_maximum_fusion.2), channel_id=1, source_target_pairs={{0,1},{1,0},{2,3},{3,2},{4,5},{5,4},{6,7},{7,6},{8,9},{9,8},{10,11... | collective-permute-start | bytes 371720 | tf_op jit(solution)/shard_map/ppermute | solution.py:350
  233.0 2.8 copy-start.8
  235.3 11.0 %collective-permute-start = (bf16[2,2,64,1536]{3,2,0,1:T(8,128)(2,1)S(1)}, bf16[2,2,64,1536]{3,2,0,1:T(8,128)(2,1)S(1)}, u32[]{:S(2)}, u32[]{:S(2)}) collective-permute-start(bf16[2,2,64,1536]{3,2,0,1:T(8,128)(2,1)S(1)} %get-tuple-element.109), channel_id=1, source_target_pairs={{0,1},{1,0},{2,3},{3,2},{4,5},{5,4},{6,7},{7,6},{8,9},{9,8},{10,11... | collective-permute-start | bytes 2359304 | tf_op jit(solution)/shard_map/ppermute | solution.py:350
  235.7 13.0 %collective-permute-start.8 = (bf16[2,256,1536]{2,1,0:T(8,128)(2,1)}, bf16[2,256,1536]{2,1,0:T(8,128)(2,1)}, u32[]{:S(2)}, u32[]{:S(2)}) collective-permute-start(bf16[2,256,1536]{2,1,0:T(8,128)(2,1)} %get-tuple-element.42.lo_i_ref), channel_id=1, source_target_pairs={{0,1},{1,0},{2,3},{3,2},{4,5},{5,4},{6,7},{7,6},{8,9},{9,8},{10,11... | collective-permute-start | bytes 4718600 | tf_op jit(solution)/shard_map/ppermute | solution.py:350
  235.9 6.9 %copy-start.1 = (bf16[2,333,1536]{2,1,0:T(8,128)(2,1)}, bf16[2,333,1536]{2,1,0:T(8,128)(2,1)S(1)}, u32[]{:S(2)}) copy-start(bf16[2,333,1536]{2,1,0:T(8,128)(2,1)S(1)} %slice.75) | copy-start | bytes 6137860
  235.9 6.7 %copy-start.7 = (bf16[2,384,1536]{2,1,0:T(8,128)(2,1)S(1)}, bf16[2,384,1536]{2,1,0:T(8,128)(2,1)}, u32[]{:S(2)}) copy-start(bf16[2,384,1536]{2,1,0:T(8,128)(2,1)} %get-tuple-element.32) | copy-start | bytes 7077892
  242.6 43.5 %collective-permute-start.1 = (bf16[2,333,1536]{2,0,1:T(2,128)(2,1)}, bf16[2,333,1536]{2,0,1:T(2,128)(2,1)}, u32[]{:S(2)}, u32[]{:S(2)}) collective-permute-start(bf16[2,333,1536]{2,0,1:T(2,128)(2,1)} %copy.96), channel_id=1, source_target_pairs={{0,1},{1,0},{2,3},{3,2},{4,5},{5,4},{6,7},{7,6},{8,9},{9,8},{10,11... | collective-permute-start | bytes 6137864 | tf_op jit(solution)/shard_map/ppermute | solution.py:350
  242.8 4.7 %copy-start.6 = (bf16[4,1536]{0,1:T(8,128)(2,1)S(1)}, bf16[4,1536]{0,1:T(8,128)(2,1)}, u32[]{:S(2)}) copy-start(bf16[4,1536]{0,1:T(8,128)(2,1)} %copy-done.5) | copy-start | bytes 36868
  246.3 46.6 %collective-permute-start.2 = (bf16[2,333,1536]{2,0,1:T(2,128)(2,1)}, bf16[2,333,1536]{2,0,1:T(2,128)(2,1)}, u32[]{:S(2)}, u32[]{:S(2)}) collective-permute-start(bf16[2,333,1536]{2,0,1:T(2,128)(2,1)} %copy.99), channel_id=1, source_target_pairs={{0,1},{1,0},{2,3},{3,2},{4,5},{5,4},{6,7},{7,6},{8,9},{9,8},{10,11... | collective-permute-start | bytes 6137864 | tf_op jit(solution)/shard_map/ppermute | solution.py:350
  247.1 88.5 %collective-permute-start.6 = (bf16[2,3,256,1536]{3,2,1,0:T(8,128)(2,1)}, bf16[2,3,256,1536]{3,2,1,0:T(8,128)(2,1)}, u32[]{:S(2)}, u32[]{:S(2)}) collective-permute-start(bf16[2,3,256,1536]{3,2,1,0:T(8,128)(2,1)} %get-tuple-element.40.ro_i_ref), channel_id=1, source_target_pairs={{0,1},{1,0},{2,3},{3,2},{4,5},{5,4},{6,7},{7,6},{8,9},{9,8},{10,11... | collective-permute-start | bytes 14155784 | tf_op jit(solution)/shard_map/ppermute | solution.py:350
  248.6 37.7 %copy-start.4 = (f32[4,1536]{0,1:T(8,128)S(1)}, f32[4,1536]{0,1:T(8,128)}, u32[]{:S(2)}) copy-start(f32[4,1536]{0,1:T(8,128)} %copy-done.3) | copy-start | bytes 73732
  248.7 56.8 %collective-permute-start.11 = (bf16[2,1,384,1536]{3,2,1,0:T(8,128)(2,1)}, bf16[2,1,384,1536]{3,2,1,0:T(8,128)(2,1)}, u32[]{:S(2)}, u32[]{:S(2)}) collective-permute-start(bf16[2,1,384,1536]{3,2,1,0:T(8,128)(2,1)} %bitcast.31), channel_id=1, source_target_pairs={{0,1},{1,0},{2,3},{3,2},{4,5},{5,4},{6,7},{7,6},{8,9},{9,8},{10,11... | collective-permute-start | bytes 7077896 | tf_op jit(solution)/shard_map/ppermute | solution.py:350
  286.0 26.8 %collective-permute-start.9 = (bf16[2,384,1536]{2,1,0:T(8,128)(2,1)}, bf16[2,384,1536]{2,1,0:T(8,128)(2,1)}, u32[]{:S(2)}, u32[]{:S(2)}) collective-permute-start(bf16[2,384,1536]{2,1,0:T(8,128)(2,1)} %get-tuple-element.43.lo_t_ref), channel_id=1, source_target_pairs={{0,1},{1,0},{2,3},{3,2},{4,5},{5,4},{6,7},{7,6},{8,9},{9,8},{10,11... | collective-permute-start | bytes 7077896 | tf_op jit(solution)/shard_map/ppermute | solution.py:350
  292.9 42.8 %collective-permute-start.5 = (bf16[2,384,1536]{2,1,0:T(8,128)(2,1)}, bf16[2,384,1536]{2,1,0:T(8,128)(2,1)}, u32[]{:S(2)}, u32[]{:S(2)}) collective-permute-start(bf16[2,384,1536]{2,1,0:T(8,128)(2,1)} %get-tuple-element.39.lo_t_ref), channel_id=1, source_target_pairs={{0,1},{1,0},{2,3},{3,2},{4,5},{5,4},{6,7},{7,6},{8,9},{9,8},{10,11... | collective-permute-start | bytes 7077896 | tf_op jit(solution)/shard_map/ppermute | solution.py:350
  294.4 2.2 copy-start.2
  305.5 30.2 %collective-permute-start.4 = (bf16[2,256,1536]{2,1,0:T(8,128)(2,1)}, bf16[2,256,1536]{2,1,0:T(8,128)(2,1)}, u32[]{:S(2)}, u32[]{:S(2)}) collective-permute-start(bf16[2,256,1536]{2,1,0:T(8,128)(2,1)} %get-tuple-element.38.lo_i_ref), channel_id=1, source_target_pairs={{0,1},{1,0},{2,3},{3,2},{4,5},{5,4},{6,7},{7,6},{8,9},{9,8},{10,11... | collective-permute-start | bytes 4718600 | tf_op jit(solution)/shard_map/ppermute | solution.py:350
  (2 other events, 1.8 us)

commit v2 on v1

v2 whole, which is shorter than its diff:
```python
import functools
import math
import jax
import jax.numpy as jnp
from jax import lax
from jax.experimental import pallas as pl
from jax.experimental.pallas import tpu as pltpu
from jax.sharding import PartitionSpec as P

NORM_EPS = 1e-6
F32 = jnp.float32
BF16 = jnp.bfloat16
NN = (((1,), (0,)), ((), ()))
NT = (((1,), (1,)), ((), ()))
TN = (((0,), (0,)), ((), ()))


def dot(lhs, rhs, dims=NN):
    return lax.dot_general(lhs, rhs, dims, preferred_element_type=F32)


def round_up(num, mult):
    return -(-num // mult) * mult


def stats(tokens):
    avg_val = jnp.mean(tokens, axis=-1, keepdims=True)
    centred = tokens - avg_val
    var_val = jnp.mean(centred * centred, axis=-1, keepdims=True)
    inv_std = lax.rsqrt(var_val + NORM_EPS)
    return centred * inv_std, inv_std


def prologue(tok_ref, cot_ref, mod_ref, hid_ref, hid_trn_ref, dy_ref, base, n_valid, chunk):
    @pl.loop(0, tok_ref.shape[0] // chunk)
    def _(step):
        rows = pl.ds(pl.multiple_of(step * chunk, chunk), chunk)
        dst = pl.ds(pl.multiple_of(base + step * chunk, chunk), chunk)
        normed, _ = stats(tok_ref[rows].astype(F32))
        hid = normed * (1.0 + mod_ref[1:2]) + mod_ref[0:1]
        if n_valid < tok_ref.shape[0]:
            row = step * chunk + lax.broadcasted_iota(jnp.int32, hid.shape, 0)
            hid = jnp.where(row < n_valid, hid, 0.0)
        hid = hid.astype(BF16)
        hid_ref[dst] = hid
        hid_trn_ref[:, dst] = hid.T
        dy_ref[dst] = (cot_ref[rows].astype(F32) * mod_ref[2:3]).astype(BF16)


def epilogue(tok_ref, cot_ref, mod_ref, bias, y_ref, acc_ref, new_ref, grad_ref, sums_ref, base, chunk):
    sums_ref[base:base + 4] = jnp.zeros((4, sums_ref.shape[1]), F32)

    @pl.loop(0, tok_ref.shape[0] // chunk)
    def _(step):
        rows = pl.ds(pl.multiple_of(step * chunk, chunk), chunk)
        tokens, cot = tok_ref[rows].astype(F32), cot_ref[rows].astype(F32)
        gate = mod_ref[2:3]
        y_out = y_ref[rows] + bias
        new_ref[rows] = (tokens + gate * y_out).astype(BF16)
        normed, inv_std = stats(tokens)
        d_hid = acc_ref[rows].astype(BF16).astype(F32)
        d_normed = d_hid * (1.0 + mod_ref[1:2])
        mean_d = jnp.mean(d_normed, axis=-1, keepdims=True)
        mean_dn = jnp.mean(d_normed * normed, axis=-1, keepdims=True)
        grad_ref[rows] = (cot + inv_std * (d_normed - mean_d - normed * mean_dn)).astype(BF16)
        sums_ref[base:base + 1] += jnp.sum(d_hid, axis=0, keepdims=True)
        sums_ref[base + 1:base + 2] += jnp.sum(d_hid * normed, axis=0, keepdims=True)
        sums_ref[base + 2:base + 3] += jnp.sum(cot * y_out, axis=0, keepdims=True)
        sums_ref[base + 3:base + 4] += jnp.sum(cot * gate, axis=0, keepdims=True)


def block_kernel(n_keys, heads, tok_i_ref, cot_i_ref, tok_t_ref, cot_t_ref, mod_ref, bo_ref, wq_ref, wk_ref, wv_ref, bq_ref, bk_ref, bv_ref, gain_ref, wo_ref,
                 hid_trn_ref, dy_ref, o_trn_ref, dp_ref, new_i_ref, new_t_ref, grad_i_ref, grad_t_ref, sums_ref, dg_ref, db_ref,
                 hid_ref, tok_ref, cot_ref, y_i_ref, y_t_ref, acc_i_ref, acc_t_ref, hat_ref, inv_ref, nat_ref, trn_ref, v_ref, do_nat_ref, do_trn_ref, dq_ref, dk_ref, dv_ref):
    step_b, step_g = pl.program_id(0), pl.program_id(1)
    n_grp = pl.num_programs(1)
    n_img = tok_ref.shape[0]
    width = wq_ref.shape[2]
    head_dim = width // heads
    att_scale = head_dim ** -0.5
    n_tok = n_img + tok_t_ref.shape[1]
    k_rows = round_up(n_keys, 16)
    k_main = k_rows - 16

    @pl.when(step_g == 0)
    def _():
        tok_ref[...] = tok_i_ref[:, 0, 0].reshape(tok_ref.shape)
        cot_ref[...] = cot_i_ref[:, 0, 0].reshape(cot_ref.shape)
        prologue(tok_ref, cot_ref, mod_ref.at[0, 0], hid_ref, hid_trn_ref.at[0], dy_ref.at[0], 0, n_img, 128)
        prologue(tok_t_ref.at[0], cot_t_ref.at[0], mod_ref.at[0, 1], hid_ref, hid_trn_ref.at[0], dy_ref.at[0], n_img, n_keys - n_img, 128)

    hid_i, hid_t = hid_ref[:n_img], hid_ref[n_img:]
    for idx, (w_ref, b_ref) in enumerate(((wq_ref, bq_ref), (wk_ref, bk_ref), (wv_ref, bv_ref))):
        raw_i = dot(hid_i, w_ref[0]) + b_ref[0:1, :]
        raw_t = dot(hid_t, w_ref[1]) + b_ref[1:2, :]
        if idx == 2:
            v_ref[:n_img] = raw_i.astype(BF16)
            v_ref[n_img:] = raw_t.astype(BF16)
            trn_ref[2, :, :n_img] = raw_i.T.astype(BF16)
            trn_ref[2, :, n_img:] = raw_t.T.astype(BF16)
        else:
            raw = jnp.concatenate([raw_i.T, raw_t.T], axis=1).reshape(heads, head_dim, n_tok)
            inv = lax.rsqrt(jnp.mean(raw * raw, axis=1, keepdims=True) + NORM_EPS)
            hat = (raw * inv).reshape(width, n_tok)
            normed = hat * gain_ref[idx]
            hat_ref[idx] = hat
            inv_ref[idx] = inv
            trn_ref[idx] = normed.astype(BF16)
            nat_ref[idx] = normed.T.astype(BF16)

    do_i = dot(dy_ref[0, :n_img], wo_ref[0], NT)
    do_t = dot(dy_ref[0, n_img:], wo_ref[1], NT)
    do_nat_ref[:n_img] = do_i.astype(BF16)
    do_nat_ref[n_img:] = do_t.astype(BF16)
    do_trn_ref[:, :n_img] = do_i.T.astype(BF16)
    do_trn_ref[:, n_img:] = do_t.T.astype(BF16)
    dk_ref[k_rows:] = jnp.zeros((n_tok - k_rows, width), F32)
    dv_ref[k_rows:] = jnp.zeros((n_tok - k_rows, width), F32)

    exp_scale = att_scale * math.log2(math.e)
    for head in range(heads):
        rows = slice(head * head_dim, (head + 1) * head_dim)
        q_trn, k_trn, v_trn = trn_ref[0, rows, :], trn_ref[1, rows, :k_rows], trn_ref[2, rows, :k_rows]
        q_nat, k_nat, v_nat = nat_ref[0, :, rows], nat_ref[1, :k_rows, rows], v_ref[:k_rows, rows]
        scores = dot(k_nat, q_trn)
        tail_row = k_main + lax.broadcasted_iota(jnp.int32, (16, n_tok), 0)
        tail = jnp.where(tail_row < n_keys, scores[k_main:], -jnp.inf)
        scores = jnp.concatenate([scores[:k_main], tail], axis=0)
        peak = jnp.max(scores, axis=0, keepdims=True)
        exps = jnp.exp2((scores - peak) * exp_scale)
        prob = exps * (1.0 / jnp.sum(exps, axis=0, keepdims=True))
        prob_lo = prob.astype(BF16)
        out_trn = dot(v_trn, prob_lo).astype(BF16)
        o_trn_ref[0, rows] = out_trn
        do_trn = do_trn_ref[rows]
        delta = jnp.sum(out_trn.astype(F32) * do_trn.astype(F32), axis=0, keepdims=True)
        d_prob = dot(v_nat, do_trn)
        d_score = (prob * (d_prob - delta)).astype(BF16)
        dv_ref[:k_rows, rows] = dot(prob_lo, do_nat_ref[:, rows])
        dk_ref[:k_rows, rows] = dot(d_score, q_nat) * att_scale
        dq_ref[rows] = dot(k_trn, d_score) * att_scale

    o_nat = o_trn_ref[0].T

    @pl.when(step_g == 0)
    def _():
        y_i_ref[...] = jnp.zeros_like(y_i_ref)
        y_t_ref[...] = jnp.zeros_like(y_t_ref)
        acc_i_ref[...] = jnp.zeros_like(acc_i_ref)
        acc_t_ref[...] = jnp.zeros_like(acc_t_ref)

    @pl.when((step_g == 0) & (step_b == 0))
    def _():
        dg_ref[...] = jnp.zeros_like(dg_ref)

    y_i_ref[...] += dot(o_nat[:n_img], wo_ref[0])
    y_t_ref[...] += dot(o_nat[n_img:], wo_ref[1])

    d_raw = []
    for idx in range(2):
        d_out = dq_ref[...] if idx == 0 else dk_ref[...].T
        d_out = d_out.astype(BF16).astype(F32)
        hat = hat_ref[idx]
        prod = d_out * hat
        dg_ref[idx] += sum(prod[:, lo:lo + 128] for lo in range(0, n_img, 128))
        dg_ref[2 + idx] += sum(prod[:, lo:lo + 128] for lo in range(n_img, n_tok, 128))
        d_hat = (d_out * gain_ref[idx]).reshape(heads, head_dim, n_tok)
        hat = hat.reshape(heads, head_dim, n_tok)
        mean_dh = jnp.mean(d_hat * hat, axis=1, keepdims=True)
        d_raw.append((inv_ref[idx] * (d_hat - hat * mean_dh)).reshape(width, n_tok).T)
    d_raw.append(dv_ref[...].astype(BF16).astype(F32))
    sums = []
    d_lo = []
    for idx in range(3):
        lo = d_raw[idx].astype(BF16)
        dp_ref[0, idx] = lo
        d_lo.append(lo)
        db_ref[0, idx:idx + 1, :] = jnp.sum(d_raw[idx][:n_img], axis=0, keepdims=True)
        db_ref[0, 3 + idx:4 + idx, :] = jnp.sum(d_raw[idx][n_img:], axis=0, keepdims=True)
    db_ref[0, 6:8, :] = jnp.zeros((2, width), F32)
    w_refs = (wq_ref, wk_ref, wv_ref)
    acc_i_ref[...] += sum(dot(d_lo[idx][:n_img], w_refs[idx][0], NT) for idx in range(3))
    acc_t_ref[...] += sum(dot(d_lo[idx][n_img:], w_refs[idx][1], NT) for idx in range(3))

    @pl.when(step_g == n_grp - 1)
    def _():
        epilogue(tok_ref, cot_ref, mod_ref.at[0, 0], bo_ref[0:1], y_i_ref, acc_i_ref, new_i_ref.at[0], grad_i_ref.at[0], sums_ref.at[0], 0, 64)
        epilogue(tok_t_ref.at[0], cot_t_ref.at[0], mod_ref.at[0, 1], bo_ref[1:2], y_t_ref, acc_t_ref, new_t_ref.at[0], grad_t_ref.at[0], sums_ref.at[0], 4, 64)


def fused_block(tokens, text, cot_t, mod, b_out, w_qkv, b_qkv, qk_gain, w_out, n_keys, heads):
    n_src, _, n_b, tok_dev, d_model = tokens.shape
    n_img, n_txt = n_src * tok_dev, text.shape[1]
    n_tok = n_img + n_txt
    head_dim = qk_gain.shape[-1]
    width = heads * head_dim
    n_grp = d_model // width
    gain_cols = jnp.tile(qk_gain, (1, 1, heads))
    gain_full = jnp.concatenate([jnp.broadcast_to(gain_cols[0][:, :, None], (2, width, n_img)), jnp.broadcast_to(gain_cols[1][:, :, None], (2, width, n_txt))], axis=2)

    def rows_spec(n_rows, **mode):
        return pl.BlockSpec((1, n_rows, d_model), lambda b, g: (b, 0, 0), **mode)

    def w_spec(idx):
        return pl.BlockSpec((2, d_model, width), lambda b, g: (0, 0, idx * n_grp + g))

    def b_spec(idx):
        return pl.BlockSpec((2, width), lambda b, g: (0, idx * n_grp + g))

    def img_spec(idx):
        return pl.BlockSpec((n_src, 1, 1, tok_dev, d_model), lambda b, g: (0, idx, b, 0, 0), pipeline_mode=pl.Buffered(1))

    once = pl.Buffered(1)
    in_specs = [img_spec(0), img_spec(1), rows_spec(n_txt, pipeline_mode=once), rows_spec(n_txt, pipeline_mode=once), pl.BlockSpec((1, 2, 3, d_model), lambda b, g: (b, 0, 0, 0)), pl.BlockSpec((2, d_model), lambda b, g: (0, 0)), w_spec(0), w_spec(1), w_spec(2), b_spec(0), b_spec(1), b_spec(2),
                pl.BlockSpec((2, width, n_tok), lambda b, g: (0, 0, 0)), pl.BlockSpec((2, width, d_model), lambda b, g: (0, g, 0))]
    out_specs = [pl.BlockSpec((1, d_model, n_tok), lambda b, g: (b, 0, 0)), rows_spec(n_tok), pl.BlockSpec((1, width, n_tok), lambda b, g: (b, g, 0)), pl.BlockSpec((1, 3, n_tok, width), lambda b, g: (b, 0, 0, g)),
                 rows_spec(n_img), rows_spec(n_txt), rows_spec(n_img), rows_spec(n_txt), pl.BlockSpec((1, 8, d_model), lambda b, g: (b, 0, 0)),
                 pl.BlockSpec((4, width, 128), lambda b, g: (0, 0, 0)), pl.BlockSpec((1, 8, width), lambda b, g: (b, 0, g))]
    shape = jax.ShapeDtypeStruct
    rows_shape = [shape((n_b, n_img, d_model), BF16), shape((n_b, n_txt, d_model), BF16)]
    out_shape = [shape((n_b, d_model, n_tok), BF16), shape((n_b, n_tok, d_model), BF16), shape((n_b, d_model, n_tok), BF16), shape((n_b, 3, n_tok, d_model), BF16),
                 *(rows_shape * 2), shape((n_b, 8, d_model), F32), shape((4, width, 128), F32), shape((n_b, 8, d_model), F32)]
    scratch = [pltpu.VMEM((n_tok, d_model), BF16), pltpu.VMEM((n_img, d_model), BF16), pltpu.VMEM((n_img, d_model), BF16),
               pltpu.VMEM((n_img, d_model), F32), pltpu.VMEM((n_txt, d_model), F32), pltpu.VMEM((n_img, d_model), F32), pltpu.VMEM((n_txt, d_model), F32),
               pltpu.VMEM((2, width, n_tok), F32), pltpu.VMEM((2, heads, 1, n_tok), F32),
               pltpu.VMEM((2, n_tok, width), BF16), pltpu.VMEM((3, width, n_tok), BF16), pltpu.VMEM((n_tok, width), BF16),
               pltpu.VMEM((n_tok, width), BF16), pltpu.VMEM((width, n_tok), BF16),
               pltpu.VMEM((width, n_tok), F32), pltpu.VMEM((n_tok, width), F32), pltpu.VMEM((n_tok, width), F32)]
    flops = n_b * n_tok * d_model * d_model * 16 + n_b * d_model * n_tok * n_tok * 12
    return pl.pallas_call(
        functools.partial(block_kernel, n_keys, heads),
        out_shape=out_shape, grid=(n_b, n_grp), in_specs=in_specs, out_specs=out_specs, scratch_shapes=scratch,
        compiler_params=pltpu.CompilerParams(dimension_semantics=("arbitrary", "arbitrary"), vmem_limit_bytes=67043328),
        cost_estimate=pl.CostEstimate(flops=flops, bytes_accessed=100 * 1024 * 1024, transcendentals=0),
        name="fused_block",
    )(tokens, tokens, text, cot_t, mod, b_out, w_qkv, w_qkv, w_qkv, b_qkv, b_qkv, b_qkv, gain_full, w_out)


def wgrad_kernel(n_img, n_b, with_ada, core_ref, *refs):
    lefts, rights, refs = refs[:2 * n_b], refs[2 * n_b:4 * n_b], refs[4 * n_b:]
    if with_ada:
        act_ref, dmod_ref, dmod_trn_ref, w_ref, out_ref, dw_ref, dact_ref, trn_i_ref, trn_t_ref, rhs_i_ref, rhs_t_ref = refs
    else:
        out_ref, trn_i_ref, trn_t_ref, rhs_i_ref, rhs_t_ref = refs
    d_model, n_tok = lefts[0].shape[1:]
    n_txt = n_tok - n_img
    core = core_ref[0]

    def place(idx, n_rows):
        pos = core * n_b + idx if idx < n_b else (1 - core) * n_b + idx - n_b
        return pl.ds(pl.multiple_of(pos * n_rows, n_rows), n_rows)

    @pl.when(pl.program_id(0) == 0)
    def _():
        for idx in range(2 * n_b):
            trn_i_ref[:, place(idx, n_img)] = lefts[idx][0, :, :n_img]
            trn_t_ref[:, place(idx, n_txt)] = lefts[idx][0, :, n_img:]
        if with_ada:
            dact_ref[...] = jnp.zeros_like(dact_ref)

    for idx in range(2 * n_b):
        rhs_i_ref[place(idx, n_img)] = rights[idx][0, 0, :n_img]
        rhs_t_ref[place(idx, n_txt)] = rights[idx][0, 0, n_img:]

    chunk = 512

    @pl.loop(0, d_model // chunk)
    def _(step):
        rows = pl.ds(pl.multiple_of(step * chunk, chunk), chunk)
        out_ref[0, rows] = dot(trn_i_ref[rows], rhs_i_ref[...])
        out_ref[1, rows] = dot(trn_t_ref[rows], rhs_t_ref[...])
        if with_ada:
            for branch in range(2):
                dw_ref[branch, rows] = dot(act_ref[rows], dmod_ref[branch].astype(BF16))
                dact_ref[rows] += dot(w_ref[branch, rows], dmod_trn_ref[branch].astype(BF16))


def wgrad(core, lefts, rights, n_img, block, name, ada=None):
    n_b = len(lefts) // 2
    _, d_model, n_tok = lefts[0].shape
    n_c, wide = rights[0].shape[1], rights[0].shape[3]
    per = wide // block
    cols = n_c * wide
    left_spec = pl.BlockSpec((1, d_model, n_tok), lambda j: (0, 0, 0), pipeline_mode=pl.Buffered(1))
    right_spec = pl.BlockSpec((1, 1, n_tok, block), lambda j: (0, j // per, 0, j % per))
    mat_spec = pl.BlockSpec((2, d_model, block), lambda j: (0, 0, j))
    in_specs = [pl.BlockSpec(memory_space=pltpu.SMEM)] + [left_spec] * (2 * n_b) + [right_spec] * (2 * n_b)
    out_shape, out_specs, extra = [jax.ShapeDtypeStruct((2, d_model, cols), F32)], [mat_spec], []
    if ada is not None:
        cond_act, d_mod, w_ada = ada
        n_batch = cond_act.shape[0]
        d_mod = jnp.pad(d_mod, ((0, 0), (0, 16 - n_batch), (0, 0)))
        extra = [jnp.pad(cond_act, ((0, 16 - n_batch), (0, 0))).T, d_mod, d_mod.swapaxes(1, 2), w_ada]
        in_specs += [pl.BlockSpec((d_model, 16), lambda j: (0, 0)), pl.BlockSpec((2, 16, block), lambda j: (0, 0, j)), pl.BlockSpec((2, block, 16), lambda j: (0, j, 0)), mat_spec]
        out_shape += [jax.ShapeDtypeStruct((2, d_model, cols), F32), jax.ShapeDtypeStruct((d_model, 16), F32)]
        out_specs += [mat_spec, pl.BlockSpec((d_model, 16), lambda j: (0, 0))]
    return pl.pallas_call(
        functools.partial(wgrad_kernel, n_img, n_b, ada is not None),
        out_shape=out_shape, grid=(n_c * per,), in_specs=in_specs, out_specs=out_specs,
        scratch_shapes=[pltpu.VMEM((d_model, 2 * n_b * n_img), BF16), pltpu.VMEM((d_model, 2 * n_b * (n_tok - n_img)), BF16),
                        pltpu.VMEM((2 * n_b * n_img, block), BF16), pltpu.VMEM((2 * n_b * (n_tok - n_img), block), BF16)],
        compiler_params=pltpu.CompilerParams(dimension_semantics=("arbitrary",), vmem_limit_bytes=60 * 1024 * 1024),
        cost_estimate=pl.CostEstimate(flops=4 * n_b * n_tok * d_model * cols, bytes_accessed=(8 if ada is None else 24) * d_model * cols, transcendentals=0),
        name=name,
    )(core[None], *lefts, *rights, *extra)


def ada_fwd_kernel(act_ref, w_ref, b_ref, out_ref):
    out_ref[0] = dot(act_ref[...], w_ref[0]) + b_ref[pl.ds(pl.program_id(0), 1), :]


def ada_fwd(cond_act, w_ada, b_ada, block):
    n_b, d_model = cond_act.shape
    wide = w_ada.shape[2]
    act = jnp.pad(cond_act, ((0, 16 - n_b), (0, 0)))
    return pl.pallas_call(
        ada_fwd_kernel,
        out_shape=jax.ShapeDtypeStruct((2, 16, wide), F32), grid=(2, wide // block),
        in_specs=[pl.BlockSpec((16, d_model), lambda s, j: (0, 0)), pl.BlockSpec((1, d_model, block), lambda s, j: (s, 0, j)), pl.BlockSpec((2, block), lambda s, j: (0, j))],
        out_specs=pl.BlockSpec((1, 16, block), lambda s, j: (s, 0, j)),
        compiler_params=pltpu.CompilerParams(dimension_semantics=("arbitrary", "arbitrary"), vmem_limit_bytes=40 * 1024 * 1024),
        cost_estimate=pl.CostEstimate(flops=64 * d_model * wide, bytes_accessed=4 * d_model * wide, transcendentals=0),
        name="ada_fwd",
    )(act, w_ada, b_ada)[:, :n_b]


def solution(mesh):
    sp_size = mesh.shape['sp']
    pair = 2
    n_chips = sp_size // pair
    pairs = [(idx, idx + 1 - 2 * (idx % pair)) for idx in range(sp_size)]

    def swap(arr):
        return lax.ppermute(arr, 'sp', pairs)

    def both(arr):
        return arr, swap(arr)

    def device_fn(image_in, text_in, cond_vec, w_ada, b_ada, w_qkv, b_qkv, qk_gain, w_out, b_out, image_cot, text_cot):
        n_batch, tok_dev, d_model = image_in.shape
        ctx_len = text_in.shape[1]
        n_img = tok_dev * sp_size
        n_own = n_batch // pair
        n_txt = round_up(n_img + ctx_len, 128) - n_img
        me = lax.axis_index('sp')
        core, chip = lax.rem(me, pair), lax.div(me, pair)
        own_lo = core * n_own

        img_pair = jnp.stack([image_in, image_cot]).reshape(2, pair, n_own, 1, tok_dev, d_model)
        tokens = [lax.all_to_all(jnp.concatenate([img_pair[:, :, idx].swapaxes(0, 1)] * n_chips, axis=0), 'sp', 0, 0) for idx in range(n_own)]

        def own(arr, axis=0):
            return lax.dynamic_slice_in_dim(arr, own_lo, n_own, axis)

        def ordered(mine, other, axis=0):
            return jnp.where(core == 0, jnp.concatenate([mine, other], axis), jnp.concatenate([other, mine], axis))

        cond_act = jax.nn.silu(cond_vec.astype(F32)).astype(BF16)
        cond_mod = ada_fwd(cond_act, w_ada, b_ada, 1536)
        own_mod = own(cond_mod, 1).reshape(2, n_own, 3, d_model).swapaxes(0, 1)
        pad_rows = ((0, 0), (0, n_txt - ctx_len), (0, 0))
        text_own, cot_own = jnp.pad(own(text_in), pad_rows), jnp.pad(own(text_cot), pad_rows)

        outs = []
        for idx in range(n_own):
            one = slice(idx, idx + 1)
            outs.append(fused_block(tokens[idx], text_own[one], cot_own[one], own_mod[one], b_out, w_qkv, b_qkv, qk_gain, w_out, n_img + ctx_len, 4))
        sums, db = (jnp.concatenate([out[pos] for out in outs]) for pos in (8, 10))
        new_i, new_t, grad_i, grad_t = (jnp.concatenate([out[pos] for out in outs]) for pos in (4, 5, 6, 7))
        dg = sum(out[9] for out in outs)
        factors = [[out[pos] for out in outs] for pos in range(4)]
        factors[1] = [arr[:, None] for arr in factors[1]]
        hid_trn, dy, o_trn, dp = [arrs + [swap(arr) for arr in arrs] for arrs in factors]

        sums = sums.reshape(n_own, 2, 4, d_model)
        d_mod = sums[:, :, :3].swapaxes(0, 1).reshape(2, n_own, 3 * d_model)
        rest = jnp.concatenate([jnp.sum(sums[:, :, 3], 0).reshape(-1), jnp.sum(db, 0)[:6].reshape(-1), jnp.sum(jnp.sum(dg, -1).reshape(2, 2, -1, qk_gain.shape[-1]), 2).reshape(-1)])
        small = jnp.concatenate([d_mod.reshape(-1), rest])
        small_other = swap(small)
        d_mod_all = ordered(d_mod, small_other[:d_mod.size].reshape(d_mod.shape), 1)
        rest = rest + small_other[d_mod.size:]
        cut = (2 * d_model, 8 * d_model)
        db_out, db_qkv, d_gain = rest[:cut[0]].reshape(2, d_model), rest[cut[0]:cut[1]].reshape(2, 3 * d_model), rest[cut[1]:].reshape(qk_gain.shape)

        dw_out, = wgrad(core, o_trn, dy, n_img, 256, "wgrad_out")
        dw_qkv, dw_ada, d_act = wgrad(core, hid_trn, dp, n_img, 256, "wgrad_qkv", (cond_act, d_mod_all, w_ada))
        d_act = d_act.T[:n_batch]
        db_ada = jnp.sum(d_mod_all, axis=1)
        _, pull_act = jax.vjp(jax.nn.silu, cond_vec.astype(F32))
        grad_cond = pull_act(d_act.astype(BF16).astype(F32))[0]

        img_pair = jnp.stack([new_i, grad_i], axis=1)
        chip_lo = chip * pair * tok_dev
        img_mine = lax.dynamic_slice_in_dim(img_pair, chip_lo + core * tok_dev, tok_dev, 2)
        img_send = lax.dynamic_slice_in_dim(img_pair, chip_lo + (1 - core) * tok_dev, tok_dev, 2)
        img_pair = ordered(img_mine, swap(img_send))
        text_new, grad_text = ordered(*both(new_t[:, :ctx_len])), ordered(*both(grad_t[:, :ctx_len]))
        return (img_pair[:, 0], text_new, img_pair[:, 1], grad_text, grad_cond, dw_ada, db_ada, dw_qkv, db_qkv, d_gain, dw_out, db_out)

    data_spec = P('dp', 'sp', None)
    batch_spec = P('dp')
    rep_spec = P()
    in_specs = (data_spec, batch_spec, batch_spec, rep_spec, rep_spec, rep_spec, rep_spec, rep_spec, rep_spec, rep_spec, data_spec, batch_spec)
    out_specs = (data_spec, batch_spec, data_spec, batch_spec, batch_spec, batch_spec, batch_spec, batch_spec, batch_spec, batch_spec, batch_spec, batch_spec)
    return jax.shard_map(device_fn, mesh=mesh, in_specs=in_specs, out_specs=out_specs, check_vma=False)
```

time: 394 us -> 377 us (0.957)
  Pallas kernels: 302 us -> 274 us
  waiting for transfers between devices: 15.2 us -> 0.04 us
  local copies, waits for them, and re-layouts: 42.6 us -> 56.7 us
  other arithmetic: 18.5 us -> 24.8 us
  starting transfers between devices: 7.88 us -> 12.3 us
    pallas_call x1 -> x2, Pallas kernels: 182 us -> 163 us  [fused_block(): pl.pallas_call(functools.partial(block_kernel, n_keys, heads), out_shape=...]
    all_to_all x1 -> x2, waiting for transfers between devices: 12 us -> 0.01 us  [device_fn(): lax.all_to_all(jnp.concatenate([img_pair[:, :, idx].swapaxes(0, 1)] * n_c...]
    pallas_call x3 -> x2, Pallas kernels: 109 us -> 99.9 us  [wgrad(): pl.pallas_call(functools.partial(wgrad_kernel, n_img, n_b, ada is not Non...]
    concatenate x0 -> x2, local copies, waits for them, and re-layouts: none -> 5.85 us  [the longest x1 2.93 us: ordered(): jnp.concatenate([mine, other], axis)]
    transpose x1 -> x2, local copies, waits for them, and re-layouts: 0.08 us -> 5.6 us  [the longest x1 4.74 us: wgrad(): d_mod.swapaxes(1, 2)]
    reduce_sum x1, other arithmetic: 0.83 us -> 6.31 us  [device_fn(): db_ada = jnp.sum(d_mod_all, axis=1)]
    unnamed x32 -> x41, local copies, waits for them, and re-layouts: 13.7 us -> 18.1 us
    all_to_all x1 -> x2, starting transfers between devices: 4.77 us -> 9.02 us  [device_fn(): lax.all_to_all(jnp.concatenate([img_pair[:, :, idx].swapaxes(0, 1)] * n_c...]
  transfers between devices with their start and end apart: 13 -> 14, of which waited for: 2 -> 0; matrix products, arithmetic and copies ran while one was open for 15% -> 19% of each run, Pallas kernels for 18% -> 31%
where the time goes in v2:
time: 377 us; the launch traced here: 369 us
  Pallas kernels  274 us (73%)
  local copies, waits for them, and re-layouts  56.7 us (15%)
  other arithmetic  24.8 us (7%)
  starting transfers between devices  12.3 us (3%)
    pallas_call x2, Pallas kernels, fused_block(): pl.pallas_call(functools.partial(block_kernel, n_keys, heads), out_shape=...  163 us
    pallas_call x2, Pallas kernels, wgrad(): pl.pallas_call(functools.partial(wgrad_kernel, n_img, n_b, ada is not Non...  99.9 us
    unnamed x41, local copies, waits for them, and re-layouts  18.1 us
    pallas_call x1, Pallas kernels, ada_fwd(): pl.pallas_call(ada_fwd_kernel, out_shape=jax.ShapeDtypeStruct((2, 16, wid...  11.1 us
    all_to_all x2, starting transfers between devices, device_fn(): lax.all_to_all(jnp.concatenate([img_pair[:, :, idx].swapaxes(0, 1)] * n_c...  9.02 us
    dynamic_slice x2, local copies, waits for them, and re-layouts, own(): return lax.dynamic_slice_in_dim(arr, own_lo, n_own, axis)  7.65 us
  transfers between devices with their start and end apart: 14, of which 0 were waited for; matrix products, arithmetic and copies ran while one was open for 19% of the time, Pallas kernels for 31%

profile of v2, /device:TPU:0, one launch (start us, length us, event | category | flops | bytes accessed | tf_op | source)
XLA Modules:
  0.0 369.5 jit_solution(12118281428619462218)
XLA Ops:
  3.5 4.6 %all-to-all-start = ((bf16[4,2,1,64,1536]{4,3,1,2,0:T(8,128)(2,1)}), bf16[4,2,1,64,1536]{4,3,1,2,0:T(8,128)(2,1)}, u32[]{:S(2)}, u32[]{:S(2)}) async-start(bf16[4,2,1,64,1536]{4,3,1,2,0:T(8,128)(2,1)} %maximum_bitcast_fusion), calls=%async_computation | async-start | bytes 3145728 | tf_op jit(solution)/shard_map/all_to_all | solution.py:350
  10.9 7.6 %constant_dynamic-slice_fusion.1 = (bf16[2,333,1536]{2,0,1:T(2,128)(2,1)S(1)}, bf16[2,333,1536]{2,0,1:T(2,128)(2,1)S(1)}) fusion(bf16[4,333,1536]{2,0,1:T(4,128)(2,1)} %param.23, s32[]{:T(128)S(6)} %select_n.40, bf16[4,333,1536]{2,0,1:T(4,128)(2,1)} %param.13), kind=kLoop, calls=%fused_computation.48 | loop fusion | bytes 8183812 | tf_op jit(solution)/shard_map/dynamic_slice | solution.py:353
  20.8 11.1 %ada_fwd.1 = f32[2,16,4608]{2,1,0:T(8,128)S(1)} custom-call(bf16[16,1536]{1,0:T(8,128)(2,1)S(1)} %pad.18.clone.act_ref, bf16[2,1536,4608]{2,1,0:T(8,128)(2,1)} %refs_11_.1, f32[2,4608]{1,0:T(2,128)S(1)} %copy-done), custom_call_target="tpu_custom_call" | custom-call | flops 452984832 | bytes 28311552 | tf_op jit(solution)/shard_map/ada_fwd/pallas_call | solution.py:316
  34.4 1.6 pad_slice_fusion.3
  36.0 1.6 pad_slice_fusion.1
  38.3 4.4 %all-to-all-start.1 = ((bf16[4,2,1,64,1536]{4,3,2,1,0:T(8,128)(2,1)}), bf16[4,2,1,64,1536]{4,3,2,1,0:T(8,128)(2,1)}, u32[]{:S(2)}, u32[]{:S(2)}) async-start(bf16[4,2,1,64,1536]{4,3,2,1,0:T(8,128)(2,1)} %pad_maximum_fusion.2), calls=%async_computation.1 | async-start | bytes 3145728 | tf_op jit(solution)/shard_map/all_to_all | solution.py:350
  42.7 81.5 %fused_block.2 = (bf16[1,1536,640]{2,1,0:T(8,128)(2,1)}, bf16[1,640,1536]{2,1,0:T(8,128)(2,1)}, bf16[1,1536,640]{2,1,0:T(8,128)(2,1)}, bf16[1,3,640,1536]{3,2,1,...) custom-call(bf16[4,2,1,64,1536]{4,3,2,1,0:T(8,128)(2,1)} %bitcast.5., ...), custom_call_target="tpu_custom_call" | custom-call | flops 31708938240 | bytes 104857600 | tf_op jit(solution)/shard_map/fused_block/pallas_call | solution.py:230
  124.2 81.7 %fused_block.3 = (bf16[1,1536,640]{2,1,0:T(8,128)(2,1)}, bf16[1,640,1536]{2,1,0:T(8,128)(2,1)}, bf16[1,1536,640]{2,1,0:T(8,128)(2,1)}, bf16[1,3,640,1536]{3,2,1,...) custom-call(bf16[4,2,1,64,1536]{4,3,2,1,0:T(8,128)(2,1)} %all-to-all, ...), custom_call_target="tpu_custom_call" | custom-call | flops 31708938240 | bytes 104857600 | tf_op jit(solution)/shard_map/fused_block/pallas_call | solution.py:230
  214.3 3.4 copy.145
  217.9 3.4 copy.148
  221.7 2.9 copy.152
  224.6 2.9 copy.153
  228.0 6.3 %fusion.5 = (f32[2,4608]{1,0:T(2,128)}, f32[2,4,4608]{1,2,0:T(8,128)}) fusion(f32[2,4,4608]{1,2,0:T(8,128)} %copy.152, f32[2,4,4608]{1,2,0:T(8,128)} %copy.153, pred[]{:T(512)S(6)} %eq.2), kind=kLoop, calls=%fused_computation.54 | loop fusion | flops 64512 | bytes 479233 | tf_op jit(solution)/shard_map/reduce_sum | solution.py:388
  234.3 3.1 copy.171
  240.2 4.7 %pad_bitcast_fusion.1.refs_10_ = f32[2,4608,16]{2,1,0:T(8,128)} fusion(f32[2,4,4608]{1,2,0:T(8,128)} %get-tuple-element.135), kind=kLoop, calls=%fused_computation.53 | loop fusion | bytes 737280 | tf_op jit(solution)/shard_map/transpose | solution.py:293
  245.0 1.6 maximum_select_fusion.2
  248.8 22.5 %wgrad_out.1 = f32[2,1536,1536]{2,1,0:T(8,128)} custom-call(s32[1]{0:T(128)} %bitcast.15.core_ref, bf16[1,1536,640]{2,1,0:T(8,128)(2,1)} %get-tuple-element.58.refs_0_, bf16[1,1536,640]{2,1,0:T(8,128)(2,1)} %get-tuple-element.59.refs_1_, bf16[1,1536,640]{2,1,0:T(8,128)(2,1)} %collective-permute-done.8.refs_2_, ...), custom_call_target="tpu_custom_call" | custom-call | flops 12079595520 | bytes 18874368 | tf_op jit(solution)/shard_map/wgrad_out/pallas_call | solution.py:297
  271.3 1.9 copy.146
  273.5 2.0 maximum_select_fusion
  275.5 5.1 %copy.157 = bf16[4,333,1536]{2,0,1:T(4,128)(2,1)} copy(bf16[4,333,1536]{2,1,0:T(8,128)(2,1)S(1)} %maximum_select_fusion) | data formatting | bytes 8183808
  280.6 1.8 copy.149
  282.4 1.8 maximum_select_fusion.1
  284.2 5.1 %copy.158 = bf16[4,333,1536]{2,0,1:T(4,128)(2,1)} copy(bf16[4,333,1536]{2,1,0:T(8,128)(2,1)S(1)} %maximum_select_fusion.1) | data formatting | bytes 8183808
  289.4 77.4 %wgrad_qkv.1 = (f32[2,1536,4608]{2,1,0:T(8,128)}, f32[2,1536,4608]{2,1,0:T(8,128)}, f32[1536,16]{1,0:T(8,128)}) custom-call(s32[1]{0:T(128)} %bitcast.15.core_ref, bf16[1,1536,640]{2,1,0:T(8,128)(2,1)} %get-tuple-element.45.refs_0_, bf16[1,1536,640]{2,1,0:T(8,128)(2,1)} %get-tuple-element.46.refs_1_, bf16[1,1536,640]{2,1,0:T(8,128)(2,1)} %collective-permute-done.3.refs_2_, ...), custom_call_target="tpu_custom_call" | custom-call | flops 36238786560 | bytes 169869312 | tf_op jit(solution)/shard_map/wgrad_qkv/pallas_call | solution.py:297
  (120 shorter events, 27.9 us)
Async XLA Ops:
  3.5 4.6 %copy-start.14 = (bf16[4,1536]{1,0:T(4,128)(2,1)S(1)}, bf16[4,1536]{1,0:T(4,128)(2,1)}, u32[]{:S(2)}) copy-start(bf16[4,1536]{1,0:T(4,128)(2,1)} %param.14) | copy-start | bytes 36868
  3.5 34.8 %all-to-all-start = ((bf16[4,2,1,64,1536]{4,3,1,2,0:T(8,128)(2,1)}), bf16[4,2,1,64,1536]{4,3,1,2,0:T(8,128)(2,1)}, u32[]{:S(2)}, u32[]{:S(2)}) async-start(bf16[4,2,1,64,1536]{4,3,1,2,0:T(8,128)(2,1)} %maximum_bitcast_fusion), calls=%async_computation | async-start | bytes 3145728 | tf_op jit(solution)/shard_map/all_to_all | solution.py:350
  20.8 11.3 %copy-start.15 = (f32[2,2,64]{2,1,0:T(2,128)S(1)}, f32[2,2,64]{2,1,0:T(2,128)}, u32[]{:S(2)}) copy-start(f32[2,2,64]{2,1,0:T(2,128)} %param.19) | copy-start | bytes 3076
  38.3 85.9 %all-to-all-start.1 = ((bf16[4,2,1,64,1536]{4,3,2,1,0:T(8,128)(2,1)}), bf16[4,2,1,64,1536]{4,3,2,1,0:T(8,128)(2,1)}, u32[]{:S(2)}, u32[]{:S(2)}) async-start(bf16[4,2,1,64,1536]{4,3,2,1,0:T(8,128)(2,1)} %pad_maximum_fusion.2), calls=%async_computation.1 | async-start | bytes 3145728 | tf_op jit(solution)/shard_map/all_to_all | solution.py:350
  205.8 4.8 %copy-start.11 = (bf16[1,256,1536]{2,1,0:T(8,128)(2,1)S(1)}, bf16[1,256,1536]{2,1,0:T(8,128)(2,1)}, u32[]{:S(2)}) copy-start(bf16[1,256,1536]{2,1,0:T(8,128)(2,1)} %get-tuple-element.37) | copy-start | bytes 2359300
  208.3 3.7 copy-start.10
  208.3 3.7 copy-start.12
  209.5 4.1 %collective-permute-start.7 = (f32[30976]{0:T(1024)S(1)}, f32[30976]{0:T(1024)S(1)}, u32[]{:S(2)}, u32[]{:S(2)}) collective-permute-start(f32[30976]{0:T(1024)S(1)} %pad_maximum_fusion.7), channel_id=1, source_target_pairs={{0,1},{1,0},{2,3},{3,2},{4,5},{5,4},{6,7},{7,6},{8,9},{9,8},{10,11... | collective-permute-start | bytes 371720 | tf_op jit(solution)/shard_map/ppermute | solution.py:334
  210.2 17.3 %collective-permute-start.8 = (bf16[1,1536,640]{2,1,0:T(8,128)(2,1)}, bf16[1,1536,640]{2,1,0:T(8,128)(2,1)}, u32[]{:S(2)}, u32[]{:S(2)}) collective-permute-start(bf16[1,1536,640]{2,1,0:T(8,128)(2,1)} %get-tuple-element.58.refs_0_), channel_id=1, source_target_pairs={{0,1},{1,0},{2,3},{3,2},{4,5},{5,4},{6,7},{7,6},{8,9},{9,8},{10,11... | collective-permute-start | bytes 5898248 | tf_op jit(solution)/shard_map/ppermute | solution.py:334
  210.2 17.7 %collective-permute-start.9 = (bf16[1,1536,640]{2,1,0:T(8,128)(2,1)}, bf16[1,1536,640]{2,1,0:T(8,128)(2,1)}, u32[]{:S(2)}, u32[]{:S(2)}) collective-permute-start(bf16[1,1536,640]{2,1,0:T(8,128)(2,1)} %get-tuple-element.59.refs_1_), channel_id=1, source_target_pairs={{0,1},{1,0},{2,3},{3,2},{4,5},{5,4},{6,7},{7,6},{8,9},{9,8},{10,11... | collective-permute-start | bytes 5898248 | tf_op jit(solution)/shard_map/ppermute | solution.py:334
  213.2 8.2 %collective-permute-start = (bf16[2,2,64,1536]{3,2,0,1:T(8,128)(2,1)}, bf16[2,2,64,1536]{3,2,0,1:T(8,128)(2,1)}, u32[]{:S(2)}, u32[]{:S(2)}) collective-permute-start(bf16[2,2,64,1536]{3,2,0,1:T(8,128)(2,1)} %get-tuple-element.137), channel_id=1, source_target_pairs={{0,1},{1,0},{2,3},{3,2},{4,5},{5,4},{6,7},{7,6},{8,9},{9,8},{10,11... | collective-permute-start | bytes 2359304 | tf_op jit(solution)/shard_map/ppermute | solution.py:334
  213.2 76.2 %collective-permute-start.5 = (bf16[1,3,640,1536]{3,2,1,0:T(8,128)(2,1)}, bf16[1,3,640,1536]{3,2,1,0:T(8,128)(2,1)}, u32[]{:S(2)}, u32[]{:S(2)}) collective-permute-start(bf16[1,3,640,1536]{3,2,1,0:T(8,128)(2,1)} %get-tuple-element.47.refs_4_), channel_id=1, source_target_pairs={{0,1},{1,0},{2,3},{3,2},{4,5},{5,4},{6,7},{7,6},{8,9},{9,8},{10,11... | collective-permute-start | bytes 17694728 | tf_op jit(solution)/shard_map/ppermute | solution.py:334
  213.7 75.7 %collective-permute-start.6 = (bf16[1,3,640,1536]{3,2,1,0:T(8,128)(2,1)}, bf16[1,3,640,1536]{3,2,1,0:T(8,128)(2,1)}, u32[]{:S(2)}, u32[]{:S(2)}) collective-permute-start(bf16[1,3,640,1536]{3,2,1,0:T(8,128)(2,1)} %get-tuple-element.48.refs_5_), channel_id=1, source_target_pairs={{0,1},{1,0},{2,3},{3,2},{4,5},{5,4},{6,7},{7,6},{8,9},{9,8},{10,11... | collective-permute-start | bytes 17694728 | tf_op jit(solution)/shard_map/ppermute | solution.py:334
  214.2 3.5 copy-start.1
  221.4 25.2 %collective-permute-start.10 = (bf16[1,1,640,1536]{3,2,1,0:T(8,128)(2,1)}, bf16[1,1,640,1536]{3,2,1,0:T(8,128)(2,1)}, u32[]{:S(2)}, u32[]{:S(2)}) collective-permute-start(bf16[1,1,640,1536]{3,2,1,0:T(8,128)(2,1)} %bitcast.46), channel_id=1, source_target_pairs={{0,1},{1,0},{2,3},{3,2},{4,5},{5,4},{6,7},{7,6},{8,9},{9,8},{10,11... | collective-permute-start | bytes 5898248 | tf_op jit(solution)/shard_map/ppermute | solution.py:334
  227.5 20.9 %collective-permute-start.1 = (bf16[2,333,1536]{2,0,1:T(2,128)(2,1)}, bf16[2,333,1536]{2,0,1:T(2,128)(2,1)}, u32[]{:S(2)}, u32[]{:S(2)}) collective-permute-start(bf16[2,333,1536]{2,0,1:T(2,128)(2,1)} %copy.145), channel_id=1, source_target_pairs={{0,1},{1,0},{2,3},{3,2},{4,5},{5,4},{6,7},{7,6},{8,9},{9,8},{10,11... | collective-permute-start | bytes 6137864 | tf_op jit(solution)/shard_map/ppermute | solution.py:334
  227.9 20.4 %collective-permute-start.11 = (bf16[1,1,640,1536]{3,2,1,0:T(8,128)(2,1)}, bf16[1,1,640,1536]{3,2,1,0:T(8,128)(2,1)}, u32[]{:S(2)}, u32[]{:S(2)}) collective-permute-start(bf16[1,1,640,1536]{3,2,1,0:T(8,128)(2,1)} %bitcast.48), channel_id=1, source_target_pairs={{0,1},{1,0},{2,3},{3,2},{4,5},{5,4},{6,7},{7,6},{8,9},{9,8},{10,11... | collective-permute-start | bytes 5898248 | tf_op jit(solution)/shard_map/ppermute | solution.py:334
  234.3 4.0 %slice-start = ((f32[12544]{0:T(1024)}), f32[9216]{0:T(1024)S(1)}, s32[]{:S(2)}) async-start(f32[12544]{0:T(1024)} %copy-done.13), calls=%async_computation.2 | async-start | bytes 73728 | tf_op jit(solution)/shard_map/slice | solution.py:383
  234.3 4.6 %slice-start.1 = ((f32[12544]{0:T(1024)}), f32[256]{0:T(256)S(1)}, s32[]{:S(2)}) async-start(f32[12544]{0:T(1024)} %copy-done.13), calls=%async_computation.3 | async-start | bytes 2048 | tf_op jit(solution)/shard_map/slice | solution.py:383
  234.3 5.3 %slice-start.2 = ((f32[12544]{0:T(1024)}), f32[3072]{0:T(1024)S(1)}, s32[]{:S(2)}) async-start(f32[12544]{0:T(1024)} %copy-done.13), calls=%async_computation.4 | async-start | bytes 24576 | tf_op jit(solution)/shard_map/slice | solution.py:383
  246.6 34.0 %collective-permute-start.2 = (bf16[2,333,1536]{2,0,1:T(2,128)(2,1)}, bf16[2,333,1536]{2,0,1:T(2,128)(2,1)}, u32[]{:S(2)}, u32[]{:S(2)}) collective-permute-start(bf16[2,333,1536]{2,0,1:T(2,128)(2,1)} %copy.148), channel_id=1, source_target_pairs={{0,1},{1,0},{2,3},{3,2},{4,5},{5,4},{6,7},{7,6},{8,9},{9,8},{10,11... | collective-permute-start | bytes 6137864 | tf_op jit(solution)/shard_map/ppermute | solution.py:334
  248.2 41.1 %collective-permute-start.3 = (bf16[1,1536,640]{2,1,0:T(8,128)(2,1)}, bf16[1,1536,640]{2,1,0:T(8,128)(2,1)}, u32[]{:S(2)}, u32[]{:S(2)}) collective-permute-start(bf16[1,1536,640]{2,1,0:T(8,128)(2,1)} %get-tuple-element.45.refs_0_), channel_id=1, source_target_pairs={{0,1},{1,0},{2,3},{3,2},{4,5},{5,4},{6,7},{7,6},{8,9},{9,8},{10,11... | collective-permute-start | bytes 5898248 | tf_op jit(solution)/shard_map/ppermute | solution.py:334
  248.4 41.0 %collective-permute-start.4 = (bf16[1,1536,640]{2,1,0:T(8,128)(2,1)}, bf16[1,1536,640]{2,1,0:T(8,128)(2,1)}, u32[]{:S(2)}, u32[]{:S(2)}) collective-permute-start(bf16[1,1536,640]{2,1,0:T(8,128)(2,1)} %get-tuple-element.46.refs_1_), channel_id=1, source_target_pairs={{0,1},{1,0},{2,3},{3,2},{4,5},{5,4},{6,7},{7,6},{8,9},{9,8},{10,11... | collective-permute-start | bytes 5898248 | tf_op jit(solution)/shard_map/ppermute | solution.py:334
  289.4 78.7 %copy-start.5 = (f32[4,1536]{0,1:T(8,128)S(1)}, f32[4,1536]{0,1:T(8,128)}, u32[]{:S(2)}) copy-start(f32[4,1536]{0,1:T(8,128)} %copy-done.4) | copy-start | bytes 73732
  (9 other events, 21.3 us)

commit v3 on v2

--- a/solution.py
+++ b/solution.py
@@ -12,7 +12,6 @@
 BF16 = jnp.bfloat16
 NN = (((1,), (0,)), ((), ()))
 NT = (((1,), (1,)), ((), ()))
-TN = (((0,), (0,)), ((), ()))
 
 
 def dot(lhs, rhs, dims=NN):
@@ -70,7 +69,7 @@
 
 
 def block_kernel(n_keys, heads, tok_i_ref, cot_i_ref, tok_t_ref, cot_t_ref, mod_ref, bo_ref, wq_ref, wk_ref, wv_ref, bq_ref, bk_ref, bv_ref, gain_ref, wo_ref,
-                 hid_trn_ref, dy_ref, o_trn_ref, dp_ref, new_i_ref, new_t_ref, grad_i_ref, grad_t_ref, sums_ref, dg_ref, db_ref,
+                 hid_trn_ref, dy_ref, o_trn_ref, dp_ref, img_ref, txt_ref, sums_ref, dg_ref, db_ref,
                  hid_ref, tok_ref, cot_ref, y_i_ref, y_t_ref, acc_i_ref, acc_t_ref, hat_ref, inv_ref, nat_ref, trn_ref, v_ref, do_nat_ref, do_trn_ref, dq_ref, dk_ref, dv_ref):
     step_b, step_g = pl.program_id(0), pl.program_id(1)
     n_grp = pl.num_programs(1)
@@ -118,27 +117,34 @@
     dv_ref[k_rows:] = jnp.zeros((n_tok - k_rows, width), F32)
 
     exp_scale = att_scale * math.log2(math.e)
+
+    def scores_of(head):
+        rows = slice(head * head_dim, (head + 1) * head_dim)
+        return dot(nat_ref[1, :k_rows, rows], trn_ref[0, rows, :])
+
+    scores = scores_of(0)
     for head in range(heads):
         rows = slice(head * head_dim, (head + 1) * head_dim)
-        q_trn, k_trn, v_trn = trn_ref[0, rows, :], trn_ref[1, rows, :k_rows], trn_ref[2, rows, :k_rows]
-        q_nat, k_nat, v_nat = nat_ref[0, :, rows], nat_ref[1, :k_rows, rows], v_ref[:k_rows, rows]
-        scores = dot(k_nat, q_trn)
+        k_trn, v_trn = trn_ref[1, rows, :k_rows], trn_ref[2, rows, :k_rows]
+        q_nat, v_nat = nat_ref[0, :, rows], v_ref[:k_rows, rows]
+        do_trn = do_trn_ref[rows]
+        ahead = scores_of(head + 1) if head + 1 < heads else None
+        d_prob = dot(v_nat, do_trn)
         tail_row = k_main + lax.broadcasted_iota(jnp.int32, (16, n_tok), 0)
         tail = jnp.where(tail_row < n_keys, scores[k_main:], -jnp.inf)
         scores = jnp.concatenate([scores[:k_main], tail], axis=0)
         peak = jnp.max(scores, axis=0, keepdims=True)
         exps = jnp.exp2((scores - peak) * exp_scale)
-        prob = exps * (1.0 / jnp.sum(exps, axis=0, keepdims=True))
-        prob_lo = prob.astype(BF16)
+        inv_sum = 1.0 / jnp.sum(exps, axis=0, keepdims=True)
+        prob_lo = (exps * inv_sum).astype(BF16)
         out_trn = dot(v_trn, prob_lo).astype(BF16)
         o_trn_ref[0, rows] = out_trn
-        do_trn = do_trn_ref[rows]
         delta = jnp.sum(out_trn.astype(F32) * do_trn.astype(F32), axis=0, keepdims=True)
-        d_prob = dot(v_nat, do_trn)
-        d_score = (prob * (d_prob - delta)).astype(BF16)
+        d_score = (exps * inv_sum * (d_prob - delta)).astype(BF16)
         dv_ref[:k_rows, rows] = dot(prob_lo, do_nat_ref[:, rows])
         dk_ref[:k_rows, rows] = dot(d_score, q_nat) * att_scale
         dq_ref[rows] = dot(k_trn, d_score) * att_scale
+        scores = ahead
 
     o_nat = o_trn_ref[0].T
 
@@ -169,7 +175,6 @@
         mean_dh = jnp.mean(d_hat * hat, axis=1, keepdims=True)
         d_raw.append((inv_ref[idx] * (d_hat - hat * mean_dh)).reshape(width, n_tok).T)
     d_raw.append(dv_ref[...].astype(BF16).astype(F32))
-    sums = []
     d_lo = []
     for idx in range(3):
         lo = d_raw[idx].astype(BF16)
@@ -184,8 +189,8 @@
 
     @pl.when(step_g == n_grp - 1)
     def _():
-        epilogue(tok_ref, cot_ref, mod_ref.at[0, 0], bo_ref[0:1], y_i_ref, acc_i_ref, new_i_ref.at[0], grad_i_ref.at[0], sums_ref.at[0], 0, 64)
-        epilogue(tok_t_ref.at[0], cot_t_ref.at[0], mod_ref.at[0, 1], bo_ref[1:2], y_t_ref, acc_t_ref, new_t_ref.at[0], grad_t_ref.at[0], sums_ref.at[0], 4, 64)
+        epilogue(tok_ref, cot_ref, mod_ref.at[0, 0], bo_ref[0:1], y_i_ref, acc_i_ref, img_ref.at[0, 0], img_ref.at[0, 1], sums_ref.at[0], 0, 64)
+        epilogue(tok_t_ref.at[0], cot_t_ref.at[0], mod_ref.at[0, 1], bo_ref[1:2], y_t_ref, acc_t_ref, txt_ref.at[0, 0], txt_ref.at[0, 1], sums_ref.at[0], 4, 64)
 
 
 def fused_block(tokens, text, cot_t, mod, b_out, w_qkv, b_qkv, qk_gain, w_out, n_keys, heads):
@@ -214,12 +219,11 @@
     in_specs = [img_spec(0), img_spec(1), rows_spec(n_txt, pipeline_mode=once), rows_spec(n_txt, pipeline_mode=once), pl.BlockSpec((1, 2, 3, d_model), lambda b, g: (b, 0, 0, 0)), pl.BlockSpec((2, d_model), lambda b, g: (0, 0)), w_spec(0), w_spec(1), w_spec(2), b_spec(0), b_spec(1), b_spec(2),
                 pl.BlockSpec((2, width, n_tok), lambda b, g: (0, 0, 0)), pl.BlockSpec((2, width, d_model), lambda b, g: (0, g, 0))]
     out_specs = [pl.BlockSpec((1, d_model, n_tok), lambda b, g: (b, 0, 0)), rows_spec(n_tok), pl.BlockSpec((1, width, n_tok), lambda b, g: (b, g, 0)), pl.BlockSpec((1, 3, n_tok, width), lambda b, g: (b, 0, 0, g)),
-                 rows_spec(n_img), rows_spec(n_txt), rows_spec(n_img), rows_spec(n_txt), pl.BlockSpec((1, 8, d_model), lambda b, g: (b, 0, 0)),
+                 pl.BlockSpec((1, 2, n_img, d_model), lambda b, g: (b, 0, 0, 0)), pl.BlockSpec((1, 2, n_txt, d_model), lambda b, g: (b, 0, 0, 0)), pl.BlockSpec((1, 8, d_model), lambda b, g: (b, 0, 0)),
                  pl.BlockSpec((4, width, 128), lambda b, g: (0, 0, 0)), pl.BlockSpec((1, 8, width), lambda b, g: (b, 0, g))]
     shape = jax.ShapeDtypeStruct
-    rows_shape = [shape((n_b, n_img, d_model), BF16), shape((n_b, n_txt, d_model), BF16)]
     out_shape = [shape((n_b, d_model, n_tok), BF16), shape((n_b, n_tok, d_model), BF16), shape((n_b, d_model, n_tok), BF16), shape((n_b, 3, n_tok, d_model), BF16),
-                 *(rows_shape * 2), shape((n_b, 8, d_model), F32), shape((4, width, 128), F32), shape((n_b, 8, d_model), F32)]
+                 shape((n_b, 2, n_img, d_model), BF16), shape((n_b, 2, n_txt, d_model), BF16), shape((n_b, 8, d_model), F32), shape((4, width, 128), F32), shape((n_b, 8, d_model), F32)]
     scratch = [pltpu.VMEM((n_tok, d_model), BF16), pltpu.VMEM((n_img, d_model), BF16), pltpu.VMEM((n_img, d_model), BF16),
                pltpu.VMEM((n_img, d_model), F32), pltpu.VMEM((n_txt, d_model), F32), pltpu.VMEM((n_img, d_model), F32), pltpu.VMEM((n_txt, d_model), F32),
                pltpu.VMEM((2, width, n_tok), F32), pltpu.VMEM((2, heads, 1, n_tok), F32),
@@ -239,7 +243,7 @@
 def wgrad_kernel(n_img, n_b, with_ada, core_ref, *refs):
     lefts, rights, refs = refs[:2 * n_b], refs[2 * n_b:4 * n_b], refs[4 * n_b:]
     if with_ada:
-        act_ref, dmod_ref, dmod_trn_ref, w_ref, out_ref, dw_ref, dact_ref, trn_i_ref, trn_t_ref, rhs_i_ref, rhs_t_ref = refs
+        act_ref, dmod_ref, w_ref, out_ref, dw_ref, dact_ref, trn_i_ref, trn_t_ref, rhs_i_ref, rhs_t_ref = refs
     else:
         out_ref, trn_i_ref, trn_t_ref, rhs_i_ref, rhs_t_ref = refs
     d_model, n_tok = lefts[0].shape[1:]
@@ -263,6 +267,9 @@
         rhs_t_ref[place(idx, n_txt)] = rights[idx][0, 0, n_img:]
 
     chunk = 512
+    if with_ada:
+        dmods = [dmod_ref[branch, 0].astype(BF16) for branch in range(2)]
+        dmods_trn = [dmod_ref[branch, 0].T.astype(BF16) for branch in range(2)]
 
     @pl.loop(0, d_model // chunk)
     def _(step):
@@ -271,11 +278,11 @@
         out_ref[1, rows] = dot(trn_t_ref[rows], rhs_t_ref[...])
         if with_ada:
             for branch in range(2):
-                dw_ref[branch, rows] = dot(act_ref[rows], dmod_ref[branch].astype(BF16))
-                dact_ref[rows] += dot(w_ref[branch, rows], dmod_trn_ref[branch].astype(BF16))
-
-
-def wgrad(core, lefts, rights, n_img, block, name, ada=None):
+                dw_ref[branch, rows] = dot(act_ref[rows], dmods[branch])
+                dact_ref[rows] += dot(w_ref[branch, rows], dmods_trn[branch])
+
+
+def wgrad(core, lefts, rights, n_img, block, ada=None):
     n_b = len(lefts) // 2
     _, d_model, n_tok = lefts[0].shape
     n_c, wide = rights[0].shape[1], rights[0].shape[3]
@@ -289,9 +296,8 @@
     if ada is not None:
         cond_act, d_mod, w_ada = ada
         n_batch = cond_act.shape[0]
-        d_mod = jnp.pad(d_mod, ((0, 0), (0, 16 - n_batch), (0, 0)))
-        extra = [jnp.pad(cond_act, ((0, 16 - n_batch), (0, 0))).T, d_mod, d_mod.swapaxes(1, 2), w_ada]
-        in_specs += [pl.BlockSpec((d_model, 16), lambda j: (0, 0)), pl.BlockSpec((2, 16, block), lambda j: (0, 0, j)), pl.BlockSpec((2, block, 16), lambda j: (0, j, 0)), mat_spec]
+        extra = [jnp.pad(cond_act, ((0, 16 - n_batch), (0, 0))).T, jnp.pad(d_mod, ((0, 0), (0, 0), (0, 16 - n_batch), (0, 0))), w_ada]
+        in_specs += [pl.BlockSpec((d_model, 16), lambda j: (0, 0)), pl.BlockSpec((2, 1, 16, block), lambda j: (0, j // per, 0, j % per)), mat_spec]
         out_shape += [jax.ShapeDtypeStruct((2, d_model, cols), F32), jax.ShapeDtypeStruct((d_model, 16), F32)]
         out_specs += [mat_spec, pl.BlockSpec((d_model, 16), lambda j: (0, 0))]
     return pl.pallas_call(
@@ -299,9 +305,8 @@
         out_shape=out_shape, grid=(n_c * per,), in_specs=in_specs, out_specs=out_specs,
         scratch_shapes=[pltpu.VMEM((d_model, 2 * n_b * n_img), BF16), pltpu.VMEM((d_model, 2 * n_b * (n_tok - n_img)), BF16),
                         pltpu.VMEM((2 * n_b * n_img, block), BF16), pltpu.VMEM((2 * n_b * (n_tok - n_img), block), BF16)],
-        compiler_params=pltpu.CompilerParams(dimension_semantics=("arbitrary",), vmem_limit_bytes=60 * 1024 * 1024),
+        compiler_params=pltpu.CompilerParams(dimension_semantics=("arbitrary",), vmem_limit_bytes=67043328),
         cost_estimate=pl.CostEstimate(flops=4 * n_b * n_tok * d_model * cols, bytes_accessed=(8 if ada is None else 24) * d_model * cols, transcendentals=0),
-        name=name,
     )(core[None], *lefts, *rights, *extra)
 
 
@@ -333,9 +338,6 @@
     def swap(arr):
         return lax.ppermute(arr, 'sp', pairs)
 
-    def both(arr):
-        return arr, swap(arr)
-
     def device_fn(image_in, text_in, cond_vec, w_ada, b_ada, w_qkv, b_qkv, qk_gain, w_out, b_out, image_cot, text_cot):
         n_batch, tok_dev, d_model = image_in.shape
         ctx_len = text_in.shape[1]
@@ -361,40 +363,42 @@
         pad_rows = ((0, 0), (0, n_txt - ctx_len), (0, 0))
         text_own, cot_own = jnp.pad(own(text_in), pad_rows), jnp.pad(own(text_cot), pad_rows)
 
-        outs = []
+        outs, others = [], []
         for idx in range(n_own):
             one = slice(idx, idx + 1)
-            outs.append(fused_block(tokens[idx], text_own[one], cot_own[one], own_mod[one], b_out, w_qkv, b_qkv, qk_gain, w_out, n_img + ctx_len, 4))
-        sums, db = (jnp.concatenate([out[pos] for out in outs]) for pos in (8, 10))
-        new_i, new_t, grad_i, grad_t = (jnp.concatenate([out[pos] for out in outs]) for pos in (4, 5, 6, 7))
-        dg = sum(out[9] for out in outs)
-        factors = [[out[pos] for out in outs] for pos in range(4)]
-        factors[1] = [arr[:, None] for arr in factors[1]]
-        hid_trn, dy, o_trn, dp = [arrs + [swap(arr) for arr in arrs] for arrs in factors]
-
-        sums = sums.reshape(n_own, 2, 4, d_model)
-        d_mod = sums[:, :, :3].swapaxes(0, 1).reshape(2, n_own, 3 * d_model)
-        rest = jnp.concatenate([jnp.sum(sums[:, :, 3], 0).reshape(-1), jnp.sum(db, 0)[:6].reshape(-1), jnp.sum(jnp.sum(dg, -1).reshape(2, 2, -1, qk_gain.shape[-1]), 2).reshape(-1)])
-        small = jnp.concatenate([d_mod.reshape(-1), rest])
-        small_other = swap(small)
-        d_mod_all = ordered(d_mod, small_other[:d_mod.size].reshape(d_mod.shape), 1)
-        rest = rest + small_other[d_mod.size:]
-        cut = (2 * d_model, 8 * d_model)
-        db_out, db_qkv, d_gain = rest[:cut[0]].reshape(2, d_model), rest[cut[0]:cut[1]].reshape(2, 3 * d_model), rest[cut[1]:].reshape(qk_gain.shape)
-
-        dw_out, = wgrad(core, o_trn, dy, n_img, 256, "wgrad_out")
-        dw_qkv, dw_ada, d_act = wgrad(core, hid_trn, dp, n_img, 256, "wgrad_qkv", (cond_act, d_mod_all, w_ada))
+            out = list(fused_block(tokens[idx], text_own[one], cot_own[one], own_mod[one], b_out, w_qkv, b_qkv, qk_gain, w_out, n_img + ctx_len, 4))
+            out[1] = out[1][:, None]
+            other = {}
+            for pos_set in ((2, 1), (0, 3), (5,)):
+                other.update({pos: swap(out[pos]) for pos in pos_set})
+            others.append(other)
+            outs.append(out)
+        hid_trn, dy, o_trn, dp, txt = [[out[pos] for out in outs] + [other[pos] for other in others] for pos in (0, 1, 2, 3, 5)]
+
+        sums = jnp.concatenate([out[6] for out in outs])
+        db = sum(out[8] for out in outs)
+        dg = jnp.sum(sum(out[7] for out in outs), -1)
+        sums_other = swap(sums)
+        sums = ordered(sums, sums_other).swapaxes(0, 1).reshape(2, 4, n_batch, d_model)
+        rest = jnp.concatenate([db[0, :6], jnp.pad(dg, ((0, 0), (0, d_model - dg.shape[1])))])
+        rest_other = swap(rest)
+        rest = rest + rest_other
+        d_mod, db_out, db_qkv = sums[:, :3], jnp.sum(sums[:, 3], 1), rest[:6].reshape(2, 3 * d_model)
+        d_gain = jnp.sum(rest[6:, :dg.shape[1]].reshape(2, 2, -1, qk_gain.shape[-1]), 2)
+
+        dw_out, = wgrad(core, o_trn, dy, n_img, 256)
+        dw_qkv, dw_ada, d_act = wgrad(core, hid_trn, dp, n_img, 512, (cond_act, d_mod, w_ada))
         d_act = d_act.T[:n_batch]
-        db_ada = jnp.sum(d_mod_all, axis=1)
+        db_ada = jnp.sum(d_mod, axis=2).reshape(2, 3 * d_model)
         _, pull_act = jax.vjp(jax.nn.silu, cond_vec.astype(F32))
         grad_cond = pull_act(d_act.astype(BF16).astype(F32))[0]
 
-        img_pair = jnp.stack([new_i, grad_i], axis=1)
+        img_pair = jnp.concatenate([out[4] for out in outs])
         chip_lo = chip * pair * tok_dev
         img_mine = lax.dynamic_slice_in_dim(img_pair, chip_lo + core * tok_dev, tok_dev, 2)
         img_send = lax.dynamic_slice_in_dim(img_pair, chip_lo + (1 - core) * tok_dev, tok_dev, 2)
         img_pair = ordered(img_mine, swap(img_send))
-        text_new, grad_text = ordered(*both(new_t[:, :ctx_len])), ordered(*both(grad_t[:, :ctx_len]))
+        text_new, grad_text = (ordered(jnp.concatenate([arr[:, pos, :ctx_len] for arr in txt[:n_own]]), jnp.concatenate([arr[:, pos, :ctx_len] for arr in txt[n_own:]])) for pos in range(2))
         return (img_pair[:, 0], text_new, img_pair[:, 1], grad_text, grad_cond, dw_ada, db_ada, dw_qkv, db_qkv, d_gain, dw_out, db_out)
 
     data_spec = P('dp', 'sp', None)
@@ -402,4 +406,5 @@
     rep_spec = P()
     in_specs = (data_spec, batch_spec, batch_spec, rep_spec, rep_spec, rep_spec, rep_spec, rep_spec, rep_spec, rep_spec, data_spec, batch_spec)
     out_specs = (data_spec, batch_spec, data_spec, batch_spec, batch_spec, batch_spec, batch_spec, batch_spec, batch_spec, batch_spec, batch_spec, batch_spec)
+
     return jax.shard_map(device_fn, mesh=mesh, in_specs=in_specs, out_specs=out_specs, check_vma=False)

time: 377 us -> 353 us (0.936)
  other arithmetic: 24.8 us -> 13.6 us
  Pallas kernels: 274 us -> 263 us
  local copies, waits for them, and re-layouts: 56.7 us -> 48.9 us
  waiting for transfers between devices: 0.04 us -> 6.32 us
    squeeze x0 -> x4, local copies, waits for them, and re-layouts: none -> 9.43 us  [device_fn(): arr[:, pos, :ctx_len]]
    slice x10 -> x2, local copies, waits for them, and re-layouts: 7.48 us -> 0.01 us  [the longest x1 0.01 us: device_fn(): rest[6:, :dg.shape[1]].reshape(2, 2, -1, qk_gain.shape[-1])]
    reduce_sum x5 -> x4, other arithmetic: 8.74 us -> 1.57 us  [the longest x1 0.64 us: device_fn(): jnp.sum(sums[:, 3], 1)]
    ppermute x12 -> x13, waiting for transfers between devices: 0.03 us -> 6.32 us  [swap(): return lax.ppermute(arr, 'sp', pairs)]
    pallas_call x2, Pallas kernels: 99.9 us -> 93.9 us  [wgrad(): pl.pallas_call(functools.partial(wgrad_kernel, n_img, n_b, ada is not Non...]
    pallas_call x2, Pallas kernels: 163 us -> 158 us  [fused_block(): pl.pallas_call(functools.partial(block_kernel, n_keys, heads), out_shape=...]
    transpose x2 -> x1, local copies, waits for them, and re-layouts: 4.75 us -> 0.13 us  [device_fn(): ordered(sums, sums_other).swapaxes(0, 1).reshape(2, 4, n_batch, d_model)]
    unnamed x41 -> x44, local copies, waits for them, and re-layouts: 18.1 us -> 19.1 us
  transfers between devices with their start and end apart: 14 -> 15, of which waited for: 0 -> 1; matrix products, arithmetic and copies ran while one was open for 19% -> 14% of each run, Pallas kernels for 31% -> 33%
where the time goes in v3:
time: 353 us; the launch traced here: 346 us
  Pallas kernels  263 us (75%)
  local copies, waits for them, and re-layouts  48.9 us (14%)
  other arithmetic  13.6 us (4%)
  starting transfers between devices  12.7 us (4%)
  waiting for transfers between devices  6.32 us (2%)
    pallas_call x2, Pallas kernels, fused_block(): pl.pallas_call(functools.partial(block_kernel, n_keys, heads), out_shape=...  158 us
    pallas_call x2, Pallas kernels, wgrad(): pl.pallas_call(functools.partial(wgrad_kernel, n_img, n_b, ada is not Non...  93.9 us
    unnamed x44, local copies, waits for them, and re-layouts  19.1 us
    pallas_call x1, Pallas kernels, ada_fwd(): pl.pallas_call(ada_fwd_kernel, out_shape=jax.ShapeDtypeStruct((2, 16, wid...  11.1 us
    squeeze x4, local copies, waits for them, and re-layouts, device_fn(): arr[:, pos, :ctx_len]  9.43 us
    all_to_all x2, starting transfers between devices, device_fn(): lax.all_to_all(jnp.concatenate([img_pair[:, :, idx].swapaxes(0, 1)] * n_c...  8.84 us
    dynamic_slice x2, local copies, waits for them, and re-layouts, own(): return lax.dynamic_slice_in_dim(arr, own_lo, n_own, axis)  7.65 us
  transfers between devices with their start and end apart: 15, of which 1 were waited for; matrix products, arithmetic and copies ran while one was open for 14% of the time, Pallas kernels for 33%

profile of v3, /device:TPU:0, one launch (start us, length us, event | category | flops | bytes accessed | tf_op | source)
XLA Modules:
  0.0 346.0 jit_solution(482985059623015261)
XLA Ops:
  0.6 1.5 pad_maximum_fusion.2
  3.5 4.5 %all-to-all-start = ((bf16[4,2,1,64,1536]{4,3,1,2,0:T(8,128)(2,1)}), bf16[4,2,1,64,1536]{4,3,1,2,0:T(8,128)(2,1)}, u32[]{:S(2)}, u32[]{:S(2)}) async-start(bf16[4,2,1,64,1536]{4,3,1,2,0:T(8,128)(2,1)} %maximum_bitcast_fusion), calls=%async_computation | async-start | bytes 3145728 | tf_op jit(solution)/shard_map/all_to_all | solution.py:352
  9.4 7.6 %constant_dynamic-slice_fusion.3 = (bf16[2,333,1536]{2,0,1:T(2,128)(2,1)S(1)}, bf16[2,333,1536]{2,0,1:T(2,128)(2,1)S(1)}) fusion(bf16[4,333,1536]{2,0,1:T(4,128)(2,1)} %param.23, s32[]{:T(128)S(6)} %select_n.40, bf16[4,333,1536]{2,0,1:T(4,128)(2,1)} %param.13), kind=kLoop, calls=%fused_computation.49 | loop fusion | bytes 8183812 | tf_op jit(solution)/shard_map/dynamic_slice | solution.py:355
  17.1 1.5 copy.89
  19.3 11.1 %ada_fwd.1 = f32[2,16,4608]{2,1,0:T(8,128)S(1)} custom-call(bf16[16,1536]{1,0:T(8,128)(2,1)S(1)} %pad.22.clone.act_ref, bf16[2,1536,4608]{2,1,0:T(8,128)(2,1)} %refs_10_.1, f32[2,4608]{1,0:T(2,128)S(1)} %copy-done), custom_call_target="tpu_custom_call" | custom-call | flops 452984832 | bytes 28311552 | tf_op jit(solution)/shard_map/ada_fwd/pallas_call | solution.py:321
  34.3 1.6 pad_slice_fusion.2
  35.8 1.6 pad_slice_fusion
  38.1 4.4 %all-to-all-start.1 = ((bf16[4,2,1,64,1536]{4,3,2,1,0:T(8,128)(2,1)}), bf16[4,2,1,64,1536]{4,3,2,1,0:T(8,128)(2,1)}, u32[]{:S(2)}, u32[]{:S(2)}) async-start(bf16[4,2,1,64,1536]{4,3,2,1,0:T(8,128)(2,1)} %pad_maximum_fusion), calls=%async_computation.1 | async-start | bytes 3145728 | tf_op jit(solution)/shard_map/all_to_all | solution.py:352
  42.5 79.1 %fused_block.2 = (bf16[1,1536,640]{2,1,0:T(8,128)(2,1)}, bf16[1,640,1536]{2,1,0:T(8,128)(2,1)}, bf16[1,1536,640]{2,1,0:T(8,128)(2,1)}, bf16[1,3,640,1536]{3,2,1,...) custom-call(bf16[4,2,1,64,1536]{4,3,2,1,0:T(8,128)(2,1)} %bitcast.5., ...), custom_call_target="tpu_custom_call" | custom-call | flops 31708938240 | bytes 104857600 | tf_op jit(solution)/shard_map/fused_block/pallas_call | solution.py:234
  121.6 2.7 constant_dynamic-update-slice_fusion.1
  124.3 79.0 %fused_block.3 = (bf16[1,1536,640]{2,1,0:T(8,128)(2,1)}, bf16[1,640,1536]{2,1,0:T(8,128)(2,1)}, bf16[1,1536,640]{2,1,0:T(8,128)(2,1)}, bf16[1,3,640,1536]{3,2,1,...) custom-call(bf16[4,2,1,64,1536]{4,3,2,1,0:T(8,128)(2,1)} %all-to-all, ...), custom_call_target="tpu_custom_call" | custom-call | flops 31708938240 | bytes 104857600 | tf_op jit(solution)/shard_map/fused_block/pallas_call | solution.py:234
  203.2 2.8 constant_dynamic-update-slice_fusion
  206.1 1.6 constant_dynamic-slice_fusion.1
  209.7 6.3 %collective-permute-done.8 = f32[10,1536]{1,0:T(8,128)S(1)} collective-permute-done((f32[10,1536]{1,0:T(8,128)S(1)}, f32[10,1536]{1,0:T(8,128)S(1)}, u32[]{:S(2)}, u32[]{:S(2)}) %collective-permute-start.8) | collective-permute-done | bytes 61472 | tf_op jit(solution)/shard_map/ppermute | solution.py:339
  216.4 3.0 slice_bitcast_fusion.4
  219.5 3.0 slice_bitcast_fusion.5
  230.1 22.5 %shard_map.212 = f32[2,1536,1536]{2,1,0:T(8,128)} custom-call(s32[1]{0:T(128)} %bitcast.21.core_ref, bf16[1,1536,640]{2,1,0:T(8,128)(2,1)} %get-tuple-element.50.refs_0_, bf16[1,1536,640]{2,1,0:T(8,128)(2,1)} %get-tuple-element.51.refs_1_, bf16[1,1536,640]{2,1,0:T(8,128)(2,1)} %copy-done.16, bf16[1,1536,640]{2,1,0:T(8,128)(2,1)} %collective-permute-done.10.refs_3_, ...), custom_call_target="tpu_custom_call" | custom-call | flops 12079595520 | bytes 18874368 | tf_op jit(solution)/shard_map/pallas_call | solution.py:303
  253.0 1.7 slice_bitcast_fusion
  254.7 1.8 slice_bitcast_fusion.1
  256.8 1.9 maximum_select_fusion
  258.7 5.1 %copy.84 = bf16[4,333,1536]{2,0,1:T(4,128)(2,1)} copy(bf16[4,333,1536]{2,1,0:T(8,128)(2,1)S(1)} %maximum_select_fusion) | data formatting | bytes 8183808
  263.8 1.9 maximum_select_fusion.1
  265.7 5.1 %copy.85 = bf16[4,333,1536]{2,0,1:T(4,128)(2,1)} copy(bf16[4,333,1536]{2,1,0:T(8,128)(2,1)S(1)} %maximum_select_fusion.1) | data formatting | bytes 8183808
  270.9 71.4 %shard_map.211 = (f32[2,1536,4608]{2,1,0:T(8,128)}, f32[2,1536,4608]{2,1,0:T(8,128)}, f32[1536,16]{1,0:T(8,128)}) custom-call(s32[1]{0:T(128)} %bitcast.21.core_ref, bf16[1,1536,640]{2,1,0:T(8,128)(2,1)} %get-tuple-element.37.refs_0_, bf16[1,1536,640]{2,1,0:T(8,128)(2,1)} %get-tuple-element.38.refs_1_, bf16[1,1536,640]{2,1,0:T(8,128)(2,1)} %collective-permute-done.3.refs_2_, ...), custom_call_target="tpu_custom_call" | custom-call | flops 36238786560 | bytes 169869312 | tf_op jit(solution)/shard_map/pallas_call | solution.py:303
  (105 shorter events, 22.2 us)
Async XLA Ops:
  2.2 5.8 %copy-start.13 = (bf16[4,1536]{1,0:T(4,128)(2,1)S(1)}, bf16[4,1536]{1,0:T(4,128)(2,1)}, u32[]{:S(2)}) copy-start(bf16[4,1536]{1,0:T(4,128)(2,1)} %param.14) | copy-start | bytes 36868
  3.5 34.6 %all-to-all-start = ((bf16[4,2,1,64,1536]{4,3,1,2,0:T(8,128)(2,1)}), bf16[4,2,1,64,1536]{4,3,1,2,0:T(8,128)(2,1)}, u32[]{:S(2)}, u32[]{:S(2)}) async-start(bf16[4,2,1,64,1536]{4,3,1,2,0:T(8,128)(2,1)} %maximum_bitcast_fusion), calls=%async_computation | async-start | bytes 3145728 | tf_op jit(solution)/shard_map/all_to_all | solution.py:352
  8.2 8.9 %copy-start.2 = (f32[4,1536]{0,1:T(8,128)}, f32[4,1536]{0,1:T(8,128)S(1)}, u32[]{:S(2)}) copy-start(f32[4,1536]{0,1:T(8,128)S(1)} %copy.76) | copy-start | bytes 73732
  19.3 11.3 %copy-start.14 = (f32[2,2,64]{2,1,0:T(2,128)S(1)}, f32[2,2,64]{2,1,0:T(2,128)}, u32[]{:S(2)}) copy-start(f32[2,2,64]{2,1,0:T(2,128)} %param.19) | copy-start | bytes 3076
  38.1 86.2 %all-to-all-start.1 = ((bf16[4,2,1,64,1536]{4,3,2,1,0:T(8,128)(2,1)}), bf16[4,2,1,64,1536]{4,3,2,1,0:T(8,128)(2,1)}, u32[]{:S(2)}, u32[]{:S(2)}) async-start(bf16[4,2,1,64,1536]{4,3,2,1,0:T(8,128)(2,1)} %pad_maximum_fusion), calls=%async_computation.1 | async-start | bytes 3145728 | tf_op jit(solution)/shard_map/all_to_all | solution.py:352
  203.2 5.1 %copy-start.15 = (bf16[1,1536,640]{2,1,0:T(8,128)(2,1)S(1)}, bf16[1,1536,640]{2,1,0:T(8,128)(2,1)}, u32[]{:S(2)}) copy-start(bf16[1,1536,640]{2,1,0:T(8,128)(2,1)} %get-tuple-element.50.refs_0_) | copy-start | bytes 5898244
  206.0 3.1 copy-start.12
  206.0 3.2 copy-start.9
  206.0 3.2 copy-start.10
  207.7 14.8 %collective-permute-start = (bf16[2,2,64,1536]{3,2,1,0:T(8,128)(2,1)S(1)}, bf16[2,2,64,1536]{3,2,1,0:T(8,128)(2,1)S(1)}, u32[]{:S(2)}, u32[]{:S(2)}) collective-permute-start(bf16[2,2,64,1536]{3,2,1,0:T(8,128)(2,1)S(1)} %get-tuple-element.103), channel_id=1, source_target_pairs={{0,1},{1,0},{2,3},{3,2},{4,5},{5,4},{6,7},{7,6},{8,9},{9,8},{10,11... | collective-permute-start | bytes 2359304 | tf_op jit(solution)/shard_map/ppermute | solution.py:339
  208.3 14.5 %collective-permute-start.9 = (bf16[1,1536,640]{2,1,0:T(8,128)(2,1)S(1)}, bf16[1,1536,640]{2,1,0:T(8,128)(2,1)S(1)}, u32[]{:S(2)}, u32[]{:S(2)}) collective-permute-start(bf16[1,1536,640]{2,1,0:T(8,128)(2,1)S(1)} %copy-done.15), channel_id=1, source_target_pairs={{0,1},{1,0},{2,3},{3,2},{4,5},{5,4},{6,7},{7,6},{8,9},{9,8},{10,11... | collective-permute-start | bytes 5898248 | tf_op jit(solution)/shard_map/ppermute | solution.py:339
  208.4 17.1 %collective-permute-start.10 = (bf16[1,1536,640]{2,1,0:T(8,128)(2,1)}, bf16[1,1536,640]{2,1,0:T(8,128)(2,1)}, u32[]{:S(2)}, u32[]{:S(2)}) collective-permute-start(bf16[1,1536,640]{2,1,0:T(8,128)(2,1)} %get-tuple-element.51.refs_1_), channel_id=1, source_target_pairs={{0,1},{1,0},{2,3},{3,2},{4,5},{5,4},{6,7},{7,6},{8,9},{9,8},{10,11... | collective-permute-start | bytes 5898248 | tf_op jit(solution)/shard_map/ppermute | solution.py:339
  209.1 6.9 %collective-permute-start.8 = (f32[10,1536]{1,0:T(8,128)S(1)}, f32[10,1536]{1,0:T(8,128)S(1)}, u32[]{:S(2)}, u32[]{:S(2)}) collective-permute-start(f32[10,1536]{1,0:T(8,128)S(1)} %select_maximum_fusion), channel_id=1, source_target_pairs={{0,1},{1,0},{2,3},{3,2},{4,5},{5,4},{6,7},{7,6},{8,9},{9,8},{10,11... | collective-permute-start | bytes 184328 | tf_op jit(solution)/shard_map/ppermute | solution.py:339
  209.2 10.1 %collective-permute-start.7 = (f32[2,8,1536]{2,1,0:T(8,128)S(1)}, f32[2,8,1536]{2,1,0:T(8,128)S(1)}, u32[]{:S(2)}, u32[]{:S(2)}) collective-permute-start(f32[2,8,1536]{2,1,0:T(8,128)S(1)} %pad_maximum_fusion.3), channel_id=1, source_target_pairs={{0,1},{1,0},{2,3},{3,2},{4,5},{5,4},{6,7},{7,6},{8,9},{9,8},{10,11... | collective-permute-start | bytes 294920 | tf_op jit(solution)/shard_map/ppermute | solution.py:339
  216.0 12.0 %collective-permute-start.11 = (bf16[1,1,640,1536]{3,2,1,0:T(8,128)(2,1)}, bf16[1,1,640,1536]{3,2,1,0:T(8,128)(2,1)}, u32[]{:S(2)}, u32[]{:S(2)}) collective-permute-start(bf16[1,1,640,1536]{3,2,1,0:T(8,128)(2,1)} %bitcast.27.refs_4_), channel_id=1, source_target_pairs={{0,1},{1,0},{2,3},{3,2},{4,5},{5,4},{6,7},{7,6},{8,9},{9,8},{10,11... | collective-permute-start | bytes 5898248 | tf_op jit(solution)/shard_map/ppermute | solution.py:339
  219.4 10.5 %collective-permute-start.12 = (bf16[1,1,640,1536]{3,2,1,0:T(8,128)(2,1)}, bf16[1,1,640,1536]{3,2,1,0:T(8,128)(2,1)}, u32[]{:S(2)}, u32[]{:S(2)}) collective-permute-start(bf16[1,1,640,1536]{3,2,1,0:T(8,128)(2,1)} %bitcast.28.refs_5_), channel_id=1, source_target_pairs={{0,1},{1,0},{2,3},{3,2},{4,5},{5,4},{6,7},{7,6},{8,9},{9,8},{10,11... | collective-permute-start | bytes 5898248 | tf_op jit(solution)/shard_map/ppermute | solution.py:339
  222.5 48.3 %collective-permute-start.5 = (bf16[1,3,640,1536]{3,2,1,0:T(8,128)(2,1)}, bf16[1,3,640,1536]{3,2,1,0:T(8,128)(2,1)}, u32[]{:S(2)}, u32[]{:S(2)}) collective-permute-start(bf16[1,3,640,1536]{3,2,1,0:T(8,128)(2,1)} %get-tuple-element.39.refs_4_), channel_id=1, source_target_pairs={{0,1},{1,0},{2,3},{3,2},{4,5},{5,4},{6,7},{7,6},{8,9},{9,8},{10,11... | collective-permute-start | bytes 17694728 | tf_op jit(solution)/shard_map/ppermute | solution.py:339
  222.9 48.0 %collective-permute-start.6 = (bf16[1,3,640,1536]{3,2,1,0:T(8,128)(2,1)}, bf16[1,3,640,1536]{3,2,1,0:T(8,128)(2,1)}, u32[]{:S(2)}, u32[]{:S(2)}) collective-permute-start(bf16[1,3,640,1536]{3,2,1,0:T(8,128)(2,1)} %get-tuple-element.40.refs_5_), channel_id=1, source_target_pairs={{0,1},{1,0},{2,3},{3,2},{4,5},{5,4},{6,7},{7,6},{8,9},{9,8},{10,11... | collective-permute-start | bytes 17694728 | tf_op jit(solution)/shard_map/ppermute | solution.py:339
  225.5 27.1 %collective-permute-start.2 = (bf16[1,2,384,1536]{3,2,1,0:T(8,128)(2,1)}, bf16[1,2,384,1536]{3,2,1,0:T(8,128)(2,1)}, u32[]{:S(2)}, u32[]{:S(2)}) collective-permute-start(bf16[1,2,384,1536]{3,2,1,0:T(8,128)(2,1)} %get-tuple-element.36), channel_id=1, source_target_pairs={{0,1},{1,0},{2,3},{3,2},{4,5},{5,4},{6,7},{7,6},{8,9},{9,8},{10,11... | collective-permute-start | bytes 7077896 | tf_op jit(solution)/shard_map/ppermute | solution.py:339
  228.1 26.6 %collective-permute-start.1 = (bf16[1,2,384,1536]{3,2,1,0:T(8,128)(2,1)}, bf16[1,2,384,1536]{3,2,1,0:T(8,128)(2,1)}, u32[]{:S(2)}, u32[]{:S(2)}) collective-permute-start(bf16[1,2,384,1536]{3,2,1,0:T(8,128)(2,1)} %get-tuple-element.35), channel_id=1, source_target_pairs={{0,1},{1,0},{2,3},{3,2},{4,5},{5,4},{6,7},{7,6},{8,9},{9,8},{10,11... | collective-permute-start | bytes 7077896 | tf_op jit(solution)/shard_map/ppermute | solution.py:339
  229.9 40.9 %collective-permute-start.3 = (bf16[1,1536,640]{2,1,0:T(8,128)(2,1)}, bf16[1,1536,640]{2,1,0:T(8,128)(2,1)}, u32[]{:S(2)}, u32[]{:S(2)}) collective-permute-start(bf16[1,1536,640]{2,1,0:T(8,128)(2,1)} %get-tuple-element.37.refs_0_), channel_id=1, source_target_pairs={{0,1},{1,0},{2,3},{3,2},{4,5},{5,4},{6,7},{7,6},{8,9},{9,8},{10,11... | collective-permute-start | bytes 5898248 | tf_op jit(solution)/shard_map/ppermute | solution.py:339
  252.6 18.3 %collective-permute-start.4 = (bf16[1,1536,640]{2,1,0:T(8,128)(2,1)}, bf16[1,1536,640]{2,1,0:T(8,128)(2,1)}, u32[]{:S(2)}, u32[]{:S(2)}) collective-permute-start(bf16[1,1536,640]{2,1,0:T(8,128)(2,1)} %get-tuple-element.38.refs_1_), channel_id=1, source_target_pairs={{0,1},{1,0},{2,3},{3,2},{4,5},{5,4},{6,7},{7,6},{8,9},{9,8},{10,11... | collective-permute-start | bytes 5898248 | tf_op jit(solution)/shard_map/ppermute | solution.py:339
  258.7 5.2 %copy-start.3 = (bf16[1,333,1536]{2,1,0:T(8,128)(2,1)S(1)}, bf16[1,333,1536]{2,1,0:T(8,128)(2,1)}, u32[]{:S(2)}) copy-start(bf16[1,333,1536]{2,1,0:T(8,128)(2,1)} %get-tuple-element.106) | copy-start | bytes 3068932
  258.7 5.2 %copy-start.5 = (bf16[1,333,1536]{2,1,0:T(8,128)(2,1)S(1)}, bf16[1,333,1536]{2,1,0:T(8,128)(2,1)}, u32[]{:S(2)}) copy-start(bf16[1,333,1536]{2,1,0:T(8,128)(2,1)} %get-tuple-element.104) | copy-start | bytes 3068932
  (8 other events, 16.8 us)

commit v4 on v3

--- a/solution.py
+++ b/solution.py
@@ -88,10 +88,14 @@
         prologue(tok_ref, cot_ref, mod_ref.at[0, 0], hid_ref, hid_trn_ref.at[0], dy_ref.at[0], 0, n_img, 128)
         prologue(tok_t_ref.at[0], cot_t_ref.at[0], mod_ref.at[0, 1], hid_ref, hid_trn_ref.at[0], dy_ref.at[0], n_img, n_keys - n_img, 128)
 
-    hid_i, hid_t = hid_ref[:n_img], hid_ref[n_img:]
+    hid_i, hid_t = hid_ref[:n_img], hid_ref[n_img:k_rows]
+
+    def pad_tail(arr):
+        return jnp.concatenate([arr, jnp.zeros((n_tok - k_rows, width), F32)], axis=0)
+
     for idx, (w_ref, b_ref) in enumerate(((wq_ref, bq_ref), (wk_ref, bk_ref), (wv_ref, bv_ref))):
         raw_i = dot(hid_i, w_ref[0]) + b_ref[0:1, :]
-        raw_t = dot(hid_t, w_ref[1]) + b_ref[1:2, :]
+        raw_t = pad_tail(dot(hid_t, w_ref[1]) + b_ref[1:2, :])
         if idx == 2:
             v_ref[:n_img] = raw_i.astype(BF16)
             v_ref[n_img:] = raw_t.astype(BF16)
@@ -108,7 +112,7 @@
             nat_ref[idx] = normed.T.astype(BF16)
 
     do_i = dot(dy_ref[0, :n_img], wo_ref[0], NT)
-    do_t = dot(dy_ref[0, n_img:], wo_ref[1], NT)
+    do_t = pad_tail(dot(dy_ref[0, n_img:k_rows], wo_ref[1], NT))
     do_nat_ref[:n_img] = do_i.astype(BF16)
     do_nat_ref[n_img:] = do_t.astype(BF16)
     do_trn_ref[:, :n_img] = do_i.T.astype(BF16)
@@ -117,34 +121,48 @@
     dv_ref[k_rows:] = jnp.zeros((n_tok - k_rows, width), F32)
 
     exp_scale = att_scale * math.log2(math.e)
-
-    def scores_of(head):
-        rows = slice(head * head_dim, (head + 1) * head_dim)
-        return dot(nat_ref[1, :k_rows, rows], trn_ref[0, rows, :])
-
-    scores = scores_of(0)
-    for head in range(heads):
-        rows = slice(head * head_dim, (head + 1) * head_dim)
-        k_trn, v_trn = trn_ref[1, rows, :k_rows], trn_ref[2, rows, :k_rows]
-        q_nat, v_nat = nat_ref[0, :, rows], v_ref[:k_rows, rows]
+    two = 2 * head_dim
+
+    def diag_cols(arr):
+        top = lax.broadcasted_iota(jnp.int32, arr.shape, 0) < head_dim
+        zero = jnp.zeros_like(arr)
+        return jnp.concatenate([jnp.where(top, arr, zero), jnp.where(top, zero, arr)], axis=1)
+
+    def diag_rows(arr):
+        left = lax.broadcasted_iota(jnp.int32, arr.shape, 1) < head_dim
+        zero = jnp.zeros_like(arr)
+        return jnp.concatenate([jnp.where(left, arr, zero), jnp.where(left, zero, arr)], axis=0)
+
+    def diag_take(arr):
+        return jnp.concatenate([arr[:head_dim, :n_tok], arr[head_dim:, n_tok:]], axis=0)
+
+    def scores_of(lo):
+        rows = slice(lo, lo + two)
+        return dot(nat_ref[1, :k_rows, rows], diag_cols(trn_ref[0, rows, :]))
+
+    ahead = scores_of(0)
+    for lo in range(0, width, two):
+        rows = slice(lo, lo + two)
         do_trn = do_trn_ref[rows]
-        ahead = scores_of(head + 1) if head + 1 < heads else None
-        d_prob = dot(v_nat, do_trn)
-        tail_row = k_main + lax.broadcasted_iota(jnp.int32, (16, n_tok), 0)
+        scores = ahead
+        d_prob = dot(v_ref[:k_rows, rows], diag_cols(do_trn))
+        if lo + two < width:
+            ahead = scores_of(lo + two)
+        tail_row = k_main + lax.broadcasted_iota(jnp.int32, (16, 2 * n_tok), 0)
         tail = jnp.where(tail_row < n_keys, scores[k_main:], -jnp.inf)
         scores = jnp.concatenate([scores[:k_main], tail], axis=0)
         peak = jnp.max(scores, axis=0, keepdims=True)
         exps = jnp.exp2((scores - peak) * exp_scale)
         inv_sum = 1.0 / jnp.sum(exps, axis=0, keepdims=True)
         prob_lo = (exps * inv_sum).astype(BF16)
-        out_trn = dot(v_trn, prob_lo).astype(BF16)
+        out_trn = diag_take(dot(trn_ref[2, rows, :k_rows], prob_lo)).astype(BF16)
         o_trn_ref[0, rows] = out_trn
-        delta = jnp.sum(out_trn.astype(F32) * do_trn.astype(F32), axis=0, keepdims=True)
+        prod = out_trn.astype(F32) * do_trn.astype(F32)
+        delta = jnp.concatenate([jnp.sum(prod[:head_dim], axis=0, keepdims=True), jnp.sum(prod[head_dim:], axis=0, keepdims=True)], axis=1)
         d_score = (exps * inv_sum * (d_prob - delta)).astype(BF16)
-        dv_ref[:k_rows, rows] = dot(prob_lo, do_nat_ref[:, rows])
-        dk_ref[:k_rows, rows] = dot(d_score, q_nat) * att_scale
-        dq_ref[rows] = dot(k_trn, d_score) * att_scale
-        scores = ahead
+        dv_ref[:k_rows, rows] = dot(prob_lo, diag_rows(do_nat_ref[:, rows]))
+        dk_ref[:k_rows, rows] = dot(d_score, diag_rows(nat_ref[0, :, rows])) * att_scale
+        dq_ref[rows] = diag_take(dot(trn_ref[1, rows, :k_rows], d_score)) * att_scale
 
     o_nat = o_trn_ref[0].T
 
@@ -160,7 +178,7 @@
         dg_ref[...] = jnp.zeros_like(dg_ref)
 
     y_i_ref[...] += dot(o_nat[:n_img], wo_ref[0])
-    y_t_ref[...] += dot(o_nat[n_img:], wo_ref[1])
+    y_t_ref[:k_rows - n_img] += dot(o_nat[n_img:k_rows], wo_ref[1])
 
     d_raw = []
     for idx in range(2):
@@ -185,7 +203,7 @@
     db_ref[0, 6:8, :] = jnp.zeros((2, width), F32)
     w_refs = (wq_ref, wk_ref, wv_ref)
     acc_i_ref[...] += sum(dot(d_lo[idx][:n_img], w_refs[idx][0], NT) for idx in range(3))
-    acc_t_ref[...] += sum(dot(d_lo[idx][n_img:], w_refs[idx][1], NT) for idx in range(3))
+    acc_t_ref[:k_rows - n_img] += sum(dot(d_lo[idx][n_img:k_rows], w_refs[idx][1], NT) for idx in range(3))
 
     @pl.when(step_g == n_grp - 1)
     def _():
@@ -268,7 +286,6 @@
 
     chunk = 512
     if with_ada:
-        dmods = [dmod_ref[branch, 0].astype(BF16) for branch in range(2)]
         dmods_trn = [dmod_ref[branch, 0].T.astype(BF16) for branch in range(2)]
 
     @pl.loop(0, d_model // chunk)
@@ -277,8 +294,9 @@
         out_ref[0, rows] = dot(trn_i_ref[rows], rhs_i_ref[...])
         out_ref[1, rows] = dot(trn_t_ref[rows], rhs_t_ref[...])
         if with_ada:
+            act = act_ref[rows].astype(F32)
             for branch in range(2):
-                dw_ref[branch, rows] = dot(act_ref[rows], dmods[branch])
+                dw_ref[branch, rows] = sum(act[:, idx:idx + 1] * dmod_ref[branch, 0, idx:idx + 1, :] for idx in range(2 * n_b))
                 dact_ref[rows] += dot(w_ref[branch, rows], dmods_trn[branch])
 
 
@@ -358,7 +376,7 @@
             return jnp.where(core == 0, jnp.concatenate([mine, other], axis), jnp.concatenate([other, mine], axis))
 
         cond_act = jax.nn.silu(cond_vec.astype(F32)).astype(BF16)
-        cond_mod = ada_fwd(cond_act, w_ada, b_ada, 1536)
+        cond_mod = ada_fwd(cond_act, w_ada, b_ada, 768)
         own_mod = own(cond_mod, 1).reshape(2, n_own, 3, d_model).swapaxes(0, 1)
         pad_rows = ((0, 0), (0, n_txt - ctx_len), (0, 0))
         text_own, cot_own = jnp.pad(own(text_in), pad_rows), jnp.pad(own(text_cot), pad_rows)
@@ -386,19 +404,18 @@
         d_mod, db_out, db_qkv = sums[:, :3], jnp.sum(sums[:, 3], 1), rest[:6].reshape(2, 3 * d_model)
         d_gain = jnp.sum(rest[6:, :dg.shape[1]].reshape(2, 2, -1, qk_gain.shape[-1]), 2)
 
-        dw_out, = wgrad(core, o_trn, dy, n_img, 256)
+        dw_out, = wgrad(core, o_trn, dy, n_img, 512)
         dw_qkv, dw_ada, d_act = wgrad(core, hid_trn, dp, n_img, 512, (cond_act, d_mod, w_ada))
         d_act = d_act.T[:n_batch]
         db_ada = jnp.sum(d_mod, axis=2).reshape(2, 3 * d_model)
         _, pull_act = jax.vjp(jax.nn.silu, cond_vec.astype(F32))
         grad_cond = pull_act(d_act.astype(BF16).astype(F32))[0]
 
-        img_pair = jnp.concatenate([out[4] for out in outs])
         chip_lo = chip * pair * tok_dev
-        img_mine = lax.dynamic_slice_in_dim(img_pair, chip_lo + core * tok_dev, tok_dev, 2)
-        img_send = lax.dynamic_slice_in_dim(img_pair, chip_lo + (1 - core) * tok_dev, tok_dev, 2)
+        img_mine, img_send = (jnp.concatenate([lax.dynamic_slice_in_dim(out[4], chip_lo + pos * tok_dev, tok_dev, 2) for out in outs]) for pos in (core, 1 - core))
         img_pair = ordered(img_mine, swap(img_send))
-        text_new, grad_text = (ordered(jnp.concatenate([arr[:, pos, :ctx_len] for arr in txt[:n_own]]), jnp.concatenate([arr[:, pos, :ctx_len] for arr in txt[n_own:]])) for pos in range(2))
+        txt = ordered(jnp.concatenate(txt[:n_own]), jnp.concatenate(txt[n_own:]))
+        text_new, grad_text = txt[:, 0, :ctx_len], txt[:, 1, :ctx_len]
         return (img_pair[:, 0], text_new, img_pair[:, 1], grad_text, grad_cond, dw_ada, db_ada, dw_qkv, db_qkv, d_gain, dw_out, db_out)
 
     data_spec = P('dp', 'sp', None)

time: 353 us -> 345 us (0.977)
  local copies, waits for them, and re-layouts: 48.9 us -> 33.1 us
  other arithmetic: 13.6 us -> 22.7 us
    squeeze x4 -> x1, local copies, waits for them, and re-layouts: 9.43 us -> 0.79 us  [device_fn(): text_new, grad_text = (txt[:, 0, :ctx_len], txt[:, 1, :ctx_len])]
    select_n x3 -> x2, other arithmetic: 3.98 us -> 10 us  [ordered(): jnp.where(core == 0, jnp.concatenate([mine, other], axis), jnp.concatenat...]
    pallas_call x2, Pallas kernels: 158 us -> 153 us  [fused_block(): pl.pallas_call(functools.partial(block_kernel, n_keys, heads), out_shape=...]
    unnamed x44 -> x29, local copies, waits for them, and re-layouts: 19.1 us -> 15 us
where the time goes in v4:
time: 345 us; the launch traced here: 338 us
  Pallas kernels  263 us (76%)
  local copies, waits for them, and re-layouts  33.1 us (10%)
  other arithmetic  22.7 us (7%)
  starting transfers between devices  12.6 us (4%)
  waiting for transfers between devices  5.25 us (2%)
    pallas_call x2, Pallas kernels, fused_block(): pl.pallas_call(functools.partial(block_kernel, n_keys, heads), out_shape=...  153 us
    pallas_call x2, Pallas kernels, wgrad(): pl.pallas_call(functools.partial(wgrad_kernel, n_img, n_b, ada is not Non...  95.7 us
    unnamed x29, local copies, waits for them, and re-layouts  15 us
    pallas_call x1, Pallas kernels, ada_fwd(): pl.pallas_call(ada_fwd_kernel, out_shape=jax.ShapeDtypeStruct((2, 16, wid...  14.1 us
    select_n x2, other arithmetic, ordered(): jnp.where(core == 0, jnp.concatenate([mine, other], axis), jnp.concatenat...  10 us
    all_to_all x2, starting transfers between devices, device_fn(): lax.all_to_all(jnp.concatenate([img_pair[:, :, idx].swapaxes(0, 1)] * n_c...  8.84 us
    dynamic_slice x2, local copies, waits for them, and re-layouts, own(): return lax.dynamic_slice_in_dim(arr, own_lo, n_own, axis)  7.65 us
  transfers between devices with their start and end apart: 15, of which 1 were waited for; matrix products, arithmetic and copies ran while one was open for 14% of the time, Pallas kernels for 33%

profile of v4, /device:TPU:0, one launch (start us, length us, event | category | flops | bytes accessed | tf_op | source)
XLA Modules:
  0.0 337.9 jit_solution(6997992197074057227)
XLA Ops:
  0.6 1.5 fusion.2
  2.2 1.3 maximum_bitcast_fusion
  3.5 4.5 %all-to-all-start = ((bf16[4,2,1,64,1536]{4,3,1,2,0:T(8,128)(2,1)}), bf16[4,2,1,64,1536]{4,3,1,2,0:T(8,128)(2,1)}, u32[]{:S(2)}, u32[]{:S(2)}) async-start(bf16[4,2,1,64,1536]{4,3,1,2,0:T(8,128)(2,1)} %maximum_bitcast_fusion), calls=%async_computation | async-start | bytes 3145728 | tf_op jit(solution)/shard_map/all_to_all | solution.py:370
  8.0 1.3 pad_maximum_fusion
  9.3 7.6 %constant_dynamic-slice_fusion.5 = (bf16[2,333,1536]{2,0,1:T(2,128)(2,1)S(1)}, bf16[2,333,1536]{2,0,1:T(2,128)(2,1)S(1)}) fusion(bf16[4,333,1536]{2,0,1:T(4,128)(2,1)} %param.23, s32[]{:T(128)S(6)} %select_n.38, bf16[4,333,1536]{2,0,1:T(4,128)(2,1)} %param.13), kind=kLoop, calls=%fused_computation.43 | loop fusion | bytes 8183812 | tf_op jit(solution)/shard_map/dynamic_slice | solution.py:373
  16.9 1.5 copy.89
  19.9 14.1 %ada_fwd.1 = f32[2,16,4608]{2,1,0:T(8,128)S(1)} custom-call(bf16[16,1536]{1,0:T(8,128)(2,1)S(1)} %pad.22.clone.act_ref, bf16[2,1536,4608]{2,1,0:T(8,128)(2,1)} %refs_10_.1, f32[2,4608]{1,0:T(2,128)S(1)} %copy-done), custom_call_target="tpu_custom_call" | custom-call | flops 452984832 | bytes 28311552 | tf_op jit(solution)/shard_map/ada_fwd/pallas_call | solution.py:339
  34.7 1.1 pad_maximum_fusion.1.gain_ref
  36.5 1.6 pad_slice_fusion.3
  38.1 1.6 pad_slice_fusion.1
  40.3 4.4 %all-to-all-start.1 = ((bf16[4,2,1,64,1536]{4,3,2,1,0:T(8,128)(2,1)}), bf16[4,2,1,64,1536]{4,3,2,1,0:T(8,128)(2,1)}, u32[]{:S(2)}, u32[]{:S(2)}) async-start(bf16[4,2,1,64,1536]{4,3,2,1,0:T(8,128)(2,1)} %pad_maximum_fusion), calls=%async_computation.1 | async-start | bytes 3145728 | tf_op jit(solution)/shard_map/all_to_all | solution.py:370
  44.7 76.7 %fused_block.2 = (bf16[1,1536,640]{2,1,0:T(8,128)(2,1)}, bf16[1,640,1536]{2,1,0:T(8,128)(2,1)}, bf16[1,1536,640]{2,1,0:T(8,128)(2,1)}, bf16[1,3,640,1536]{3,2,1,...) custom-call(bf16[4,2,1,64,1536]{4,3,2,1,0:T(8,128)(2,1)} %bitcast.5., ...), custom_call_target="tpu_custom_call" | custom-call | flops 31708938240 | bytes 104857600 | tf_op jit(solution)/shard_map/fused_block/pallas_call | solution.py:252
  121.3 76.4 %fused_block.3 = (bf16[1,1536,640]{2,1,0:T(8,128)(2,1)}, bf16[1,640,1536]{2,1,0:T(8,128)(2,1)}, bf16[1,1536,640]{2,1,0:T(8,128)(2,1)}, bf16[1,3,640,1536]{3,2,1,...) custom-call(bf16[4,2,1,64,1536]{4,3,2,1,0:T(8,128)(2,1)} %all-to-all, ...), custom_call_target="tpu_custom_call" | custom-call | flops 31708938240 | bytes 104857600 | tf_op jit(solution)/shard_map/fused_block/pallas_call | solution.py:252
  200.8 1.4 add_reduce_fusion
  202.7 1.2 constant_dynamic-slice_fusion.2
  204.1 5.2 %collective-permute-done.8 = f32[10,1536]{1,0:T(8,128)S(1)} collective-permute-done((f32[10,1536]{1,0:T(8,128)S(1)}, f32[10,1536]{1,0:T(8,128)S(1)}, u32[]{:S(2)}, u32[]{:S(2)}) %collective-permute-start.8) | collective-permute-done | bytes 61472 | tf_op jit(solution)/shard_map/ppermute | solution.py:357
  215.8 1.2 slice_bitcast_fusion.2
  217.2 22.2 %shard_map.212 = f32[2,1536,1536]{2,1,0:T(8,128)} custom-call(s32[1]{0:T(128)} %bitcast.15.core_ref, bf16[1,1536,640]{2,1,0:T(8,128)(2,1)} %get-tuple-element.50.refs_0_, bf16[1,1536,640]{2,1,0:T(8,128)(2,1)} %get-tuple-element.51.refs_1_, bf16[1,1536,640]{2,1,0:T(8,128)(2,1)} %collective-permute-done.9.refs_2_, ...), custom_call_target="tpu_custom_call" | custom-call | flops 12079595520 | bytes 18874368 | tf_op jit(solution)/shard_map/pallas_call | solution.py:321
  239.8 9.7 %maximum_select_fusion = bf16[4,2,384,1536]{3,2,1,0:T(8,128)(2,1)S(1)} fusion(bf16[1,2,384,1536]{3,2,1,0:T(8,128)(2,1)} %collective-permute-done.2, bf16[1,2,384,1536]{3,2,1,0:T(8,128)(2,1)} %collective-permute-done.1, bf16[1,2,384,1536]{3,2,1,0:T(8,128)(2,1)} %get-tuple-element.36, bf16[1,2,384,1536]{3,2,1,0:T(8,128)(2,1)} %get-tuple-element.35, pred[]{:T(512)S(6)} %eq.2), kind=kLoop, calls=%fused_computation | loop fusion | flops 33030144 | bytes 18874368 | tf_op jit(solution)/shard_map/jit(_where)/select_n | solution.py:376
  250.3 5.1 %copy.84 = bf16[4,333,1536]{2,0,1:T(4,128)(2,1)} copy(bf16[4,333,1536]{2,1,0:T(8,128)(2,1)S(1)} %get-tuple-element.103) | data formatting | bytes 8183808
  255.5 5.1 %copy.85 = bf16[4,333,1536]{2,0,1:T(4,128)(2,1)} copy(bf16[4,333,1536]{2,1,0:T(8,128)(2,1)S(1)} %get-tuple-element.102) | data formatting | bytes 8183808
  260.6 73.5 %shard_map.211 = (f32[2,1536,4608]{2,1,0:T(8,128)}, f32[2,1536,4608]{2,1,0:T(8,128)}, f32[1536,16]{1,0:T(8,128)}) custom-call(s32[1]{0:T(128)} %bitcast.15.core_ref, bf16[1,1536,640]{2,1,0:T(8,128)(2,1)} %get-tuple-element.37.refs_0_, bf16[1,1536,640]{2,1,0:T(8,128)(2,1)} %get-tuple-element.38.refs_1_, bf16[1,1536,640]{2,1,0:T(8,128)(2,1)} %collective-permute-done.3.refs_2_, ...), custom_call_target="tpu_custom_call" | custom-call | flops 36238786560 | bytes 169869312 | tf_op jit(solution)/shard_map/pallas_call | solution.py:321
  334.2 1.2 convert_bitcast_fusion
  335.4 1.4 fusion
  (87 shorter events, 15.7 us)
Async XLA Ops:
  3.5 36.8 %all-to-all-start = ((bf16[4,2,1,64,1536]{4,3,1,2,0:T(8,128)(2,1)}), bf16[4,2,1,64,1536]{4,3,1,2,0:T(8,128)(2,1)}, u32[]{:S(2)}, u32[]{:S(2)}) async-start(bf16[4,2,1,64,1536]{4,3,1,2,0:T(8,128)(2,1)} %maximum_bitcast_fusion), calls=%async_computation | async-start | bytes 3145728 | tf_op jit(solution)/shard_map/all_to_all | solution.py:370
  19.1 0.8 copy-start
  19.3 14.7 %copy-start.2 = (f32[4,1536]{0,1:T(8,128)}, f32[4,1536]{0,1:T(8,128)S(1)}, u32[]{:S(2)}) copy-start(f32[4,1536]{0,1:T(8,128)S(1)} %copy.76) | copy-start | bytes 73732
  19.6 14.5 %copy-start.3 = (bf16[4,1536]{0,1:T(8,128)(2,1)}, bf16[4,1536]{0,1:T(8,128)(2,1)S(1)}, u32[]{:S(2)}) copy-start(bf16[4,1536]{0,1:T(8,128)(2,1)S(1)} %multiply_convert_fusion) | copy-start | bytes 36868
  19.9 14.4 %copy-start.9 = (f32[2,2,64]{2,1,0:T(2,128)S(1)}, f32[2,2,64]{2,1,0:T(2,128)}, u32[]{:S(2)}) copy-start(f32[2,2,64]{2,1,0:T(2,128)} %param.19) | copy-start | bytes 3076
  34.5 2.1 copy-start.1
  40.3 81.1 %all-to-all-start.1 = ((bf16[4,2,1,64,1536]{4,3,2,1,0:T(8,128)(2,1)}), bf16[4,2,1,64,1536]{4,3,2,1,0:T(8,128)(2,1)}, u32[]{:S(2)}, u32[]{:S(2)}) async-start(bf16[4,2,1,64,1536]{4,3,2,1,0:T(8,128)(2,1)} %pad_maximum_fusion), calls=%async_computation.1 | async-start | bytes 3145728 | tf_op jit(solution)/shard_map/all_to_all | solution.py:370
  197.8 6.2 %copy-start.5 = (bf16[1,2,256,1536]{3,2,1,0:T(8,128)(2,1)S(1)}, bf16[1,2,256,1536]{3,2,1,0:T(8,128)(2,1)}, u32[]{:S(2)}) copy-start(bf16[1,2,256,1536]{3,2,1,0:T(8,128)(2,1)} %get-tuple-element.33) | copy-start | bytes 4718596
  198.8 10.7 %collective-permute-start.7 = (f32[2,8,1536]{2,1,0:T(8,128)S(1)}, f32[2,8,1536]{2,1,0:T(8,128)S(1)}, u32[]{:S(2)}, u32[]{:S(2)}) collective-permute-start(f32[2,8,1536]{2,1,0:T(8,128)S(1)} %pad_maximum_fusion.4), channel_id=1, source_target_pairs={{0,1},{1,0},{2,3},{3,2},{4,5},{5,4},{6,7},{7,6},{8,9},{9,8},{10,11... | collective-permute-start | bytes 294920 | tf_op jit(solution)/shard_map/ppermute | solution.py:357
  199.4 12.8 %collective-permute-start.9 = (bf16[1,1536,640]{2,1,0:T(8,128)(2,1)}, bf16[1,1536,640]{2,1,0:T(8,128)(2,1)}, u32[]{:S(2)}, u32[]{:S(2)}) collective-permute-start(bf16[1,1536,640]{2,1,0:T(8,128)(2,1)} %get-tuple-element.50.refs_0_), channel_id=1, source_target_pairs={{0,1},{1,0},{2,3},{3,2},{4,5},{5,4},{6,7},{7,6},{8,9},{9,8},{10,11... | collective-permute-start | bytes 5898248 | tf_op jit(solution)/shard_map/ppermute | solution.py:357
  199.4 13.1 %collective-permute-start.10 = (bf16[1,1536,640]{2,1,0:T(8,128)(2,1)}, bf16[1,1536,640]{2,1,0:T(8,128)(2,1)}, u32[]{:S(2)}, u32[]{:S(2)}) collective-permute-start(bf16[1,1536,640]{2,1,0:T(8,128)(2,1)} %get-tuple-element.51.refs_1_), channel_id=1, source_target_pairs={{0,1},{1,0},{2,3},{3,2},{4,5},{5,4},{6,7},{7,6},{8,9},{9,8},{10,11... | collective-permute-start | bytes 5898248 | tf_op jit(solution)/shard_map/ppermute | solution.py:357
  199.9 12.8 %collective-permute-start.11 = (bf16[1,1,640,1536]{3,2,1,0:T(8,128)(2,1)}, bf16[1,1,640,1536]{3,2,1,0:T(8,128)(2,1)}, u32[]{:S(2)}, u32[]{:S(2)}) collective-permute-start(bf16[1,1,640,1536]{3,2,1,0:T(8,128)(2,1)} %bitcast.53), channel_id=1, source_target_pairs={{0,1},{1,0},{2,3},{3,2},{4,5},{5,4},{6,7},{7,6},{8,9},{9,8},{10,11... | collective-permute-start | bytes 5898248 | tf_op jit(solution)/shard_map/ppermute | solution.py:357
  202.2 7.1 %collective-permute-start.8 = (f32[10,1536]{1,0:T(8,128)S(1)}, f32[10,1536]{1,0:T(8,128)S(1)}, u32[]{:S(2)}, u32[]{:S(2)}) collective-permute-start(f32[10,1536]{1,0:T(8,128)S(1)} %select_maximum_fusion), channel_id=1, source_target_pairs={{0,1},{1,0},{2,3},{3,2},{4,5},{5,4},{6,7},{7,6},{8,9},{9,8},{10,11... | collective-permute-start | bytes 184328 | tf_op jit(solution)/shard_map/ppermute | solution.py:357
  202.7 7.1 %copy-start.4 = (bf16[4,1536]{0,1:T(8,128)(2,1)S(1)}, bf16[4,1536]{0,1:T(8,128)(2,1)}, u32[]{:S(2)}) copy-start(bf16[4,1536]{0,1:T(8,128)(2,1)} %copy-done.3) | copy-start | bytes 36868
  204.0 9.2 %copy-start.6 = (f32[1,8,1536]{2,1,0:T(8,128)S(1)}, f32[1,8,1536]{2,1,0:T(8,128)}, u32[]{:S(2)}) copy-start(f32[1,8,1536]{2,1,0:T(8,128)} %get-tuple-element.41) | copy-start | bytes 147460
  204.0 9.1 %copy-start.7 = (f32[1,8,1536]{2,1,0:T(8,128)S(1)}, f32[1,8,1536]{2,1,0:T(8,128)}, u32[]{:S(2)}) copy-start(f32[1,8,1536]{2,1,0:T(8,128)} %get-tuple-element.42) | copy-start | bytes 147460
  209.3 2.7 collective-permute-start
  209.5 7.6 %collective-permute-start.12 = (bf16[1,1,640,1536]{3,2,1,0:T(8,128)(2,1)}, bf16[1,1,640,1536]{3,2,1,0:T(8,128)(2,1)}, u32[]{:S(2)}, u32[]{:S(2)}) collective-permute-start(bf16[1,1,640,1536]{3,2,1,0:T(8,128)(2,1)} %bitcast.22.refs_5_), channel_id=1, source_target_pairs={{0,1},{1,0},{2,3},{3,2},{4,5},{5,4},{6,7},{7,6},{8,9},{9,8},{10,11... | collective-permute-start | bytes 5898248 | tf_op jit(solution)/shard_map/ppermute | solution.py:357
  212.1 27.3 %collective-permute-start.2 = (bf16[1,2,384,1536]{3,2,1,0:T(8,128)(2,1)}, bf16[1,2,384,1536]{3,2,1,0:T(8,128)(2,1)}, u32[]{:S(2)}, u32[]{:S(2)}) collective-permute-start(bf16[1,2,384,1536]{3,2,1,0:T(8,128)(2,1)} %get-tuple-element.36), channel_id=1, source_target_pairs={{0,1},{1,0},{2,3},{3,2},{4,5},{5,4},{6,7},{7,6},{8,9},{9,8},{10,11... | collective-permute-start | bytes 7077896 | tf_op jit(solution)/shard_map/ppermute | solution.py:357
  212.2 27.6 %collective-permute-start.1 = (bf16[1,2,384,1536]{3,2,1,0:T(8,128)(2,1)}, bf16[1,2,384,1536]{3,2,1,0:T(8,128)(2,1)}, u32[]{:S(2)}, u32[]{:S(2)}) collective-permute-start(bf16[1,2,384,1536]{3,2,1,0:T(8,128)(2,1)} %get-tuple-element.35), channel_id=1, source_target_pairs={{0,1},{1,0},{2,3},{3,2},{4,5},{5,4},{6,7},{7,6},{8,9},{9,8},{10,11... | collective-permute-start | bytes 7077896 | tf_op jit(solution)/shard_map/ppermute | solution.py:357
  212.6 48.0 %collective-permute-start.5 = (bf16[1,3,640,1536]{3,2,1,0:T(8,128)(2,1)}, bf16[1,3,640,1536]{3,2,1,0:T(8,128)(2,1)}, u32[]{:S(2)}, u32[]{:S(2)}) collective-permute-start(bf16[1,3,640,1536]{3,2,1,0:T(8,128)(2,1)} %get-tuple-element.39.refs_4_), channel_id=1, source_target_pairs={{0,1},{1,0},{2,3},{3,2},{4,5},{5,4},{6,7},{7,6},{8,9},{9,8},{10,11... | collective-permute-start | bytes 17694728 | tf_op jit(solution)/shard_map/ppermute | solution.py:357
  212.7 47.9 %collective-permute-start.6 = (bf16[1,3,640,1536]{3,2,1,0:T(8,128)(2,1)}, bf16[1,3,640,1536]{3,2,1,0:T(8,128)(2,1)}, u32[]{:S(2)}, u32[]{:S(2)}) collective-permute-start(bf16[1,3,640,1536]{3,2,1,0:T(8,128)(2,1)} %get-tuple-element.40.refs_5_), channel_id=1, source_target_pairs={{0,1},{1,0},{2,3},{3,2},{4,5},{5,4},{6,7},{7,6},{8,9},{9,8},{10,11... | collective-permute-start | bytes 17694728 | tf_op jit(solution)/shard_map/ppermute | solution.py:357
  217.1 43.5 %collective-permute-start.3 = (bf16[1,1536,640]{2,1,0:T(8,128)(2,1)}, bf16[1,1536,640]{2,1,0:T(8,128)(2,1)}, u32[]{:S(2)}, u32[]{:S(2)}) collective-permute-start(bf16[1,1536,640]{2,1,0:T(8,128)(2,1)} %get-tuple-element.37.refs_0_), channel_id=1, source_target_pairs={{0,1},{1,0},{2,3},{3,2},{4,5},{5,4},{6,7},{7,6},{8,9},{9,8},{10,11... | collective-permute-start | bytes 5898248 | tf_op jit(solution)/shard_map/ppermute | solution.py:357
  239.4 21.2 %collective-permute-start.4 = (bf16[1,1536,640]{2,1,0:T(8,128)(2,1)}, bf16[1,1536,640]{2,1,0:T(8,128)(2,1)}, u32[]{:S(2)}, u32[]{:S(2)}) collective-permute-start(bf16[1,1536,640]{2,1,0:T(8,128)(2,1)} %get-tuple-element.38.refs_1_), channel_id=1, source_target_pairs={{0,1},{1,0},{2,3},{3,2},{4,5},{5,4},{6,7},{7,6},{8,9},{9,8},{10,11... | collective-permute-start | bytes 5898248 | tf_op jit(solution)/shard_map/ppermute | solution.py:357
  (1 other events, 0.7 us)

commit v5 on v4

--- a/solution.py
+++ b/solution.py
@@ -286,6 +286,7 @@
 
     chunk = 512
     if with_ada:
+        dmods = [dmod_ref[branch, 0].astype(BF16) for branch in range(2)]
         dmods_trn = [dmod_ref[branch, 0].T.astype(BF16) for branch in range(2)]
 
     @pl.loop(0, d_model // chunk)
@@ -294,9 +295,8 @@
         out_ref[0, rows] = dot(trn_i_ref[rows], rhs_i_ref[...])
         out_ref[1, rows] = dot(trn_t_ref[rows], rhs_t_ref[...])
         if with_ada:
-            act = act_ref[rows].astype(F32)
             for branch in range(2):
-                dw_ref[branch, rows] = sum(act[:, idx:idx + 1] * dmod_ref[branch, 0, idx:idx + 1, :] for idx in range(2 * n_b))
+                dw_ref[branch, rows] = dot(act_ref[rows], dmods[branch])
                 dact_ref[rows] += dot(w_ref[branch, rows], dmods_trn[branch])
 
 
@@ -376,7 +376,7 @@
             return jnp.where(core == 0, jnp.concatenate([mine, other], axis), jnp.concatenate([other, mine], axis))
 
         cond_act = jax.nn.silu(cond_vec.astype(F32)).astype(BF16)
-        cond_mod = ada_fwd(cond_act, w_ada, b_ada, 768)
+        cond_mod = ada_fwd(cond_act, w_ada, b_ada, 1536)
         own_mod = own(cond_mod, 1).reshape(2, n_own, 3, d_model).swapaxes(0, 1)
         pad_rows = ((0, 0), (0, n_txt - ctx_len), (0, 0))
         text_own, cot_own = jnp.pad(own(text_in), pad_rows), jnp.pad(own(text_cot), pad_rows)
@@ -414,8 +414,7 @@
         chip_lo = chip * pair * tok_dev
         img_mine, img_send = (jnp.concatenate([lax.dynamic_slice_in_dim(out[4], chip_lo + pos * tok_dev, tok_dev, 2) for out in outs]) for pos in (core, 1 - core))
         img_pair = ordered(img_mine, swap(img_send))
-        txt = ordered(jnp.concatenate(txt[:n_own]), jnp.concatenate(txt[n_own:]))
-        text_new, grad_text = txt[:, 0, :ctx_len], txt[:, 1, :ctx_len]
+        text_new, grad_text = (ordered(jnp.concatenate([arr[:, pos, :ctx_len] for arr in txt[:n_own]]), jnp.concatenate([arr[:, pos, :ctx_len] for arr in txt[n_own:]])) for pos in range(2))
         return (img_pair[:, 0], text_new, img_pair[:, 1], grad_text, grad_cond, dw_ada, db_ada, dw_qkv, db_qkv, d_gain, dw_out, db_out)
 
     data_spec = P('dp', 'sp', None)

time: 345 us -> 345 us (level)
  local copies, waits for them, and re-layouts: 33.1 us -> 45.5 us
  other arithmetic: 22.7 us -> 15 us
  Pallas kernels: 263 us -> 257 us
    squeeze x1 -> x4, local copies, waits for them, and re-layouts: 0.79 us -> 9.47 us  [device_fn(): arr[:, pos, :ctx_len]]
    select_n x2 -> x3, other arithmetic: 10 us -> 4.28 us  [ordered(): jnp.where(core == 0, jnp.concatenate([mine, other], axis), jnp.concatenat...]
    unnamed x29 -> x45, local copies, waits for them, and re-layouts: 15 us -> 16.4 us
  transfers between devices with their start and end apart: 15 -> 15, of which waited for: 1 -> 1; matrix products, arithmetic and copies ran while one was open for 14% -> 15% of each run, Pallas kernels for 33% -> 32%
where the time goes in v5:
time: 345 us; the launch traced here: 338 us
  Pallas kernels  257 us (74%)
  local copies, waits for them, and re-layouts  45.5 us (13%)
  other arithmetic  15 us (4%)
  starting transfers between devices  12.8 us (4%)
  waiting for transfers between devices  6.32 us (2%)
    pallas_call x2, Pallas kernels, fused_block(): pl.pallas_call(functools.partial(block_kernel, n_keys, heads), out_shape=...  153 us
    pallas_call x2, Pallas kernels, wgrad(): pl.pallas_call(functools.partial(wgrad_kernel, n_img, n_b, ada is not Non...  93.2 us
    unnamed x45, local copies, waits for them, and re-layouts  16.4 us
    pallas_call x1, Pallas kernels, ada_fwd(): pl.pallas_call(ada_fwd_kernel, out_shape=jax.ShapeDtypeStruct((2, 16, wid...  11.1 us
    squeeze x4, local copies, waits for them, and re-layouts, device_fn(): arr[:, pos, :ctx_len]  9.47 us
    all_to_all x2, starting transfers between devices, device_fn(): lax.all_to_all(jnp.concatenate([img_pair[:, :, idx].swapaxes(0, 1)] * n_c...  8.95 us
    dynamic_slice x2, local copies, waits for them, and re-layouts, own(): return lax.dynamic_slice_in_dim(arr, own_lo, n_own, axis)  7.65 us
  transfers between devices with their start and end apart: 15, of which 1 were waited for; matrix products, arithmetic and copies ran while one was open for 15% of the time, Pallas kernels for 32%

profile of v5, /device:TPU:0, one launch (start us, length us, event | category | flops | bytes accessed | tf_op | source)
XLA Modules:
  0.0 338.3 jit_solution(152879926670653267)
XLA Ops:
  0.6 1.5 fusion.2
  3.5 4.6 %all-to-all-start.1 = ((bf16[4,2,1,64,1536]{4,3,2,1,0:T(8,128)(2,1)}), bf16[4,2,1,64,1536]{4,3,2,1,0:T(8,128)(2,1)}, u32[]{:S(2)}, u32[]{:S(2)}) async-start(bf16[4,2,1,64,1536]{4,3,2,1,0:T(8,128)(2,1)} %pad_maximum_fusion), calls=%async_computation.1 | async-start | bytes 3145728 | tf_op jit(solution)/shard_map/all_to_all | solution.py:370
  9.6 7.6 %constant_dynamic-slice_fusion.5 = (bf16[2,333,1536]{2,0,1:T(2,128)(2,1)S(1)}, bf16[2,333,1536]{2,0,1:T(2,128)(2,1)S(1)}) fusion(bf16[4,333,1536]{2,0,1:T(4,128)(2,1)} %param.23, s32[]{:T(128)S(6)} %select_n.42, bf16[4,333,1536]{2,0,1:T(4,128)(2,1)} %param.13), kind=kLoop, calls=%fused_computation.50 | loop fusion | bytes 8183812 | tf_op jit(solution)/shard_map/dynamic_slice | solution.py:373
  17.2 1.5 copy.89
  19.5 11.1 %ada_fwd.1 = f32[2,16,4608]{2,1,0:T(8,128)S(1)} custom-call(bf16[16,1536]{1,0:T(8,128)(2,1)S(1)} %pad.22.clone.act_ref, bf16[2,1536,4608]{2,1,0:T(8,128)(2,1)} %refs_10_.1, f32[2,4608]{1,0:T(2,128)S(1)} %copy-done), custom_call_target="tpu_custom_call" | custom-call | flops 452984832 | bytes 28311552 | tf_op jit(solution)/shard_map/ada_fwd/pallas_call | solution.py:339
  34.4 1.7 pad_slice_fusion.3
  36.1 1.6 pad_slice_fusion.1
  38.3 4.4 %all-to-all-start = ((bf16[4,2,1,64,1536]{4,3,1,2,0:T(8,128)(2,1)}), bf16[4,2,1,64,1536]{4,3,1,2,0:T(8,128)(2,1)}, u32[]{:S(2)}, u32[]{:S(2)}) async-start(bf16[4,2,1,64,1536]{4,3,1,2,0:T(8,128)(2,1)} %maximum_bitcast_fusion), calls=%async_computation | async-start | bytes 3145728 | tf_op jit(solution)/shard_map/all_to_all | solution.py:370
  42.7 76.6 %fused_block.3 = (bf16[1,1536,640]{2,1,0:T(8,128)(2,1)}, bf16[1,640,1536]{2,1,0:T(8,128)(2,1)}, bf16[1,1536,640]{2,1,0:T(8,128)(2,1)}, bf16[1,3,640,1536]{3,2,1,...) custom-call(bf16[4,2,1,64,1536]{4,3,2,1,0:T(8,128)(2,1)} %all-to-all, ...), custom_call_target="tpu_custom_call" | custom-call | flops 31708938240 | bytes 104857600 | tf_op jit(solution)/shard_map/fused_block/pallas_call | solution.py:252
  119.3 2.1 constant_dynamic-slice_fusion.2
  121.4 76.4 %fused_block.2 = (bf16[1,1536,640]{2,1,0:T(8,128)(2,1)}, bf16[1,640,1536]{2,1,0:T(8,128)(2,1)}, bf16[1,1536,640]{2,1,0:T(8,128)(2,1)}, bf16[1,3,640,1536]{3,2,1,...) custom-call(bf16[4,2,1,64,1536]{4,3,2,1,0:T(8,128)(2,1)} %bitcast.5., ...), custom_call_target="tpu_custom_call" | custom-call | flops 31708938240 | bytes 104857600 | tf_op jit(solution)/shard_map/fused_block/pallas_call | solution.py:252
  197.9 1.3 constant_dynamic-slice_fusion.3
  202.4 6.3 %collective-permute-done.8 = f32[10,1536]{1,0:T(8,128)S(1)} collective-permute-done((f32[10,1536]{1,0:T(8,128)S(1)}, f32[10,1536]{1,0:T(8,128)S(1)}, u32[]{:S(2)}, u32[]{:S(2)}) %collective-permute-start.8) | collective-permute-done | bytes 61472 | tf_op jit(solution)/shard_map/ppermute | solution.py:357
  209.0 3.0 slice_bitcast_fusion.4
  212.2 3.0 slice_bitcast_fusion.5
  222.8 22.2 %shard_map.212 = f32[2,1536,1536]{2,1,0:T(8,128)} custom-call(s32[1]{0:T(128)} %bitcast.21.core_ref, bf16[1,1536,640]{2,1,0:T(8,128)(2,1)} %get-tuple-element.50.refs_0_, bf16[1,1536,640]{2,1,0:T(8,128)(2,1)} %get-tuple-element.51.refs_1_, bf16[1,1536,640]{2,1,0:T(8,128)(2,1)} %copy-done.17, bf16[1,1536,640]{2,1,0:T(8,128)(2,1)} %collective-permute-done.10.refs_3_, ...), custom_call_target="tpu_custom_call" | custom-call | flops 12079595520 | bytes 18874368 | tf_op jit(solution)/shard_map/pallas_call | solution.py:321
  245.4 1.7 slice_bitcast_fusion
  247.1 1.8 slice_bitcast_fusion.1
  249.2 1.9 maximum_select_fusion
  251.1 5.1 %copy.84 = bf16[4,333,1536]{2,0,1:T(4,128)(2,1)} copy(bf16[4,333,1536]{2,1,0:T(8,128)(2,1)S(1)} %maximum_select_fusion) | data formatting | bytes 8183808
  256.2 2.1 maximum_select_fusion.1
  258.4 5.1 %copy.85 = bf16[4,333,1536]{2,0,1:T(4,128)(2,1)} copy(bf16[4,333,1536]{2,1,0:T(8,128)(2,1)S(1)} %maximum_select_fusion.1) | data formatting | bytes 8183808
  263.5 71.0 %shard_map.211 = (f32[2,1536,4608]{2,1,0:T(8,128)}, f32[2,1536,4608]{2,1,0:T(8,128)}, f32[1536,16]{1,0:T(8,128)}) custom-call(s32[1]{0:T(128)} %bitcast.21.core_ref, bf16[1,1536,640]{2,1,0:T(8,128)(2,1)} %get-tuple-element.37.refs_0_, bf16[1,1536,640]{2,1,0:T(8,128)(2,1)} %get-tuple-element.38.refs_1_, bf16[1,1536,640]{2,1,0:T(8,128)(2,1)} %collective-permute-done.3.refs_2_, ...), custom_call_target="tpu_custom_call" | custom-call | flops 36238786560 | bytes 169869312 | tf_op jit(solution)/shard_map/pallas_call | solution.py:321
  335.7 1.4 fusion
  (107 shorter events, 21.9 us)
Async XLA Ops:
  3.5 4.6 %copy-start.14 = (bf16[4,1536]{1,0:T(4,128)(2,1)S(1)}, bf16[4,1536]{1,0:T(4,128)(2,1)}, u32[]{:S(2)}) copy-start(bf16[4,1536]{1,0:T(4,128)(2,1)} %param.14) | copy-start | bytes 36868
  3.5 34.9 %all-to-all-start.1 = ((bf16[4,2,1,64,1536]{4,3,2,1,0:T(8,128)(2,1)}), bf16[4,2,1,64,1536]{4,3,2,1,0:T(8,128)(2,1)}, u32[]{:S(2)}, u32[]{:S(2)}) async-start(bf16[4,2,1,64,1536]{4,3,2,1,0:T(8,128)(2,1)} %pad_maximum_fusion), calls=%async_computation.1 | async-start | bytes 3145728 | tf_op jit(solution)/shard_map/all_to_all | solution.py:370
  8.3 8.9 %copy-start.2 = (f32[4,1536]{0,1:T(8,128)}, f32[4,1536]{0,1:T(8,128)S(1)}, u32[]{:S(2)}) copy-start(f32[4,1536]{0,1:T(8,128)S(1)} %copy.76) | copy-start | bytes 73732
  19.5 11.3 %copy-start.15 = (f32[2,2,64]{2,1,0:T(2,128)S(1)}, f32[2,2,64]{2,1,0:T(2,128)}, u32[]{:S(2)}) copy-start(f32[2,2,64]{2,1,0:T(2,128)} %param.19) | copy-start | bytes 3076
  38.3 83.0 %all-to-all-start = ((bf16[4,2,1,64,1536]{4,3,1,2,0:T(8,128)(2,1)}), bf16[4,2,1,64,1536]{4,3,1,2,0:T(8,128)(2,1)}, u32[]{:S(2)}, u32[]{:S(2)}) async-start(bf16[4,2,1,64,1536]{4,3,1,2,0:T(8,128)(2,1)} %maximum_bitcast_fusion), calls=%async_computation | async-start | bytes 3145728 | tf_op jit(solution)/shard_map/all_to_all | solution.py:370
  197.8 3.9 %copy-start.12 = (f32[1,8,1536]{2,1,0:T(8,128)S(1)}, f32[1,8,1536]{2,1,0:T(8,128)}, u32[]{:S(2)}) copy-start(f32[1,8,1536]{2,1,0:T(8,128)} %get-tuple-element.47) | copy-start | bytes 147460
  197.9 4.0 %copy-start.10 = (f32[1,8,1536]{2,1,0:T(8,128)S(1)}, f32[1,8,1536]{2,1,0:T(8,128)}, u32[]{:S(2)}) copy-start(f32[1,8,1536]{2,1,0:T(8,128)} %get-tuple-element.42) | copy-start | bytes 147460
  197.9 4.0 %copy-start.11 = (f32[1,8,1536]{2,1,0:T(8,128)S(1)}, f32[1,8,1536]{2,1,0:T(8,128)}, u32[]{:S(2)}) copy-start(f32[1,8,1536]{2,1,0:T(8,128)} %get-tuple-element.41) | copy-start | bytes 147460
  200.3 14.9 %collective-permute-start = (bf16[2,2,64,1536]{3,2,1,0:T(8,128)(2,1)S(1)}, bf16[2,2,64,1536]{3,2,1,0:T(8,128)(2,1)S(1)}, u32[]{:S(2)}, u32[]{:S(2)}) collective-permute-start(bf16[2,2,64,1536]{3,2,1,0:T(8,128)(2,1)S(1)} %pad_maximum_fusion.3), channel_id=1, source_target_pairs={{0,1},{1,0},{2,3},{3,2},{4,5},{5,4},{6,7},{7,6},{8,9},{9,8},{10,11... | collective-permute-start | bytes 2359304 | tf_op jit(solution)/shard_map/ppermute | solution.py:357
  201.0 14.6 %collective-permute-start.9 = (bf16[1,1536,640]{2,1,0:T(8,128)(2,1)S(1)}, bf16[1,1536,640]{2,1,0:T(8,128)(2,1)S(1)}, u32[]{:S(2)}, u32[]{:S(2)}) collective-permute-start(bf16[1,1536,640]{2,1,0:T(8,128)(2,1)S(1)} %copy-done.16), channel_id=1, source_target_pairs={{0,1},{1,0},{2,3},{3,2},{4,5},{5,4},{6,7},{7,6},{8,9},{9,8},{10,11... | collective-permute-start | bytes 5898248 | tf_op jit(solution)/shard_map/ppermute | solution.py:357
  201.0 17.1 %collective-permute-start.10 = (bf16[1,1536,640]{2,1,0:T(8,128)(2,1)}, bf16[1,1536,640]{2,1,0:T(8,128)(2,1)}, u32[]{:S(2)}, u32[]{:S(2)}) collective-permute-start(bf16[1,1536,640]{2,1,0:T(8,128)(2,1)} %get-tuple-element.51.refs_1_), channel_id=1, source_target_pairs={{0,1},{1,0},{2,3},{3,2},{4,5},{5,4},{6,7},{7,6},{8,9},{9,8},{10,11... | collective-permute-start | bytes 5898248 | tf_op jit(solution)/shard_map/ppermute | solution.py:357
  201.8 6.9 %collective-permute-start.8 = (f32[10,1536]{1,0:T(8,128)S(1)}, f32[10,1536]{1,0:T(8,128)S(1)}, u32[]{:S(2)}, u32[]{:S(2)}) collective-permute-start(f32[10,1536]{1,0:T(8,128)S(1)} %select_maximum_fusion), channel_id=1, source_target_pairs={{0,1},{1,0},{2,3},{3,2},{4,5},{5,4},{6,7},{7,6},{8,9},{9,8},{10,11... | collective-permute-start | bytes 184328 | tf_op jit(solution)/shard_map/ppermute | solution.py:357
  201.9 10.2 %collective-permute-start.7 = (f32[2,8,1536]{2,1,0:T(8,128)S(1)}, f32[2,8,1536]{2,1,0:T(8,128)S(1)}, u32[]{:S(2)}, u32[]{:S(2)}) collective-permute-start(f32[2,8,1536]{2,1,0:T(8,128)S(1)} %pad_maximum_fusion.4), channel_id=1, source_target_pairs={{0,1},{1,0},{2,3},{3,2},{4,5},{5,4},{6,7},{7,6},{8,9},{9,8},{10,11... | collective-permute-start | bytes 294920 | tf_op jit(solution)/shard_map/ppermute | solution.py:357
  208.7 12.1 %collective-permute-start.11 = (bf16[1,1,640,1536]{3,2,1,0:T(8,128)(2,1)}, bf16[1,1,640,1536]{3,2,1,0:T(8,128)(2,1)}, u32[]{:S(2)}, u32[]{:S(2)}) collective-permute-start(bf16[1,1,640,1536]{3,2,1,0:T(8,128)(2,1)} %bitcast.27.refs_4_), channel_id=1, source_target_pairs={{0,1},{1,0},{2,3},{3,2},{4,5},{5,4},{6,7},{7,6},{8,9},{9,8},{10,11... | collective-permute-start | bytes 5898248 | tf_op jit(solution)/shard_map/ppermute | solution.py:357
  212.0 10.6 %collective-permute-start.12 = (bf16[1,1,640,1536]{3,2,1,0:T(8,128)(2,1)}, bf16[1,1,640,1536]{3,2,1,0:T(8,128)(2,1)}, u32[]{:S(2)}, u32[]{:S(2)}) collective-permute-start(bf16[1,1,640,1536]{3,2,1,0:T(8,128)(2,1)} %bitcast.28.refs_5_), channel_id=1, source_target_pairs={{0,1},{1,0},{2,3},{3,2},{4,5},{5,4},{6,7},{7,6},{8,9},{9,8},{10,11... | collective-permute-start | bytes 5898248 | tf_op jit(solution)/shard_map/ppermute | solution.py:357
  215.2 5.9 %copy-start.7 = (bf16[1,2,64,1536]{3,2,1,0:T(8,128)(2,1)S(1)}, bf16[1,2,64,1536]{3,2,1,0:T(8,128)(2,1)}, u32[]{:S(2)}) copy-start(bf16[1,2,64,1536]{3,2,1,0:T(8,128)(2,1)} %get-tuple-element.118) | copy-start | bytes 1179652
  215.2 48.4 %collective-permute-start.5 = (bf16[1,3,640,1536]{3,2,1,0:T(8,128)(2,1)}, bf16[1,3,640,1536]{3,2,1,0:T(8,128)(2,1)}, u32[]{:S(2)}, u32[]{:S(2)}) collective-permute-start(bf16[1,3,640,1536]{3,2,1,0:T(8,128)(2,1)} %get-tuple-element.39.refs_4_), channel_id=1, source_target_pairs={{0,1},{1,0},{2,3},{3,2},{4,5},{5,4},{6,7},{7,6},{8,9},{9,8},{10,11... | collective-permute-start | bytes 17694728 | tf_op jit(solution)/shard_map/ppermute | solution.py:357
  215.5 48.0 %collective-permute-start.6 = (bf16[1,3,640,1536]{3,2,1,0:T(8,128)(2,1)}, bf16[1,3,640,1536]{3,2,1,0:T(8,128)(2,1)}, u32[]{:S(2)}, u32[]{:S(2)}) collective-permute-start(bf16[1,3,640,1536]{3,2,1,0:T(8,128)(2,1)} %get-tuple-element.40.refs_5_), channel_id=1, source_target_pairs={{0,1},{1,0},{2,3},{3,2},{4,5},{5,4},{6,7},{7,6},{8,9},{9,8},{10,11... | collective-permute-start | bytes 17694728 | tf_op jit(solution)/shard_map/ppermute | solution.py:357
  218.2 26.8 %collective-permute-start.2 = (bf16[1,2,384,1536]{3,2,1,0:T(8,128)(2,1)}, bf16[1,2,384,1536]{3,2,1,0:T(8,128)(2,1)}, u32[]{:S(2)}, u32[]{:S(2)}) collective-permute-start(bf16[1,2,384,1536]{3,2,1,0:T(8,128)(2,1)} %get-tuple-element.36), channel_id=1, source_target_pairs={{0,1},{1,0},{2,3},{3,2},{4,5},{5,4},{6,7},{7,6},{8,9},{9,8},{10,11... | collective-permute-start | bytes 7077896 | tf_op jit(solution)/shard_map/ppermute | solution.py:357
  220.7 26.3 %collective-permute-start.1 = (bf16[1,2,384,1536]{3,2,1,0:T(8,128)(2,1)}, bf16[1,2,384,1536]{3,2,1,0:T(8,128)(2,1)}, u32[]{:S(2)}, u32[]{:S(2)}) collective-permute-start(bf16[1,2,384,1536]{3,2,1,0:T(8,128)(2,1)} %get-tuple-element.35), channel_id=1, source_target_pairs={{0,1},{1,0},{2,3},{3,2},{4,5},{5,4},{6,7},{7,6},{8,9},{9,8},{10,11... | collective-permute-start | bytes 7077896 | tf_op jit(solution)/shard_map/ppermute | solution.py:357
  222.7 40.9 %collective-permute-start.3 = (bf16[1,1536,640]{2,1,0:T(8,128)(2,1)}, bf16[1,1536,640]{2,1,0:T(8,128)(2,1)}, u32[]{:S(2)}, u32[]{:S(2)}) collective-permute-start(bf16[1,1536,640]{2,1,0:T(8,128)(2,1)} %get-tuple-element.37.refs_0_), channel_id=1, source_target_pairs={{0,1},{1,0},{2,3},{3,2},{4,5},{5,4},{6,7},{7,6},{8,9},{9,8},{10,11... | collective-permute-start | bytes 5898248 | tf_op jit(solution)/shard_map/ppermute | solution.py:357
  245.0 18.5 %collective-permute-start.4 = (bf16[1,1536,640]{2,1,0:T(8,128)(2,1)}, bf16[1,1536,640]{2,1,0:T(8,128)(2,1)}, u32[]{:S(2)}, u32[]{:S(2)}) collective-permute-start(bf16[1,1536,640]{2,1,0:T(8,128)(2,1)} %get-tuple-element.38.refs_1_), channel_id=1, source_target_pairs={{0,1},{1,0},{2,3},{3,2},{4,5},{5,4},{6,7},{7,6},{8,9},{9,8},{10,11... | collective-permute-start | bytes 5898248 | tf_op jit(solution)/shard_map/ppermute | solution.py:357
  251.1 5.2 %copy-start.3 = (bf16[1,333,1536]{2,1,0:T(8,128)(2,1)S(1)}, bf16[1,333,1536]{2,1,0:T(8,128)(2,1)}, u32[]{:S(2)}) copy-start(bf16[1,333,1536]{2,1,0:T(8,128)(2,1)} %get-tuple-element.104) | copy-start | bytes 3068932
  251.1 5.2 %copy-start.5 = (bf16[1,333,1536]{2,1,0:T(8,128)(2,1)S(1)}, bf16[1,333,1536]{2,1,0:T(8,128)(2,1)}, u32[]{:S(2)}) copy-start(bf16[1,333,1536]{2,1,0:T(8,128)(2,1)} %get-tuple-element.102) | copy-start | bytes 3068932
  (9 other events, 22.5 us)
